TPU v7x, 32 devices: a whole 2x2x4 slice. The times are simulated.
32 devices in a mesh: mem: 4 (over z), tx: 4 (over y, core), ty: 2 (over x).
Axes of the slice: x: 2, y: 2, z: 4, core: 2. Of those that a mesh axis runs over, the one named last changes fastest.
Arguments:
- alpha: float32 [32, 4, 64, 64], P('mem', None, 'tx', 'ty'), may hold values from -6 to 6
- filter_rate: float32 [64, 64], P('tx', 'ty'), may hold values from 0.1 to 0.24
- block_list: int32 [4, 2, 32], P('tx', 'ty'), may hold values from 0 to 63, as said below
- interp_weights: float32 [4, 2, 32, 64, 256], P('tx', 'ty'), may hold values from -0.75 to 0.75
- perturbations: bfloat16 [32, 4, 4, 256, 256], P('mem', None, None, ('tx', 'ty')), may hold values from -1.5 to 1.5
- obs_cells: int32 [4, 2, 512], P('tx', 'ty'), may hold values from 0 to 8191
- obs_count: int32 [4, 2], P('tx', 'ty'), may hold values from 1 to 512, as said below
- departures: float32 [4, 2, 16, 512], P('tx', 'ty', 'mem'), may hold values from -6 to 6
- obs_weight: float32 [4, 2, 16, 512], P('tx', 'ty', 'mem'), may hold values from 0.25 to 2.5
Outputs:
- increment: float32 [16, 256, 256], P('mem', ('tx', 'ty'))
- weighted_departure: float32 [4, 2, 16, 512], P('tx', 'ty', 'mem')
- gradient: float32 [32, 4, 64, 64], P('mem', None, 'tx', 'ty')
Inputs may be any that keep to these rules, and one draw needn't show every extreme that they name: `block_list`: Among the fine blocks of one tile, at most 2 distinct coarse blocks of any one tile are named; every tile names exactly 2 distinct blocks of its own. `obs_count`: some tile has all 512 slots in use in every draw.
All inputs are finite; a program needn't handle non-finite values.
Results may differ from a plain program's by a relative error of at most 0.0003.
Values sent between devices are 32-bit elements; how exact they have to be, the bound alone decides.
No kernel may reach another device: no remote copies, remote signals or barrier semaphores. Data moves between devices by JAX's collectives and lax.ppermute only.
A program may use at most 64 MiB of HBM per device.

v0:
```python
import functools

import jax
import jax.numpy as jnp
from jax import lax
from jax.experimental import pallas as pl
from jax.experimental.pallas import tpu as pltpu
from jax.sharding import PartitionSpec as P


CB = 8
SWEEPS = 4
LANES = 128
SUB = 8
PITCH_PAD = 8


VM = pl.BlockSpec(memory_space=pltpu.VMEM)
HB = pl.BlockSpec(memory_space=pltpu.HBM)
SM = pl.BlockSpec(memory_space=pltpu.SMEM)


def params(mib):
    return pltpu.CompilerParams(vmem_limit_bytes=mib << 20)


def split2(v, n):
    if n & (n - 1) == 0:
        return v >> (n.bit_length() - 1), v & (n - 1)
    return lax.div(v, n), lax.rem(v, n)


def hi_lo(v):
    hi = v.astype(jnp.bfloat16)
    return hi, (v - hi.astype(jnp.float32)).astype(jnp.bfloat16)


def lane_ids(shape):
    return lax.broadcasted_iota(jnp.int32, shape, len(shape) - 1)


class Sizes:
    def __init__(self, alpha, weights, perts, cells, departures):
        self.n_tx, self.n_ty, self.n_mem = (lax.axis_size(a) for a in ("tx", "ty", "mem"))
        self.tiles = self.n_tx * self.n_ty
        self.chips = self.tiles // 2
        self.members, self.levels, self.cx, self.cy = alpha.shape
        self.rows = self.members * self.levels
        self.rg = self.rows // SUB
        self.fine, self.block, self.bcells = weights.shape[2:]
        self.vars = perts.shape[2]
        self.slabs = self.levels * self.vars
        self.slab_dev = departures.shape[2]
        self.obs = cells.shape[-1]
        self.nx, self.ny = self.n_tx * self.cx, self.n_ty * self.cy
        self.groups = LANES // self.ny
        self.xl = self.nx // self.groups
        self.nq = LANES // self.cy
        self.xq = self.cx // self.nq
        self.t_rows = self.xq * self.rg
        self.ct = self.bcells // LANES
        self.ot = self.obs // LANES
        self.blk_x, self.blk_y = self.cx // CB, self.cy // CB
        assert self.n_tx % 2 == 0 and self.groups * self.ny == LANES and self.ny == CB * CB
        assert self.xl % CB == 0 and self.nq * self.cy == LANES and self.xq * self.nq == self.cx
        assert self.xq <= SUB and self.rows % SUB == 0 and self.groups == 2
        assert self.slab_dev * self.ot <= self.slabs

    def block_place(self, bid):
        tile, kb = split2(bid, self.blk_x * self.blk_y)
        a, b = split2(tile, self.n_ty)
        bx, by = split2(kb, self.blk_y)
        gx, gy = a * self.blk_x + bx, b * self.blk_y + by
        g, xg = split2(gx, self.xl // CB)
        return xg * CB + gy, g

    def tile_at(self, step, back, other_core):
        tx, ty = lax.axis_index("tx"), lax.axis_index("ty")
        half = self.n_tx // 2
        chip_y, core = split2(tx, 2)
        dy, dx = divmod(step, self.n_ty)
        if back:
            dy, dx = half - dy, self.n_ty - dx
        y = lax.rem(chip_y + dy, half)
        x = lax.rem(ty + dx, self.n_ty)
        if other_core:
            core = 1 - core
        return (y * 2 + core) * self.n_ty + x

    def chip_perm(self, step):
        half = self.n_tx // 2
        dy, dx = divmod(step, self.n_ty)
        pairs = []
        for y in range(half):
            for core in range(2):
                for x in range(self.n_ty):
                    to = ((y + dy) % half * 2 + core) * self.n_ty + (x + dx) % self.n_ty
                    pairs.append(((y * 2 + core) * self.n_ty + x, to))
        return pairs

    def core_perm(self):
        return [(i, (i // self.n_ty ^ 1) * self.n_ty + i % self.n_ty) for i in range(self.tiles)]

    def pieces(self):
        table = [[] for _ in range(self.xl)]
        for a in range(self.n_tx):
            for x in range(self.cx):
                g, xl = divmod(a * self.cx + x, self.xl)
                q, xq = divmod(x, self.xq)
                for b in range(self.n_ty):
                    table[xl].append((a * self.n_ty + b, xq, q, g * self.ny // self.cy + b))
        return table


def rolled(v, shift):
    shift %= LANES
    return v if shift == 0 else pltpu.roll(v, shift, v.ndim - 1)


def pack_kernel(z, alpha_hbm, rate_hbm, out_ref, alpha_ref, rate_ref, sems):
    copies = [
        pltpu.make_async_copy(alpha_hbm, alpha_ref, sems.at[0]),
        pltpu.make_async_copy(rate_hbm, rate_ref, sems.at[1]),
    ]
    for copy in copies:
        copy.start()
    for copy in copies:
        copy.wait()
    out_ref[z.t_rows] = jnp.zeros((SUB, LANES), jnp.float32)
    for x in range(z.cx):
        q, xq = divmod(x, z.xq)
        lanes = slice(q * z.cy, (q + 1) * z.cy)
        v = alpha_ref[:, x, :]
        out_ref[xq * z.rg : (xq + 1) * z.rg, :, lanes] = v.reshape(z.rg, SUB, z.cy)
        out_ref[z.t_rows, xq : xq + 1, lanes] = rate_ref[x : x + 1, :]


def prep_kernel(z, weights_ref, cells_ref, stacked_ref, column_ref):
    k = z.block

    def one(f, carry):
        hi, lo = hi_lo(weights_ref[f])
        stacked_ref[f, 0:k, :] = hi
        stacked_ref[f, k : 2 * k, :] = hi
        stacked_ref[f, 2 * k : 3 * k, :] = lo
        return carry

    lax.fori_loop(0, z.fine, one, 0, unroll=2)
    _, col = split2(cells_ref[...], z.bcells)
    ids = lax.broadcasted_iota(jnp.int32, (z.bcells, z.obs), 0)
    column_ref[...] = jnp.where(ids == col, 1.0, 0.0).astype(jnp.bfloat16)


def fill_edges(z, ref):
    lane = lane_ids((z.rg, SUB, LANES))
    ref[0] = jnp.where(lane >= z.ny, rolled(ref[z.xl], z.ny), 0.0)
    ref[z.xl + 1] = jnp.where(lane < LANES - z.ny, rolled(ref[1], -z.ny), 0.0)


def beside(z, ref, x, lane_y):
    c = ref[x + 1]
    west = jnp.where(lane_y > 0, rolled(c, 1), 0.0)
    east = jnp.where(lane_y < z.ny - 1, rolled(c, -1), 0.0)
    return c, (ref[x] + ref[x + 2]) + (west + east)


def swap_blocks(z, src, src_off, dst, dst_off):
    lane = lane_ids((SUB, LANES))

    def one(i, carry):
        xg, r = split2(i, z.rg)
        v = [src[xg * CB + j + src_off, r] for j in range(CB)]
        for bit in (1, 2, 4):
            shift = bit * CB
            low = (lane & shift) == 0
            for j in range(CB):
                if j & bit == 0:
                    a, b = v[j], v[j | bit]
                    v[j] = jnp.where(low, a, rolled(b, shift))
                    v[j | bit] = jnp.where(low, rolled(a, -shift), b)
        for j in range(CB):
            dst[xg * CB + j + dst_off, r] = v[j]
        return carry

    lax.fori_loop(0, z.xl // CB * z.rg, one, 0, unroll=8)


def forward_kernel(z, *refs):
    blocks_ref = refs[0]
    tile_refs = refs[1 : 1 + z.tiles]
    w_ref, pert_ref, cells_ref, column_ref, dep_ref, ow_ref = refs[1 + z.tiles : 7 + z.tiles]
    outs = refs[7 + z.tiles :]
    seen_ref, rate_ref = outs[:2]
    inc_refs = outs[2 : 2 + z.n_mem]
    every, field, other, fine_ref, inc = outs[2 + z.n_mem :]
    me = lax.axis_index("mem")
    for s in range(z.chips):
        every[z.tile_at(s, True, False)] = tile_refs[s][...]
        every[z.tile_at(s, True, True)] = tile_refs[z.chips + s][...]

    group = lane_ids((z.rg, SUB, LANES)) // z.cy
    group_row = lane_ids((SUB, LANES)) // z.cy
    for xl, pieces in enumerate(z.pieces()):
        total, rate = None, None
        for tile, xq, q, to in pieces:
            shift = (to - q) * z.cy
            v = rolled(every[tile, xq * z.rg : (xq + 1) * z.rg], shift)
            w = rolled(jnp.broadcast_to(every[tile, z.t_rows, xq : xq + 1], (SUB, LANES)), shift)
            total = v if total is None else jnp.where(group == to, v, total)
            rate = w if rate is None else jnp.where(group_row == to, w, rate)
        field[xl + 1] = total
        rate_ref[xl] = rate

    lane_y = lane_ids((z.rg, SUB, LANES)) % z.ny
    src, dst = field, other
    for _ in range(SWEEPS):
        fill_edges(z, src)

        def row(x, carry, src=src, dst=dst):
            c, near = beside(z, src, x, lane_y)
            dst[x + 1] = c + rate_ref[x] * (near - 4.0 * c)
            return carry

        lax.fori_loop(0, z.xl, row, 0, unroll=True)
        src, dst = dst, src
    swap_blocks(z, src, 1, dst, 0)

    lane = lane_ids((z.rows, LANES))
    half = lane // z.block
    pitch = z.rows + PITCH_PAD

    def fine_block(f, carry):
        at, g = z.block_place(blocks_ref[f])
        v = dst[at].reshape(z.rows, LANES)
        v = jnp.where(half == g, v, rolled(v, z.block))
        hi = v.astype(jnp.bfloat16)
        hi32 = hi.astype(jnp.float32)
        first = jnp.where(half == 0, hi32, v - hi32).astype(jnp.bfloat16)
        lhs = jnp.concatenate([first, hi[:, : z.block]], axis=1)
        out = jnp.dot(lhs, w_ref[f], preferred_element_type=jnp.float32)
        start = pl.multiple_of(f * pitch, SUB)
        for t in range(z.ct):
            fine_ref[t, pl.ds(start, z.rows), :] = out[:, t * LANES : (t + 1) * LANES]
        return carry

    lax.fori_loop(0, z.fine, fine_block, 0, unroll=16)

    def level(l, carry):
        for t in range(z.ct):
            cols = slice(t * LANES, (t + 1) * LANES)
            fine = [
                fine_ref[t, pl.ds(m * z.levels + l, z.fine, stride=pitch), :]
                for m in range(z.members)
            ]
            for v in range(z.vars):
                total = None
                for m in range(z.members):
                    term = fine[m] * pert_ref[m, l, v, :, cols].astype(jnp.float32)
                    total = term if total is None else total + term
                inc[l * z.vars + v, :, cols] = total
        return carry

    lax.fori_loop(0, z.levels, level, 0)

    where, _ = split2(cells_ref[...], z.bcells)
    ids = lax.broadcasted_iota(jnp.int32, (z.fine, z.obs), 0)
    here = ids == where
    for l in range(z.levels):
        part = inc[l * z.vars : (l + 1) * z.vars].reshape(z.vars * z.fine, z.bcells)
        hi, lo = hi_lo(part)
        seen = jnp.dot(hi, column_ref[...], preferred_element_type=jnp.float32) + jnp.dot(
            lo, column_ref[...], preferred_element_type=jnp.float32
        )
        for v in range(z.vars):
            s = l * z.vars + v
            got = jnp.where(here, seen[v * z.fine : (v + 1) * z.fine], 0.0)
            seen_ref[s : s + 1, : z.obs] = jnp.sum(got, axis=0, keepdims=True)
    seen_ref[:, z.obs :] = jnp.zeros((z.slabs, LANES), jnp.float32)
    for g in range(z.n_mem):
        mine = slice(g * z.slab_dev, (g + 1) * z.slab_dev)
        seen_ref[mine, : z.obs] -= jnp.where(g == me, dep_ref[...], 0.0)
    for j in range(z.slab_dev):
        for t in range(z.ot):
            at = j * z.ot + t
            seen_ref[at : at + 1, z.obs :] = ow_ref[j : j + 1, t * LANES : (t + 1) * LANES]
    for s in range(z.n_mem):
        to = lax.rem(me + s, z.n_mem)
        for j in range(z.slab_dev):
            inc_refs[s][j] = inc[to * z.slab_dev + j]


def adjoint_kernel(z, *refs):
    blocks_ref, count_ref = refs[:2]
    seen_refs = refs[2 : 2 + z.n_mem]
    w_ref, pert_ref, cells_ref, column_ref, rate_ref = refs[2 + z.n_mem : 7 + z.n_mem]
    out_ref, keep_ref, send_ref = refs[7 + z.n_mem : 10 + z.n_mem]
    every, field, other, fine_ref, force, obs_w = refs[10 + z.n_mem :]
    me = lax.axis_index("mem")
    total = None
    for s in range(z.n_mem):
        part = seen_refs[s][:, : z.obs]
        total = part if total is None else total + part
        obs_w[lax.rem(me + (z.n_mem - s), z.n_mem)] = seen_refs[s][:, z.obs :]
    used = lane_ids((1, z.obs)) < count_ref[0, 0]
    where, _ = split2(cells_ref[...], z.bcells)
    ids = lax.broadcasted_iota(jnp.int32, (z.fine, z.obs), 0)
    here = ids == where
    rows = []
    for s in range(z.slabs):
        g, j = divmod(s, z.slab_dev)
        w = jnp.concatenate([obs_w[g, j * z.ot + t : j * z.ot + t + 1] for t in range(z.ot)], axis=1)
        rows.append(jnp.where(used, w * total[s : s + 1], 0.0))
    for j in range(z.slab_dev):
        mine = rows[j]
        for g in range(1, z.n_mem):
            mine = jnp.where(g == me, rows[g * z.slab_dev + j], mine)
        out_ref[j : j + 1] = mine
    dims = (((1,), (1,)), ((), ()))
    for l in range(z.levels):
        his, los = [], []
        for v in range(z.vars):
            row = jnp.where(here, rows[l * z.vars + v], 0.0)
            hi, lo = hi_lo(row)
            his.append(hi)
            los.append(lo)
        part = lax.dot_general(
            jnp.concatenate(his, axis=0), column_ref[...], dims, preferred_element_type=jnp.float32
        ) + lax.dot_general(
            jnp.concatenate(los, axis=0), column_ref[...], dims, preferred_element_type=jnp.float32
        )
        force[l * z.vars : (l + 1) * z.vars] = part.reshape(z.vars, z.fine, z.bcells)

    pitch = z.fine + PITCH_PAD

    def level(l, carry):
        for t in range(z.ct):
            cols = slice(t * LANES, (t + 1) * LANES)
            f = [force[l * z.vars + v, :, cols] for v in range(z.vars)]
            for m in range(z.members):
                grad = None
                for v in range(z.vars):
                    term = f[v] * pert_ref[m, l, v, :, cols].astype(jnp.float32)
                    grad = term if grad is None else grad + term
                start = pl.multiple_of((m * z.levels + l) * pitch, SUB)
                fine_ref[t, pl.ds(start, z.fine), :] = grad
        return carry

    lax.fori_loop(0, z.levels, level, 0)
    other[...] = jnp.zeros(other.shape, jnp.float32)
    half = lane_ids((z.rows, LANES)) // z.block

    def fine_block(f, carry):
        at, g = z.block_place(blocks_ref[f])
        grad = jnp.concatenate(
            [fine_ref[t, pl.ds(f, z.rows, stride=pitch), :] for t in range(z.ct)], axis=1
        )
        hi, lo = hi_lo(grad)
        out = lax.dot_general(
            jnp.concatenate([hi, lo], axis=0),
            w_ref[f, z.block :, :],
            dims,
            preferred_element_type=jnp.float32,
        )
        out = out[: z.rows] + out[z.rows :]
        out = out + rolled(out, z.block)
        out = jnp.where(half == g, out, 0.0)
        other[at] += out.reshape(z.rg, SUB, LANES)
        return carry

    lax.fori_loop(0, z.fine, fine_block, 0, unroll=16)
    swap_blocks(z, other, 0, field, 1)

    lane_y = lane_ids((z.rg, SUB, LANES)) % z.ny
    for _ in range(SWEEPS):

        def scale(x, carry):
            other[x + 1] = rate_ref[x] * field[x + 1]
            return carry

        lax.fori_loop(0, z.xl, scale, 0, unroll=4)
        fill_edges(z, other)

        def row(x, carry):
            c, near = beside(z, other, x, lane_y)
            field[x + 1] = field[x + 1] + near - 4.0 * c
            return carry

        lax.fori_loop(0, z.xl, row, 0, unroll=True)

    group = lane_ids((z.rg, SUB, LANES)) // z.cy
    packed = {}
    for xl, pieces in enumerate(z.pieces()):
        for tile, xq, q, to in pieces:
            packed.setdefault((tile, xq), []).append((xl, q, to))
    for (tile, xq), parts in packed.items():
        total = None
        for xl, q, to in parts:
            v = rolled(field[xl + 1], (q - to) * z.cy)
            total = v if total is None else jnp.where(group == q, v, total)
        every[tile, xq * z.rg : (xq + 1) * z.rg] = total
    for s in range(z.chips):
        keep_ref[s] = every[z.tile_at(s, False, False)]
        send_ref[s] = every[z.tile_at(s, False, True)]


def finish_kernel(z, alpha_ref, *refs):
    out_ref = refs[-1]
    total = refs[0][...]
    for ref in refs[1:-1]:
        total = total + ref[...]
    for x in range(z.cx):
        q, xq = divmod(x, z.xq)
        part = total[xq * z.rg : (xq + 1) * z.rg, :, q * z.cy : (q + 1) * z.cy]
        out_ref[:, x, :] = alpha_ref[:, x, :] + part.reshape(z.rows, z.cy)


def on_device(
    alpha,
    filter_rate,
    block_list,
    interp_weights,
    perturbations,
    obs_cells,
    obs_count,
    departures,
    obs_weight,
):
    z = Sizes(alpha, interp_weights, perturbations, obs_cells, departures)
    f32, bf16 = jnp.float32, jnp.bfloat16
    shape = jax.ShapeDtypeStruct
    coarse = alpha.reshape(z.rows, z.cx, z.cy)
    wanted = block_list.reshape(z.fine)
    weights = interp_weights.reshape(z.fine, z.block, z.bcells)
    cells = obs_cells.reshape(1, z.obs)
    dep = departures.reshape(z.slab_dev, z.obs)
    ow = obs_weight.reshape(z.slab_dev, z.obs)
    axes = ("tx", "ty")
    tile_shape = (z.t_rows, SUB, LANES)
    full_shape = (z.t_rows + 1, SUB, LANES)
    grid_shape = (z.xl + 2, z.rg, SUB, LANES)

    own = pl.pallas_call(
        functools.partial(pack_kernel, z),
        out_shape=shape(full_shape, f32),
        in_specs=[HB, HB],
        out_specs=VM,
        scratch_shapes=[
            pltpu.VMEM(coarse.shape, f32),
            pltpu.VMEM(filter_rate.shape, f32),
            pltpu.SemaphoreType.DMA((2,)),
        ],
        compiler_params=params(8),
        name="pack",
    )(coarse, filter_rate)
    tiles = [own]
    for s in range(1, z.chips):
        tiles.append(lax.ppermute(own, axes, z.chip_perm(s)))
    for s in range(z.chips):
        tiles.append(lax.ppermute(tiles[s], axes, z.core_perm()))

    stacked, column = pl.pallas_call(
        functools.partial(prep_kernel, z),
        out_shape=(shape((z.fine, 3 * z.block, z.bcells), bf16), shape((z.bcells, z.obs), bf16)),
        in_specs=[VM, VM],
        out_specs=(VM, VM),
        compiler_params=params(16),
        cost_estimate=pl.CostEstimate(flops=4_000_000, bytes_accessed=5_000_000, transcendentals=0),
        name="prep",
    )(weights, cells)

    pitch = z.rows + PITCH_PAD
    slab_shape = (z.slab_dev, z.fine, z.bcells)
    outs = pl.pallas_call(
        functools.partial(forward_kernel, z),
        out_shape=(
            shape((z.slabs, z.obs + LANES), f32),
            shape((z.xl, SUB, LANES), f32),
            *[shape(slab_shape, f32)] * z.n_mem,
        ),
        in_specs=[SM] + [VM] * (z.tiles + 6),
        out_specs=(VM,) * (2 + z.n_mem),
        scratch_shapes=[
            pltpu.VMEM((z.tiles, *full_shape), f32),
            pltpu.VMEM(grid_shape, f32),
            pltpu.VMEM(grid_shape, f32),
            pltpu.VMEM((z.ct, z.fine * pitch, LANES), f32),
            pltpu.VMEM((z.slabs, z.fine, z.bcells), f32),
        ],
        compiler_params=params(24),
        cost_estimate=pl.CostEstimate(flops=20_000_000, bytes_accessed=8_000_000, transcendentals=0),
        name="forward",
    )(wanted, *tiles, stacked, perturbations, cells, column, dep, ow)
    seen, rate, incs = outs[0], outs[1], outs[2:]

    def ring(step):
        return [(i, (i + step) % z.n_mem) for i in range(z.n_mem)]

    steps = range(1, z.n_mem)
    seens, parts = [seen], []
    for s in steps:
        seens.append(lax.ppermute(seen, "mem", ring(s)))
    for s in steps:
        parts.append(lax.ppermute(incs[s], "mem", ring(s)))

    pitch = z.fine + PITCH_PAD
    weighted, keep, send = pl.pallas_call(
        functools.partial(adjoint_kernel, z),
        out_shape=(
            shape((z.slab_dev, z.obs), f32),
            shape((z.chips, *tile_shape), f32),
            shape((z.chips, *tile_shape), f32),
        ),
        in_specs=[SM, SM] + [VM] * (z.n_mem + 5),
        out_specs=(VM, VM, VM),
        scratch_shapes=[
            pltpu.VMEM((z.tiles, *tile_shape), f32),
            pltpu.VMEM(grid_shape, f32),
            pltpu.VMEM(grid_shape, f32),
            pltpu.VMEM((z.ct, z.rows * pitch, LANES), f32),
            pltpu.VMEM((z.slabs, z.fine, z.bcells), f32),
            pltpu.VMEM((z.n_mem, z.slabs, LANES), f32),
        ],
        compiler_params=params(24),
        cost_estimate=pl.CostEstimate(flops=20_000_000, bytes_accessed=8_000_000, transcendentals=0),
        name="adjoint",
    )(wanted, obs_count, *seens, stacked, perturbations, cells, column, rate)

    came = lax.ppermute(send, axes, z.core_perm())
    sums = [keep[s] + came[s] for s in range(z.chips)]
    sums = [sums[0]] + [lax.ppermute(sums[s], axes, z.chip_perm(s)) for s in range(1, z.chips)]
    gradient = pl.pallas_call(
        functools.partial(finish_kernel, z),
        out_shape=shape((z.rows, z.cx, z.cy), f32),
        in_specs=[VM] * (1 + z.chips),
        out_specs=VM,
        compiler_params=params(8),
        name="finish",
    )(coarse, *sums)
    increment = incs[0]
    for part in parts:
        increment = increment + part
    return (increment, weighted.reshape(departures.shape), gradient.reshape(alpha.shape))


def solution(mesh):
    return jax.shard_map(
        on_device,
        mesh=mesh,
        in_specs=(
            P("mem", None, "tx", "ty"),
            P("tx", "ty"),
            P("tx", "ty", None),
            P("tx", "ty", None, None, None),
            P("mem", None, None, ("tx", "ty"), None),
            P("tx", "ty", None),
            P("tx", "ty"),
            P("tx", "ty", "mem", None),
            P("tx", "ty", "mem", None),
        ),
        out_specs=(
            P("mem", ("tx", "ty"), None),
            P("tx", "ty", "mem", None),
            P("mem", None, "tx", "ty"),
        ),
        check_vma=False,
    )
```

profile of v0, /device:TPU:0, one launch (start us, length us, event | category | flops | bytes accessed | tf_op | source)
XLA Modules:
  0.0 52.9 jit_solution(13586506025674509694)
XLA Ops:
  0.7 1.1 %copy-done.2 = f32[8,4,16,32]{3,2,1,0:T(8,128)S(1)} copy-done((f32[8,4,16,32]{3,2,1,0:T(8,128)S(1)}, f32[8,4,16,32]{3,2,1,0:T(8,128)}, u32[]{:S(2)}) %copy-start.2) | copy-done | bytes 65560
  1.7 0.7 %copy-done.7 = f32[16,32]{1,0:T(8,128)S(1)} copy-done((f32[16,32]{1,0:T(8,128)S(1)}, f32[16,32]{1,0:T(8,128)}, u32[]{:S(2)}) %copy-start.7) | copy-done | bytes 2072
  2.7 3.0 %collective-permute-start = (f32[17,8,128]{2,1,0:T(8,128)S(1)}, f32[17,8,128]{2,1,0:T(8,128)S(1)}, u32[]{:S(2)}, u32[]{:S(2)}) collective-permute-start(f32[17,8,128]{2,1,0:T(8,128)S(1)} %pack.1.refs_1_), channel_id=1, source_target_pairs={{0,1},{1,0},{2,3},{3,2},{4,5},{5,4},{6,7},{7,6},{8,9},{9,8},{10,11... | collective-permute-start | bytes 208904 | tf_op jit(solution)/shard_map/ppermute | solution.py:457
  5.7 1.5 %collective-permute-start.1 = (f32[17,8,128]{2,1,0:T(8,128)S(1)}, f32[17,8,128]{2,1,0:T(8,128)S(1)}, u32[]{:S(2)}, u32[]{:S(2)}) collective-permute-start(f32[17,8,128]{2,1,0:T(8,128)S(1)} %pack.1.refs_1_), channel_id=1, source_target_pairs={{0,4},{1,5},{2,6},{3,7},{4,0},{5,1},{6,2},{7,3},{8,12},{9,13},{10,... | collective-permute-start | bytes 208904 | tf_op jit(solution)/shard_map/ppermute | solution.py:457
  7.2 0.9 %collective-permute-done.refs_2_ = f32[17,8,128]{2,1,0:T(8,128)S(1)} collective-permute-done((f32[17,8,128]{2,1,0:T(8,128)S(1)}, f32[17,8,128]{2,1,0:T(8,128)S(1)}, u32[]{:S(2)}, u32[]{:S(2)}) %collective-permute-start) | collective-permute-done | bytes 69664 | tf_op jit(solution)/shard_map/ppermute | solution.py:457
  8.1 1.9 %collective-permute-done.1.refs_3_ = f32[17,8,128]{2,1,0:T(8,128)S(1)} collective-permute-done((f32[17,8,128]{2,1,0:T(8,128)S(1)}, f32[17,8,128]{2,1,0:T(8,128)S(1)}, u32[]{:S(2)}, u32[]{:S(2)}) %collective-permute-start.1) | collective-permute-done | bytes 69664 | tf_op jit(solution)/shard_map/ppermute | solution.py:457
  10.0 2.4 %collective-permute-done.2.refs_4_ = f32[17,8,128]{2,1,0:T(8,128)S(1)} collective-permute-done((f32[17,8,128]{2,1,0:T(8,128)S(1)}, f32[17,8,128]{2,1,0:T(8,128)S(1)}, u32[]{:S(2)}, u32[]{:S(2)}) %collective-permute-start.2) | collective-permute-done | bytes 69664 | tf_op jit(solution)/shard_map/ppermute | solution.py:457
  12.4 1.6 %copy-done.1 = f32[1,1,32,64,256]{4,3,2,1,0:T(8,128)S(1)} copy-done((f32[1,1,32,64,256]{4,3,2,1,0:T(8,128)S(1)}, f32[1,1,32,64,256]{4,3,2,1,0:T(8,128)}, u32[]{:S(2)}) %copy-start.1) | copy-done | bytes 2097176
  14.0 0.7 %copy-done.4 = s32[1,1,512]{2,1,0:T(1,128)S(1)} copy-done((s32[1,1,512]{2,1,0:T(1,128)S(1)}, s32[1,1,512]{2,1,0:T(1,128)}, u32[]{:S(2)}) %copy-start.4) | copy-done | bytes 2072
  15.4 5.2 %forward.1 = (f32[16,640]{1,0:T(8,128)S(1)}, f32[32,8,128]{2,1,0:T(8,128)S(1)}, f32[4,32,256]{2,1,0:T(8,128)S(1)}, f32[4,32,256]{2,1,0:T(8,128)S(1)}, f32[4,32,2...) custom-call(s32[32]{0:T(128)S(1)} %bitcast.24, f32[17,8,128]{2,1,0:T(8,128)S(1)} %pack.1.refs_1_, ...), custom_call_target="tpu_custom_call" | custom-call | flops 20000000 | bytes 8000000 | tf_op jit(solution)/shard_map/forward/pallas_call | solution.py:473
  20.6 1.6 %collective-permute-start.10 = (f32[16,640]{1,0:T(8,128)S(1)}, f32[16,640]{1,0:T(8,128)S(1)}, u32[]{:S(2)}, u32[]{:S(2)}) collective-permute-start(f32[16,640]{1,0:T(8,128)S(1)} %get-tuple-element.20.refs_2_), channel_id=1, source_target_pairs={{0,8},{8,16},{16,24},{24,0},{1,9},{9,17},{17,25},{25,1},{2,10},{10... | collective-permute-start | bytes 122888 | tf_op jit(solution)/shard_map/ppermute | solution.py:501
  22.2 2.6 %collective-permute-start.11 = (f32[16,640]{1,0:T(8,128)S(1)}, f32[16,640]{1,0:T(8,128)S(1)}, u32[]{:S(2)}, u32[]{:S(2)}) collective-permute-start(f32[16,640]{1,0:T(8,128)S(1)} %get-tuple-element.20.refs_2_), channel_id=1, source_target_pairs={{0,16},{8,24},{16,0},{24,8},{1,17},{9,25},{17,1},{25,9},{2,18},{10... | collective-permute-start | bytes 122888 | tf_op jit(solution)/shard_map/ppermute | solution.py:501
  24.8 1.3 %collective-permute-start.12 = (f32[16,640]{1,0:T(8,128)S(1)}, f32[16,640]{1,0:T(8,128)S(1)}, u32[]{:S(2)}, u32[]{:S(2)}) collective-permute-start(f32[16,640]{1,0:T(8,128)S(1)} %get-tuple-element.20.refs_2_), channel_id=1, source_target_pairs={{0,24},{8,0},{16,8},{24,16},{1,25},{9,1},{17,9},{25,17},{2,26},{10... | collective-permute-start | bytes 122888 | tf_op jit(solution)/shard_map/ppermute | solution.py:501
  26.8 1.6 %collective-permute-done.11.refs_4_ = f32[16,640]{1,0:T(8,128)S(1)} collective-permute-done((f32[16,640]{1,0:T(8,128)S(1)}, f32[16,640]{1,0:T(8,128)S(1)}, u32[]{:S(2)}, u32[]{:S(2)}) %collective-permute-start.11) | collective-permute-done | bytes 40992 | tf_op jit(solution)/shard_map/ppermute | solution.py:501
  28.8 6.2 %adjoint.1 = (f32[4,512]{1,0:T(4,128)}, f32[4,16,8,128]{3,2,1,0:T(8,128)S(1)}, f32[4,16,8,128]{3,2,1,0:T(8,128)S(1)}) custom-call(s32[32]{0:T(128)S(1)} %bitcast.25, s32[1,1]{1,0:T(1,128)S(6)} %copy.12.refs_1_, f32[16,640]{1,0:T(8,128)S(1)} %get-tuple-element.20.refs_2_, f32[16,640]{1,0:T(8,128)S(1)} %collective-permute-done.10.refs_3_, ...), custom_call_target="tpu_custom_call" | custom-call | flops 20000000 | bytes 8000000 | tf_op jit(solution)/shard_map/adjoint/pallas_call | solution.py:506
  35.1 3.1 %collective-permute-start.9 = (f32[4,32,256]{2,1,0:T(8,128)S(1)}, f32[4,32,256]{2,1,0:T(8,128)S(1)}, u32[]{:S(2)}, u32[]{:S(2)}) collective-permute-start(f32[4,32,256]{2,1,0:T(8,128)S(1)} %get-tuple-element.19), channel_id=1, source_target_pairs={{0,24},{8,0},{16,8},{24,16},{1,25},{9,1},{17,9},{25,17},{2,26},{10... | collective-permute-start | bytes 393224 | tf_op jit(solution)/shard_map/ppermute | solution.py:503
  38.2 0.6 %collective-permute-start.7 = (f32[4,32,256]{2,1,0:T(8,128)S(1)}, f32[4,32,256]{2,1,0:T(8,128)S(1)}, u32[]{:S(2)}, u32[]{:S(2)}) collective-permute-start(f32[4,32,256]{2,1,0:T(8,128)S(1)} %get-tuple-element.17), channel_id=1, source_target_pairs={{0,8},{8,16},{16,24},{24,0},{1,9},{9,17},{17,25},{25,1},{2,10},{10... | collective-permute-start | bytes 393224 | tf_op jit(solution)/shard_map/ppermute | solution.py:503
  38.8 0.6 %collective-permute-start.14 = (f32[16,8,128]{2,1,0:T(8,128)S(1)}, f32[16,8,128]{2,1,0:T(8,128)S(1)}, u32[]{:S(2)}, u32[]{:S(2)}) collective-permute-start(f32[16,8,128]{2,1,0:T(8,128)S(1)} %get-tuple-element.27), channel_id=1, source_target_pairs={{0,1},{1,0},{2,3},{3,2},{4,5},{5,4},{6,7},{7,6},{8,9},{9,8},{10,11... | collective-permute-start | bytes 196616 | tf_op jit(solution)/shard_map/ppermute | solution.py:530
  39.4 0.5 collective-permute-start.15
  39.9 2.3 %collective-permute-done.9 = f32[4,32,256]{2,1,0:T(8,128)S(1)} collective-permute-done((f32[4,32,256]{2,1,0:T(8,128)S(1)}, f32[4,32,256]{2,1,0:T(8,128)S(1)}, u32[]{:S(2)}, u32[]{:S(2)}) %collective-permute-start.9) | collective-permute-done | bytes 131104 | tf_op jit(solution)/shard_map/ppermute | solution.py:503
  42.2 0.5 collective-permute-start.16
  42.7 7.7 %collective-permute-done.8 = f32[4,32,256]{2,1,0:T(8,128)S(1)} collective-permute-done((f32[4,32,256]{2,1,0:T(8,128)S(1)}, f32[4,32,256]{2,1,0:T(8,128)S(1)}, u32[]{:S(2)}, u32[]{:S(2)}) %collective-permute-start.8) | collective-permute-done | bytes 131104 | tf_op jit(solution)/shard_map/ppermute | solution.py:503
  50.3 0.7 %add_add_fusion = f32[4,32,256]{2,1,0:T(8,128)} fusion(f32[4,32,256]{2,1,0:T(8,128)S(1)} %collective-permute-done.9, f32[4,32,256]{2,1,0:T(8,128)S(1)} %collective-permute-done.8, f32[4,32,256]{2,1,0:T(8,128)S(1)} %get-tuple-element.16, f32[4,32,256]{2,1,0:T(8,128)S(1)} %collective-permute-done.7), kind=kLoop, calls=%fused_computation | loop fusion | flops 98304 | bytes 655360 | tf_op jit(solution)/shard_map/add | solution.py:541
  51.1 1.8 %finish.1 = f32[32,16,32]{2,1,0:T(8,128)} custom-call(f32[32,16,32]{2,1,0:T(8,128)S(1)} %bitcast.18, f32[16,8,128]{2,1,0:T(8,128)S(1)} %get-tuple-element.28.refs_0_, f32[16,8,128]{2,1,0:T(8,128)S(1)} %collective-permute-done.14.refs_1_, f32[16,8,128]{2,1,0:T(8,128)S(1)} %collective-permute-done.15.refs_2_, f32[16,8,128]{2,1,0:T(8,128)S(1)} %collective-permute-done.16.refs_3_), custom_call_target="tpu_custom_call" | custom-call | tf_op jit(solution)/shard_map/finish/pallas_call | solution.py:531
  (35 shorter events, 1.4 us)
Async XLA Ops:
  0.6 14.5 %copy-start = (bf16[8,4,4,32,256]{4,3,2,1,0:T(8,128)(2,1)S(1)}, bf16[8,4,4,32,256]{4,3,2,1,0:T(8,128)(2,1)}, u32[]{:S(2)}) copy-start(bf16[8,4,4,32,256]{4,3,2,1,0:T(8,128)(2,1)} %refs_7_.1) | copy-start | bytes 6291460
  0.6 1.1 %copy-start.2 = (f32[8,4,16,32]{3,2,1,0:T(8,128)S(1)}, f32[8,4,16,32]{3,2,1,0:T(8,128)}, u32[]{:S(2)}) copy-start(f32[8,4,16,32]{3,2,1,0:T(8,128)} %param.9) | copy-start | bytes 196612
  1.7 0.7 %copy-start.7 = (f32[16,32]{1,0:T(8,128)S(1)}, f32[16,32]{1,0:T(8,128)}, u32[]{:S(2)}) copy-start(f32[16,32]{1,0:T(8,128)} %rate_hbm.1) | copy-start | bytes 6148
  2.7 5.5 %collective-permute-start = (f32[17,8,128]{2,1,0:T(8,128)S(1)}, f32[17,8,128]{2,1,0:T(8,128)S(1)}, u32[]{:S(2)}, u32[]{:S(2)}) collective-permute-start(f32[17,8,128]{2,1,0:T(8,128)S(1)} %pack.1.refs_1_), channel_id=1, source_target_pairs={{0,1},{1,0},{2,3},{3,2},{4,5},{5,4},{6,7},{7,6},{8,9},{9,8},{10,11... | collective-permute-start | bytes 208904 | tf_op jit(solution)/shard_map/ppermute | solution.py:457
  5.7 4.3 %collective-permute-start.1 = (f32[17,8,128]{2,1,0:T(8,128)S(1)}, f32[17,8,128]{2,1,0:T(8,128)S(1)}, u32[]{:S(2)}, u32[]{:S(2)}) collective-permute-start(f32[17,8,128]{2,1,0:T(8,128)S(1)} %pack.1.refs_1_), channel_id=1, source_target_pairs={{0,4},{1,5},{2,6},{3,7},{4,0},{5,1},{6,2},{7,3},{8,12},{9,13},{10,... | collective-permute-start | bytes 208904 | tf_op jit(solution)/shard_map/ppermute | solution.py:457
  7.2 5.2 %collective-permute-start.2 = (f32[17,8,128]{2,1,0:T(8,128)S(1)}, f32[17,8,128]{2,1,0:T(8,128)S(1)}, u32[]{:S(2)}, u32[]{:S(2)}) collective-permute-start(f32[17,8,128]{2,1,0:T(8,128)S(1)} %pack.1.refs_1_), channel_id=1, source_target_pairs={{0,5},{1,4},{2,7},{3,6},{4,1},{5,0},{6,3},{7,2},{8,13},{9,12},{10,... | collective-permute-start | bytes 208904 | tf_op jit(solution)/shard_map/ppermute | solution.py:457
  7.2 7.8 %collective-permute-start.3 = (f32[17,8,128]{2,1,0:T(8,128)S(1)}, f32[17,8,128]{2,1,0:T(8,128)S(1)}, u32[]{:S(2)}, u32[]{:S(2)}) collective-permute-start(f32[17,8,128]{2,1,0:T(8,128)S(1)} %pack.1.refs_1_), channel_id=1, source_target_pairs={{0,2},{1,3},{2,0},{3,1},{4,6},{5,7},{6,4},{7,5},{8,10},{9,11},{10,... | collective-permute-start | bytes 208904 | tf_op jit(solution)/shard_map/ppermute | solution.py:459
  8.1 6.9 %collective-permute-start.4 = (f32[17,8,128]{2,1,0:T(8,128)S(1)}, f32[17,8,128]{2,1,0:T(8,128)S(1)}, u32[]{:S(2)}, u32[]{:S(2)}) collective-permute-start(f32[17,8,128]{2,1,0:T(8,128)S(1)} %collective-permute-done.refs_2_), channel_id=1, source_target_pairs={{0,2},{1,3},{2,0},{3,1},{4,6},{5,7},{6,4},{7,5},{8,10},{9,11},{10,... | collective-permute-start | bytes 208904 | tf_op jit(solution)/shard_map/ppermute | solution.py:459
  10.0 5.1 %collective-permute-start.5 = (f32[17,8,128]{2,1,0:T(8,128)S(1)}, f32[17,8,128]{2,1,0:T(8,128)S(1)}, u32[]{:S(2)}, u32[]{:S(2)}) collective-permute-start(f32[17,8,128]{2,1,0:T(8,128)S(1)} %collective-permute-done.1.refs_3_), channel_id=1, source_target_pairs={{0,2},{1,3},{2,0},{3,1},{4,6},{5,7},{6,4},{7,5},{8,10},{9,11},{10,... | collective-permute-start | bytes 208904 | tf_op jit(solution)/shard_map/ppermute | solution.py:459
  12.4 2.7 %collective-permute-start.6 = (f32[17,8,128]{2,1,0:T(8,128)S(1)}, f32[17,8,128]{2,1,0:T(8,128)S(1)}, u32[]{:S(2)}, u32[]{:S(2)}) collective-permute-start(f32[17,8,128]{2,1,0:T(8,128)S(1)} %collective-permute-done.2.refs_4_), channel_id=1, source_target_pairs={{0,2},{1,3},{2,0},{3,1},{4,6},{5,7},{6,4},{7,5},{8,10},{9,11},{10,... | collective-permute-start | bytes 208904 | tf_op jit(solution)/shard_map/ppermute | solution.py:459
  12.4 1.6 %copy-start.1 = (f32[1,1,32,64,256]{4,3,2,1,0:T(8,128)S(1)}, f32[1,1,32,64,256]{4,3,2,1,0:T(8,128)}, u32[]{:S(2)}) copy-start(f32[1,1,32,64,256]{4,3,2,1,0:T(8,128)} %param.12) | copy-start | bytes 6291460
  14.7 0.7 %copy-start.6 = (f32[1,1,4,512]{3,2,1,0:T(4,128)S(1)}, f32[1,1,4,512]{3,2,1,0:T(4,128)}, u32[]{:S(2)}) copy-start(f32[1,1,4,512]{3,2,1,0:T(4,128)} %param.17) | copy-start | bytes 24580
  14.7 0.7 %copy-start.8 = (s32[1,1,32]{2,1,0:T(1,128)S(1)}, s32[1,1,32]{2,1,0:T(1,128)}, u32[]{:S(2)}) copy-start(s32[1,1,32]{2,1,0:T(1,128)} %param.11) | copy-start | bytes 388
  20.6 6.2 %collective-permute-start.10 = (f32[16,640]{1,0:T(8,128)S(1)}, f32[16,640]{1,0:T(8,128)S(1)}, u32[]{:S(2)}, u32[]{:S(2)}) collective-permute-start(f32[16,640]{1,0:T(8,128)S(1)} %get-tuple-element.20.refs_2_), channel_id=1, source_target_pairs={{0,8},{8,16},{16,24},{24,0},{1,9},{9,17},{17,25},{25,1},{2,10},{10... | collective-permute-start | bytes 122888 | tf_op jit(solution)/shard_map/ppermute | solution.py:501
  22.2 6.2 %collective-permute-start.11 = (f32[16,640]{1,0:T(8,128)S(1)}, f32[16,640]{1,0:T(8,128)S(1)}, u32[]{:S(2)}, u32[]{:S(2)}) collective-permute-start(f32[16,640]{1,0:T(8,128)S(1)} %get-tuple-element.20.refs_2_), channel_id=1, source_target_pairs={{0,16},{8,24},{16,0},{24,8},{1,17},{9,25},{17,1},{25,9},{2,18},{10... | collective-permute-start | bytes 122888 | tf_op jit(solution)/shard_map/ppermute | solution.py:501
  24.8 4.0 %collective-permute-start.12 = (f32[16,640]{1,0:T(8,128)S(1)}, f32[16,640]{1,0:T(8,128)S(1)}, u32[]{:S(2)}, u32[]{:S(2)}) collective-permute-start(f32[16,640]{1,0:T(8,128)S(1)} %get-tuple-element.20.refs_2_), channel_id=1, source_target_pairs={{0,24},{8,0},{16,8},{24,16},{1,25},{9,1},{17,9},{25,17},{2,26},{10... | collective-permute-start | bytes 122888 | tf_op jit(solution)/shard_map/ppermute | solution.py:501
  28.8 22.2 %copy-start.3 = (f32[8,4,16,32]{3,2,1,0:T(8,128)S(1)}, f32[8,4,16,32]{3,2,1,0:T(8,128)}, u32[]{:S(2)}) copy-start(f32[8,4,16,32]{3,2,1,0:T(8,128)} %param.9) | copy-start | bytes 196612
  35.1 3.7 %collective-permute-start.13 = (f32[4,16,8,128]{3,2,1,0:T(8,128)S(1)}, f32[4,16,8,128]{3,2,1,0:T(8,128)S(1)}, u32[]{:S(2)}, u32[]{:S(2)}) collective-permute-start(f32[4,16,8,128]{3,2,1,0:T(8,128)S(1)} %get-tuple-element.24), channel_id=1, source_target_pairs={{0,2},{1,3},{2,0},{3,1},{4,6},{5,7},{6,4},{7,5},{8,10},{9,11},{10,... | collective-permute-start | bytes 786440 | tf_op jit(solution)/shard_map/ppermute | solution.py:528
  35.1 7.1 %collective-permute-start.9 = (f32[4,32,256]{2,1,0:T(8,128)S(1)}, f32[4,32,256]{2,1,0:T(8,128)S(1)}, u32[]{:S(2)}, u32[]{:S(2)}) collective-permute-start(f32[4,32,256]{2,1,0:T(8,128)S(1)} %get-tuple-element.19), channel_id=1, source_target_pairs={{0,24},{8,0},{16,8},{24,16},{1,25},{9,1},{17,9},{25,17},{2,26},{10... | collective-permute-start | bytes 393224 | tf_op jit(solution)/shard_map/ppermute | solution.py:503
  38.2 12.1 %collective-permute-start.8 = (f32[4,32,256]{2,1,0:T(8,128)S(1)}, f32[4,32,256]{2,1,0:T(8,128)S(1)}, u32[]{:S(2)}, u32[]{:S(2)}) collective-permute-start(f32[4,32,256]{2,1,0:T(8,128)S(1)} %get-tuple-element.18), channel_id=1, source_target_pairs={{0,16},{8,24},{16,0},{24,8},{1,17},{9,25},{17,1},{25,9},{2,18},{10... | collective-permute-start | bytes 393224 | tf_op jit(solution)/shard_map/ppermute | solution.py:503
  38.2 12.1 %collective-permute-start.7 = (f32[4,32,256]{2,1,0:T(8,128)S(1)}, f32[4,32,256]{2,1,0:T(8,128)S(1)}, u32[]{:S(2)}, u32[]{:S(2)}) collective-permute-start(f32[4,32,256]{2,1,0:T(8,128)S(1)} %get-tuple-element.17), channel_id=1, source_target_pairs={{0,8},{8,16},{16,24},{24,0},{1,9},{9,17},{17,25},{25,1},{2,10},{10... | collective-permute-start | bytes 393224 | tf_op jit(solution)/shard_map/ppermute | solution.py:503
  38.8 12.2 %collective-permute-start.14 = (f32[16,8,128]{2,1,0:T(8,128)S(1)}, f32[16,8,128]{2,1,0:T(8,128)S(1)}, u32[]{:S(2)}, u32[]{:S(2)}) collective-permute-start(f32[16,8,128]{2,1,0:T(8,128)S(1)} %get-tuple-element.27), channel_id=1, source_target_pairs={{0,1},{1,0},{2,3},{3,2},{4,5},{5,4},{6,7},{7,6},{8,9},{9,8},{10,11... | collective-permute-start | bytes 196616 | tf_op jit(solution)/shard_map/ppermute | solution.py:530
  39.4 11.6 %collective-permute-start.15 = (f32[16,8,128]{2,1,0:T(8,128)S(1)}, f32[16,8,128]{2,1,0:T(8,128)S(1)}, u32[]{:S(2)}, u32[]{:S(2)}) collective-permute-start(f32[16,8,128]{2,1,0:T(8,128)S(1)} %get-tuple-element.26), channel_id=1, source_target_pairs={{0,4},{1,5},{2,6},{3,7},{4,0},{5,1},{6,2},{7,3},{8,12},{9,13},{10,... | collective-permute-start | bytes 196616 | tf_op jit(solution)/shard_map/ppermute | solution.py:530
  42.2 8.9 %collective-permute-start.16 = (f32[16,8,128]{2,1,0:T(8,128)S(1)}, f32[16,8,128]{2,1,0:T(8,128)S(1)}, u32[]{:S(2)}, u32[]{:S(2)}) collective-permute-start(f32[16,8,128]{2,1,0:T(8,128)S(1)} %get-tuple-element.25), channel_id=1, source_target_pairs={{0,5},{1,4},{2,7},{3,6},{4,1},{5,0},{6,3},{7,2},{8,13},{9,12},{10,... | collective-permute-start | bytes 196616 | tf_op jit(solution)/shard_map/ppermute | solution.py:530
  (2 other events, 1.4 us)
where the time goes:
time: 53.2 us; the launch traced here: 52.9 us
  waiting for transfers between devices  17.2 us (32%)
  starting transfers between devices  15.4 us (29%)
  Pallas kernels  13.8 us (26%)
  local copies, waits for them, and re-layouts  4.38 us (8%)
  between operations  1.4 us (3%)
  other arithmetic  0.74 us (1%)
    ppermute x3, waiting for transfers between devices, on_device(): parts.append(lax.ppermute(incs[s], 'mem', ring(s)))  9.94 us
    pallas_call x1, Pallas kernels, on_device(): pl.pallas_call(functools.partial(adjoint_kernel, z), out_shape=(shape((z....  6.24 us
    ppermute x3, starting transfers between devices, on_device(): seens.append(lax.ppermute(seen, 'mem', ring(s)))  5.56 us
    ppermute x3, waiting for transfers between devices, on_device(): tiles.append(lax.ppermute(own, axes, z.chip_perm(s)))  5.18 us
    pallas_call x1, Pallas kernels, on_device(): pl.pallas_call(functools.partial(forward_kernel, z), out_shape=(shape((z....  5.15 us
    ppermute x3, starting transfers between devices, on_device(): tiles.append(lax.ppermute(own, axes, z.chip_perm(s)))  4.57 us
    unnamed x18, local copies, waits for them, and re-layouts  4.38 us
    ppermute x3, starting transfers between devices, on_device(): parts.append(lax.ppermute(incs[s], 'mem', ring(s)))  3.68 us
  transfers between devices with their start and end apart: 17, of which 7 were waited for; matrix products, arithmetic and copies ran while one was open for 1% of the time, Pallas kernels for 1%

commit v1 on v0

--- a/solution.py
+++ b/solution.py
@@ -13,11 +13,16 @@
 LANES = 128
 SUB = 8
 PITCH_PAD = 8
+PREP_CHUNKS = 4
 
 
 VM = pl.BlockSpec(memory_space=pltpu.VMEM)
 HB = pl.BlockSpec(memory_space=pltpu.HBM)
 SM = pl.BlockSpec(memory_space=pltpu.SMEM)
+
+
+def in_hbm(v):
+    return pltpu.with_memory_space_constraint(v, pltpu.HBM)
 
 
 def params(mib):
@@ -135,8 +140,25 @@
         out_ref[z.t_rows, xq : xq + 1, lanes] = rate_ref[x : x + 1, :]
 
 
-def prep_kernel(z, weights_ref, cells_ref, stacked_ref, column_ref):
+def prep_kernel(z, *refs):
+    weights_hbm, cells_hbm, count_ref, stacked_ref, column_ref, used_ref = refs[:6]
+    weights_ref, cells_ref, sems = refs[6:]
     k = z.block
+    chunk = z.fine // PREP_CHUNKS
+    copies = []
+    for i in range(PREP_CHUNKS):
+        part = pl.ds(i * chunk, chunk)
+        copies.append(
+            pltpu.make_async_copy(weights_hbm.at[part], weights_ref.at[part], sems.at[i])
+        )
+    cells_copy = pltpu.make_async_copy(cells_hbm, cells_ref, sems.at[PREP_CHUNKS])
+    for copy in [cells_copy] + copies:
+        copy.start()
+    used_ref[...] = jnp.where(lane_ids((1, z.obs)) < count_ref[0, 0], 1.0, 0.0)
+    cells_copy.wait()
+    _, col = split2(cells_ref[...], z.bcells)
+    ids = lax.broadcasted_iota(jnp.int32, (z.bcells, z.obs), 0)
+    column_ref[...] = jnp.where(ids == col, 1.0, 0.0).astype(jnp.bfloat16)
 
     def one(f, carry):
         hi, lo = hi_lo(weights_ref[f])
@@ -145,10 +167,9 @@
         stacked_ref[f, 2 * k : 3 * k, :] = lo
         return carry
 
-    lax.fori_loop(0, z.fine, one, 0, unroll=2)
-    _, col = split2(cells_ref[...], z.bcells)
-    ids = lax.broadcasted_iota(jnp.int32, (z.bcells, z.obs), 0)
-    column_ref[...] = jnp.where(ids == col, 1.0, 0.0).astype(jnp.bfloat16)
+    for i in range(PREP_CHUNKS):
+        copies[i].wait()
+        lax.fori_loop(i * chunk, (i + 1) * chunk, one, 0, unroll=2)
 
 
 def fill_edges(z, ref):
@@ -290,7 +311,7 @@
 
 
 def adjoint_kernel(z, *refs):
-    blocks_ref, count_ref = refs[:2]
+    blocks_ref, used_ref = refs[:2]
     seen_refs = refs[2 : 2 + z.n_mem]
     w_ref, pert_ref, cells_ref, column_ref, rate_ref = refs[2 + z.n_mem : 7 + z.n_mem]
     out_ref, keep_ref, send_ref = refs[7 + z.n_mem : 10 + z.n_mem]
@@ -301,7 +322,7 @@
         part = seen_refs[s][:, : z.obs]
         total = part if total is None else total + part
         obs_w[lax.rem(me + (z.n_mem - s), z.n_mem)] = seen_refs[s][:, z.obs :]
-    used = lane_ids((1, z.obs)) < count_ref[0, 0]
+    used = used_ref[...] > 0.5
     where, _ = split2(cells_ref[...], z.bcells)
     ids = lax.broadcasted_iota(jnp.int32, (z.fine, z.obs), 0)
     here = ids == where
@@ -451,22 +472,31 @@
         ],
         compiler_params=params(8),
         name="pack",
-    )(coarse, filter_rate)
+    )(in_hbm(coarse), in_hbm(filter_rate))
     tiles = [own]
     for s in range(1, z.chips):
         tiles.append(lax.ppermute(own, axes, z.chip_perm(s)))
     for s in range(z.chips):
         tiles.append(lax.ppermute(tiles[s], axes, z.core_perm()))
 
-    stacked, column = pl.pallas_call(
+    stacked, column, used = pl.pallas_call(
         functools.partial(prep_kernel, z),
-        out_shape=(shape((z.fine, 3 * z.block, z.bcells), bf16), shape((z.bcells, z.obs), bf16)),
-        in_specs=[VM, VM],
-        out_specs=(VM, VM),
+        out_shape=(
+            shape((z.fine, 3 * z.block, z.bcells), bf16),
+            shape((z.bcells, z.obs), bf16),
+            shape((1, z.obs), f32),
+        ),
+        in_specs=[HB, HB, SM],
+        out_specs=(VM, VM, VM),
+        scratch_shapes=[
+            pltpu.VMEM(weights.shape, f32),
+            pltpu.VMEM(cells.shape, jnp.int32),
+            pltpu.SemaphoreType.DMA((PREP_CHUNKS + 1,)),
+        ],
         compiler_params=params(16),
         cost_estimate=pl.CostEstimate(flops=4_000_000, bytes_accessed=5_000_000, transcendentals=0),
         name="prep",
-    )(weights, cells)
+    )(in_hbm(weights), in_hbm(cells), obs_count)
 
     pitch = z.rows + PITCH_PAD
     slab_shape = (z.slab_dev, z.fine, z.bcells)
@@ -510,7 +540,7 @@
             shape((z.chips, *tile_shape), f32),
             shape((z.chips, *tile_shape), f32),
         ),
-        in_specs=[SM, SM] + [VM] * (z.n_mem + 5),
+        in_specs=[SM] + [VM] * (z.n_mem + 6),
         out_specs=(VM, VM, VM),
         scratch_shapes=[
             pltpu.VMEM((z.tiles, *tile_shape), f32),
@@ -523,7 +553,7 @@
         compiler_params=params(24),
         cost_estimate=pl.CostEstimate(flops=20_000_000, bytes_accessed=8_000_000, transcendentals=0),
         name="adjoint",
-    )(wanted, obs_count, *seens, stacked, perturbations, cells, column, rate)
+    )(wanted, used, *seens, stacked, perturbations, cells, column, rate)
 
     came = lax.ppermute(send, axes, z.core_perm())
     sums = [keep[s] + came[s] for s in range(z.chips)]

time: 53.2 us -> 51.8 us (0.974)
  local copies, waits for them, and re-layouts: 4.38 us -> 0.03 us
  Pallas kernels: 13.8 us -> 16.2 us
  waiting for transfers between devices: 17.2 us -> 17.8 us
    unnamed x18 -> x12, local copies, waits for them, and re-layouts: 4.38 us -> 0.03 us
    pallas_call x1, Pallas kernels: 0.35 us -> 1.65 us  [on_device(): pl.pallas_call(functools.partial(prep_kernel, z), out_shape=(shape((z.fin...]
    pallas_call x1, Pallas kernels: 0.22 us -> 1.29 us  [on_device(): pl.pallas_call(functools.partial(pack_kernel, z), out_shape=shape(full_sh...]
    ppermute x3, waiting for transfers between devices: 2.03 us -> 2.69 us  [on_device(): seens.append(lax.ppermute(seen, 'mem', ring(s)))]
  transfers between devices with their start and end apart: 17 -> 17, of which waited for: 7 -> 8; matrix products, arithmetic and copies ran while one was open for 1% -> 1% of each run, Pallas kernels for 1% -> 3%
where the time goes in v1:
time: 51.8 us; the launch traced here: 51.6 us
  waiting for transfers between devices  17.8 us (34%)
  Pallas kernels  16.2 us (31%)
  starting transfers between devices  15.4 us (30%)
  between operations  1.44 us (3%)
  other arithmetic  0.72 us (1%)
    ppermute x3, waiting for transfers between devices, on_device(): parts.append(lax.ppermute(incs[s], 'mem', ring(s)))  9.95 us
    pallas_call x1, Pallas kernels, on_device(): pl.pallas_call(functools.partial(adjoint_kernel, z), out_shape=(shape((z....  6.25 us
    ppermute x3, starting transfers between devices, on_device(): seens.append(lax.ppermute(seen, 'mem', ring(s)))  5.57 us
    pallas_call x1, Pallas kernels, on_device(): pl.pallas_call(functools.partial(forward_kernel, z), out_shape=(shape((z....  5.18 us
    ppermute x3, waiting for transfers between devices, on_device(): tiles.append(lax.ppermute(own, axes, z.chip_perm(s)))  5.18 us
    ppermute x3, starting transfers between devices, on_device(): tiles.append(lax.ppermute(own, axes, z.chip_perm(s)))  4.57 us
    ppermute x3, starting transfers between devices, on_device(): parts.append(lax.ppermute(incs[s], 'mem', ring(s)))  3.67 us
    ppermute x3, waiting for transfers between devices, on_device(): seens.append(lax.ppermute(seen, 'mem', ring(s)))  2.69 us
  transfers between devices with their start and end apart: 17, of which 8 were waited for; matrix products, arithmetic and copies ran while one was open for 1% of the time, Pallas kernels for 3%

profile of v1, /device:TPU:0, one launch (start us, length us, event | category | flops | bytes accessed | tf_op | source)
XLA Modules:
  0.0 51.6 jit_solution(8345447250002628277)
XLA Ops:
  0.7 1.3 %pack.1.refs_1_ = f32[17,8,128]{2,1,0:T(8,128)S(1)} custom-call(f32[32,16,32]{2,1,0:T(8,128)} %bitcast.16, f32[16,32]{1,0:T(8,128)} %rate_hbm.1), custom_call_target="tpu_custom_call" | custom-call | tf_op jit(solution)/shard_map/pack/pallas_call | solution.py:463
  2.0 3.0 %collective-permute-start = (f32[17,8,128]{2,1,0:T(8,128)S(1)}, f32[17,8,128]{2,1,0:T(8,128)S(1)}, u32[]{:S(2)}, u32[]{:S(2)}) collective-permute-start(f32[17,8,128]{2,1,0:T(8,128)S(1)} %pack.1.refs_1_), channel_id=1, source_target_pairs={{0,1},{1,0},{2,3},{3,2},{4,5},{5,4},{6,7},{7,6},{8,9},{9,8},{10,11... | collective-permute-start | bytes 208904 | tf_op jit(solution)/shard_map/ppermute | solution.py:478
  5.0 1.5 %collective-permute-start.1 = (f32[17,8,128]{2,1,0:T(8,128)S(1)}, f32[17,8,128]{2,1,0:T(8,128)S(1)}, u32[]{:S(2)}, u32[]{:S(2)}) collective-permute-start(f32[17,8,128]{2,1,0:T(8,128)S(1)} %pack.1.refs_1_), channel_id=1, source_target_pairs={{0,4},{1,5},{2,6},{3,7},{4,0},{5,1},{6,2},{7,3},{8,12},{9,13},{10,... | collective-permute-start | bytes 208904 | tf_op jit(solution)/shard_map/ppermute | solution.py:478
  6.6 0.9 %collective-permute-done.refs_2_ = f32[17,8,128]{2,1,0:T(8,128)S(1)} collective-permute-done((f32[17,8,128]{2,1,0:T(8,128)S(1)}, f32[17,8,128]{2,1,0:T(8,128)S(1)}, u32[]{:S(2)}, u32[]{:S(2)}) %collective-permute-start) | collective-permute-done | bytes 69664 | tf_op jit(solution)/shard_map/ppermute | solution.py:478
  7.5 1.9 %collective-permute-done.1.refs_3_ = f32[17,8,128]{2,1,0:T(8,128)S(1)} collective-permute-done((f32[17,8,128]{2,1,0:T(8,128)S(1)}, f32[17,8,128]{2,1,0:T(8,128)S(1)}, u32[]{:S(2)}, u32[]{:S(2)}) %collective-permute-start.1) | collective-permute-done | bytes 69664 | tf_op jit(solution)/shard_map/ppermute | solution.py:478
  9.3 2.4 %collective-permute-done.2.refs_4_ = f32[17,8,128]{2,1,0:T(8,128)S(1)} collective-permute-done((f32[17,8,128]{2,1,0:T(8,128)S(1)}, f32[17,8,128]{2,1,0:T(8,128)S(1)}, u32[]{:S(2)}, u32[]{:S(2)}) %collective-permute-start.2) | collective-permute-done | bytes 69664 | tf_op jit(solution)/shard_map/ppermute | solution.py:478
  12.4 1.6 %prep.1 = (bf16[32,192,256]{2,1,0:T(8,128)(2,1)S(1)}, bf16[256,512]{1,0:T(8,128)(2,1)S(1)}, f32[1,512]{1,0:T(1,128)S(1)}) custom-call(f32[32,64,256]{2,1,0:T(8,128)} %bitcast.25, s32[1,512]{1,0:T(1,128)} %bitcast.18, s32[1,1]{1,0:T(1,128)S(6)} %copy.12.refs_2_), custom_call_target="tpu_custom_call" | custom-call | flops 4000000 | bytes 5000000 | tf_op jit(solution)/shard_map/prep/pallas_call | solution.py:482
  14.1 5.2 %forward.1 = (f32[16,640]{1,0:T(8,128)S(1)}, f32[32,8,128]{2,1,0:T(8,128)S(1)}, f32[4,32,256]{2,1,0:T(8,128)S(1)}, f32[4,32,256]{2,1,0:T(8,128)S(1)}, f32[4,32,2...) custom-call(s32[32]{0:T(128)S(1)} %bitcast.23, f32[17,8,128]{2,1,0:T(8,128)S(1)} %pack.1.refs_1_, ...), custom_call_target="tpu_custom_call" | custom-call | flops 20000000 | bytes 8000000 | tf_op jit(solution)/shard_map/forward/pallas_call | solution.py:503
  19.3 1.6 %collective-permute-start.10 = (f32[16,640]{1,0:T(8,128)S(1)}, f32[16,640]{1,0:T(8,128)S(1)}, u32[]{:S(2)}, u32[]{:S(2)}) collective-permute-start(f32[16,640]{1,0:T(8,128)S(1)} %get-tuple-element.22.refs_2_), channel_id=1, source_target_pairs={{0,8},{8,16},{16,24},{24,0},{1,9},{9,17},{17,25},{25,1},{2,10},{10... | collective-permute-start | bytes 122888 | tf_op jit(solution)/shard_map/ppermute | solution.py:531
  21.0 2.6 %collective-permute-start.11 = (f32[16,640]{1,0:T(8,128)S(1)}, f32[16,640]{1,0:T(8,128)S(1)}, u32[]{:S(2)}, u32[]{:S(2)}) collective-permute-start(f32[16,640]{1,0:T(8,128)S(1)} %get-tuple-element.22.refs_2_), channel_id=1, source_target_pairs={{0,16},{8,24},{16,0},{24,8},{1,17},{9,25},{17,1},{25,9},{2,18},{10... | collective-permute-start | bytes 122888 | tf_op jit(solution)/shard_map/ppermute | solution.py:531
  23.6 1.3 %collective-permute-start.12 = (f32[16,640]{1,0:T(8,128)S(1)}, f32[16,640]{1,0:T(8,128)S(1)}, u32[]{:S(2)}, u32[]{:S(2)}) collective-permute-start(f32[16,640]{1,0:T(8,128)S(1)} %get-tuple-element.22.refs_2_), channel_id=1, source_target_pairs={{0,24},{8,0},{16,8},{24,16},{1,25},{9,1},{17,9},{25,17},{2,26},{10... | collective-permute-start | bytes 122888 | tf_op jit(solution)/shard_map/ppermute | solution.py:531
  24.9 0.4 collective-permute-done.10.refs_3_
  25.3 1.9 %collective-permute-done.11.refs_4_ = f32[16,640]{1,0:T(8,128)S(1)} collective-permute-done((f32[16,640]{1,0:T(8,128)S(1)}, f32[16,640]{1,0:T(8,128)S(1)}, u32[]{:S(2)}, u32[]{:S(2)}) %collective-permute-start.11) | collective-permute-done | bytes 40992 | tf_op jit(solution)/shard_map/ppermute | solution.py:531
  27.2 0.4 collective-permute-done.12.refs_5_
  27.6 6.2 %adjoint.1 = (f32[4,512]{1,0:T(4,128)}, f32[4,16,8,128]{3,2,1,0:T(8,128)S(1)}, f32[4,16,8,128]{3,2,1,0:T(8,128)S(1)}) custom-call(s32[32]{0:T(128)S(1)} %bitcast.24, f32[1,512]{1,0:T(1,128)S(1)} %get-tuple-element.21.refs_1_, f32[16,640]{1,0:T(8,128)S(1)} %get-tuple-element.22.refs_2_, f32[16,640]{1,0:T(8,128)S(1)} %collective-permute-done.10.refs_3_, ...), custom_call_target="tpu_custom_call" | custom-call | flops 20000000 | bytes 8000000 | tf_op jit(solution)/shard_map/adjoint/pallas_call | solution.py:536
  33.8 3.1 %collective-permute-start.9 = (f32[4,32,256]{2,1,0:T(8,128)S(1)}, f32[4,32,256]{2,1,0:T(8,128)S(1)}, u32[]{:S(2)}, u32[]{:S(2)}) collective-permute-start(f32[4,32,256]{2,1,0:T(8,128)S(1)} %get-tuple-element.20), channel_id=1, source_target_pairs={{0,24},{8,0},{16,8},{24,16},{1,25},{9,1},{17,9},{25,17},{2,26},{10... | collective-permute-start | bytes 393224 | tf_op jit(solution)/shard_map/ppermute | solution.py:533
  37.0 0.6 %collective-permute-start.7 = (f32[4,32,256]{2,1,0:T(8,128)S(1)}, f32[4,32,256]{2,1,0:T(8,128)S(1)}, u32[]{:S(2)}, u32[]{:S(2)}) collective-permute-start(f32[4,32,256]{2,1,0:T(8,128)S(1)} %get-tuple-element.18), channel_id=1, source_target_pairs={{0,8},{8,16},{16,24},{24,0},{1,9},{9,17},{17,25},{25,1},{2,10},{10... | collective-permute-start | bytes 393224 | tf_op jit(solution)/shard_map/ppermute | solution.py:533
  37.6 0.6 %collective-permute-start.14 = (f32[16,8,128]{2,1,0:T(8,128)S(1)}, f32[16,8,128]{2,1,0:T(8,128)S(1)}, u32[]{:S(2)}, u32[]{:S(2)}) collective-permute-start(f32[16,8,128]{2,1,0:T(8,128)S(1)} %get-tuple-element.29), channel_id=1, source_target_pairs={{0,1},{1,0},{2,3},{3,2},{4,5},{5,4},{6,7},{7,6},{8,9},{9,8},{10,11... | collective-permute-start | bytes 196616 | tf_op jit(solution)/shard_map/ppermute | solution.py:560
  38.2 0.5 collective-permute-start.15
  38.7 2.3 %collective-permute-done.9 = f32[4,32,256]{2,1,0:T(8,128)S(1)} collective-permute-done((f32[4,32,256]{2,1,0:T(8,128)S(1)}, f32[4,32,256]{2,1,0:T(8,128)S(1)}, u32[]{:S(2)}, u32[]{:S(2)}) %collective-permute-start.9) | collective-permute-done | bytes 131104 | tf_op jit(solution)/shard_map/ppermute | solution.py:533
  40.9 0.5 collective-permute-start.16
  41.4 7.7 %collective-permute-done.8 = f32[4,32,256]{2,1,0:T(8,128)S(1)} collective-permute-done((f32[4,32,256]{2,1,0:T(8,128)S(1)}, f32[4,32,256]{2,1,0:T(8,128)S(1)}, u32[]{:S(2)}, u32[]{:S(2)}) %collective-permute-start.8) | collective-permute-done | bytes 131104 | tf_op jit(solution)/shard_map/ppermute | solution.py:533
  49.1 0.7 %add_add_fusion = f32[4,32,256]{2,1,0:T(8,128)} fusion(f32[4,32,256]{2,1,0:T(8,128)S(1)} %collective-permute-done.9, f32[4,32,256]{2,1,0:T(8,128)S(1)} %collective-permute-done.8, f32[4,32,256]{2,1,0:T(8,128)S(1)} %get-tuple-element.17, f32[4,32,256]{2,1,0:T(8,128)S(1)} %collective-permute-done.7), kind=kLoop, calls=%fused_computation | loop fusion | flops 98304 | bytes 655360 | tf_op jit(solution)/shard_map/add | solution.py:571
  49.8 1.8 %finish.1 = f32[32,16,32]{2,1,0:T(8,128)} custom-call(f32[32,16,32]{2,1,0:T(8,128)S(1)} %bitcast.17, f32[16,8,128]{2,1,0:T(8,128)S(1)} %get-tuple-element.30.refs_0_, f32[16,8,128]{2,1,0:T(8,128)S(1)} %collective-permute-done.14.refs_1_, f32[16,8,128]{2,1,0:T(8,128)S(1)} %collective-permute-done.15.refs_2_, f32[16,8,128]{2,1,0:T(8,128)S(1)} %collective-permute-done.16.refs_3_), custom_call_target="tpu_custom_call" | custom-call | tf_op jit(solution)/shard_map/finish/pallas_call | solution.py:561
  (29 shorter events, 0.1 us)
Async XLA Ops:
  0.6 13.5 %copy-start.2 = (s32[1,1,512]{2,1,0:T(1,128)S(1)}, s32[1,1,512]{2,1,0:T(1,128)}, u32[]{:S(2)}) copy-start(s32[1,1,512]{2,1,0:T(1,128)} %param.14) | copy-start | bytes 6148
  0.6 13.5 %copy-start.5 = (s32[1,1,32]{2,1,0:T(1,128)S(1)}, s32[1,1,32]{2,1,0:T(1,128)}, u32[]{:S(2)}) copy-start(s32[1,1,32]{2,1,0:T(1,128)} %param.11) | copy-start | bytes 388
  0.7 13.5 %copy-start = (bf16[8,4,4,32,256]{4,3,2,1,0:T(8,128)(2,1)S(1)}, bf16[8,4,4,32,256]{4,3,2,1,0:T(8,128)(2,1)}, u32[]{:S(2)}) copy-start(bf16[8,4,4,32,256]{4,3,2,1,0:T(8,128)(2,1)} %refs_7_.1) | copy-start | bytes 6291460
  0.7 13.5 %copy-start.3 = (f32[1,1,4,512]{3,2,1,0:T(4,128)S(1)}, f32[1,1,4,512]{3,2,1,0:T(4,128)}, u32[]{:S(2)}) copy-start(f32[1,1,4,512]{3,2,1,0:T(4,128)} %param.16) | copy-start | bytes 24580
  0.7 13.5 %copy-start.4 = (f32[1,1,4,512]{3,2,1,0:T(4,128)S(1)}, f32[1,1,4,512]{3,2,1,0:T(4,128)}, u32[]{:S(2)}) copy-start(f32[1,1,4,512]{3,2,1,0:T(4,128)} %param.17) | copy-start | bytes 24580
  2.0 5.5 %collective-permute-start = (f32[17,8,128]{2,1,0:T(8,128)S(1)}, f32[17,8,128]{2,1,0:T(8,128)S(1)}, u32[]{:S(2)}, u32[]{:S(2)}) collective-permute-start(f32[17,8,128]{2,1,0:T(8,128)S(1)} %pack.1.refs_1_), channel_id=1, source_target_pairs={{0,1},{1,0},{2,3},{3,2},{4,5},{5,4},{6,7},{7,6},{8,9},{9,8},{10,11... | collective-permute-start | bytes 208904 | tf_op jit(solution)/shard_map/ppermute | solution.py:478
  5.0 4.3 %collective-permute-start.1 = (f32[17,8,128]{2,1,0:T(8,128)S(1)}, f32[17,8,128]{2,1,0:T(8,128)S(1)}, u32[]{:S(2)}, u32[]{:S(2)}) collective-permute-start(f32[17,8,128]{2,1,0:T(8,128)S(1)} %pack.1.refs_1_), channel_id=1, source_target_pairs={{0,4},{1,5},{2,6},{3,7},{4,0},{5,1},{6,2},{7,3},{8,12},{9,13},{10,... | collective-permute-start | bytes 208904 | tf_op jit(solution)/shard_map/ppermute | solution.py:478
  6.5 5.2 %collective-permute-start.2 = (f32[17,8,128]{2,1,0:T(8,128)S(1)}, f32[17,8,128]{2,1,0:T(8,128)S(1)}, u32[]{:S(2)}, u32[]{:S(2)}) collective-permute-start(f32[17,8,128]{2,1,0:T(8,128)S(1)} %pack.1.refs_1_), channel_id=1, source_target_pairs={{0,5},{1,4},{2,7},{3,6},{4,1},{5,0},{6,3},{7,2},{8,13},{9,12},{10,... | collective-permute-start | bytes 208904 | tf_op jit(solution)/shard_map/ppermute | solution.py:478
  6.6 7.5 %collective-permute-start.3 = (f32[17,8,128]{2,1,0:T(8,128)S(1)}, f32[17,8,128]{2,1,0:T(8,128)S(1)}, u32[]{:S(2)}, u32[]{:S(2)}) collective-permute-start(f32[17,8,128]{2,1,0:T(8,128)S(1)} %pack.1.refs_1_), channel_id=1, source_target_pairs={{0,2},{1,3},{2,0},{3,1},{4,6},{5,7},{6,4},{7,5},{8,10},{9,11},{10,... | collective-permute-start | bytes 208904 | tf_op jit(solution)/shard_map/ppermute | solution.py:480
  7.5 6.6 %collective-permute-start.4 = (f32[17,8,128]{2,1,0:T(8,128)S(1)}, f32[17,8,128]{2,1,0:T(8,128)S(1)}, u32[]{:S(2)}, u32[]{:S(2)}) collective-permute-start(f32[17,8,128]{2,1,0:T(8,128)S(1)} %collective-permute-done.refs_2_), channel_id=1, source_target_pairs={{0,2},{1,3},{2,0},{3,1},{4,6},{5,7},{6,4},{7,5},{8,10},{9,11},{10,... | collective-permute-start | bytes 208904 | tf_op jit(solution)/shard_map/ppermute | solution.py:480
  9.3 4.7 %collective-permute-start.5 = (f32[17,8,128]{2,1,0:T(8,128)S(1)}, f32[17,8,128]{2,1,0:T(8,128)S(1)}, u32[]{:S(2)}, u32[]{:S(2)}) collective-permute-start(f32[17,8,128]{2,1,0:T(8,128)S(1)} %collective-permute-done.1.refs_3_), channel_id=1, source_target_pairs={{0,2},{1,3},{2,0},{3,1},{4,6},{5,7},{6,4},{7,5},{8,10},{9,11},{10,... | collective-permute-start | bytes 208904 | tf_op jit(solution)/shard_map/ppermute | solution.py:480
  11.7 2.3 %collective-permute-start.6 = (f32[17,8,128]{2,1,0:T(8,128)S(1)}, f32[17,8,128]{2,1,0:T(8,128)S(1)}, u32[]{:S(2)}, u32[]{:S(2)}) collective-permute-start(f32[17,8,128]{2,1,0:T(8,128)S(1)} %collective-permute-done.2.refs_4_), channel_id=1, source_target_pairs={{0,2},{1,3},{2,0},{3,1},{4,6},{5,7},{6,4},{7,5},{8,10},{9,11},{10,... | collective-permute-start | bytes 208904 | tf_op jit(solution)/shard_map/ppermute | solution.py:480
  19.3 5.9 %collective-permute-start.10 = (f32[16,640]{1,0:T(8,128)S(1)}, f32[16,640]{1,0:T(8,128)S(1)}, u32[]{:S(2)}, u32[]{:S(2)}) collective-permute-start(f32[16,640]{1,0:T(8,128)S(1)} %get-tuple-element.22.refs_2_), channel_id=1, source_target_pairs={{0,8},{8,16},{16,24},{24,0},{1,9},{9,17},{17,25},{25,1},{2,10},{10... | collective-permute-start | bytes 122888 | tf_op jit(solution)/shard_map/ppermute | solution.py:531
  21.0 6.2 %collective-permute-start.11 = (f32[16,640]{1,0:T(8,128)S(1)}, f32[16,640]{1,0:T(8,128)S(1)}, u32[]{:S(2)}, u32[]{:S(2)}) collective-permute-start(f32[16,640]{1,0:T(8,128)S(1)} %get-tuple-element.22.refs_2_), channel_id=1, source_target_pairs={{0,16},{8,24},{16,0},{24,8},{1,17},{9,25},{17,1},{25,9},{2,18},{10... | collective-permute-start | bytes 122888 | tf_op jit(solution)/shard_map/ppermute | solution.py:531
  23.6 4.0 %collective-permute-start.12 = (f32[16,640]{1,0:T(8,128)S(1)}, f32[16,640]{1,0:T(8,128)S(1)}, u32[]{:S(2)}, u32[]{:S(2)}) collective-permute-start(f32[16,640]{1,0:T(8,128)S(1)} %get-tuple-element.22.refs_2_), channel_id=1, source_target_pairs={{0,24},{8,0},{16,8},{24,16},{1,25},{9,1},{17,9},{25,17},{2,26},{10... | collective-permute-start | bytes 122888 | tf_op jit(solution)/shard_map/ppermute | solution.py:531
  27.6 22.2 %copy-start.1 = (f32[8,4,16,32]{3,2,1,0:T(8,128)S(1)}, f32[8,4,16,32]{3,2,1,0:T(8,128)}, u32[]{:S(2)}) copy-start(f32[8,4,16,32]{3,2,1,0:T(8,128)} %param.9) | copy-start | bytes 196612
  33.8 3.7 %collective-permute-start.13 = (f32[4,16,8,128]{3,2,1,0:T(8,128)S(1)}, f32[4,16,8,128]{3,2,1,0:T(8,128)S(1)}, u32[]{:S(2)}, u32[]{:S(2)}) collective-permute-start(f32[4,16,8,128]{3,2,1,0:T(8,128)S(1)} %get-tuple-element.26), channel_id=1, source_target_pairs={{0,2},{1,3},{2,0},{3,1},{4,6},{5,7},{6,4},{7,5},{8,10},{9,11},{10,... | collective-permute-start | bytes 786440 | tf_op jit(solution)/shard_map/ppermute | solution.py:558
  33.8 7.1 %collective-permute-start.9 = (f32[4,32,256]{2,1,0:T(8,128)S(1)}, f32[4,32,256]{2,1,0:T(8,128)S(1)}, u32[]{:S(2)}, u32[]{:S(2)}) collective-permute-start(f32[4,32,256]{2,1,0:T(8,128)S(1)} %get-tuple-element.20), channel_id=1, source_target_pairs={{0,24},{8,0},{16,8},{24,16},{1,25},{9,1},{17,9},{25,17},{2,26},{10... | collective-permute-start | bytes 393224 | tf_op jit(solution)/shard_map/ppermute | solution.py:533
  36.9 12.1 %collective-permute-start.8 = (f32[4,32,256]{2,1,0:T(8,128)S(1)}, f32[4,32,256]{2,1,0:T(8,128)S(1)}, u32[]{:S(2)}, u32[]{:S(2)}) collective-permute-start(f32[4,32,256]{2,1,0:T(8,128)S(1)} %get-tuple-element.19), channel_id=1, source_target_pairs={{0,16},{8,24},{16,0},{24,8},{1,17},{9,25},{17,1},{25,9},{2,18},{10... | collective-permute-start | bytes 393224 | tf_op jit(solution)/shard_map/ppermute | solution.py:533
  37.0 12.1 %collective-permute-start.7 = (f32[4,32,256]{2,1,0:T(8,128)S(1)}, f32[4,32,256]{2,1,0:T(8,128)S(1)}, u32[]{:S(2)}, u32[]{:S(2)}) collective-permute-start(f32[4,32,256]{2,1,0:T(8,128)S(1)} %get-tuple-element.18), channel_id=1, source_target_pairs={{0,8},{8,16},{16,24},{24,0},{1,9},{9,17},{17,25},{25,1},{2,10},{10... | collective-permute-start | bytes 393224 | tf_op jit(solution)/shard_map/ppermute | solution.py:533
  37.6 12.2 %collective-permute-start.14 = (f32[16,8,128]{2,1,0:T(8,128)S(1)}, f32[16,8,128]{2,1,0:T(8,128)S(1)}, u32[]{:S(2)}, u32[]{:S(2)}) collective-permute-start(f32[16,8,128]{2,1,0:T(8,128)S(1)} %get-tuple-element.29), channel_id=1, source_target_pairs={{0,1},{1,0},{2,3},{3,2},{4,5},{5,4},{6,7},{7,6},{8,9},{9,8},{10,11... | collective-permute-start | bytes 196616 | tf_op jit(solution)/shard_map/ppermute | solution.py:560
  38.2 11.6 %collective-permute-start.15 = (f32[16,8,128]{2,1,0:T(8,128)S(1)}, f32[16,8,128]{2,1,0:T(8,128)S(1)}, u32[]{:S(2)}, u32[]{:S(2)}) collective-permute-start(f32[16,8,128]{2,1,0:T(8,128)S(1)} %get-tuple-element.28), channel_id=1, source_target_pairs={{0,4},{1,5},{2,6},{3,7},{4,0},{5,1},{6,2},{7,3},{8,12},{9,13},{10,... | collective-permute-start | bytes 196616 | tf_op jit(solution)/shard_map/ppermute | solution.py:560
  40.9 8.9 %collective-permute-start.16 = (f32[16,8,128]{2,1,0:T(8,128)S(1)}, f32[16,8,128]{2,1,0:T(8,128)S(1)}, u32[]{:S(2)}, u32[]{:S(2)}) collective-permute-start(f32[16,8,128]{2,1,0:T(8,128)S(1)} %get-tuple-element.27), channel_id=1, source_target_pairs={{0,5},{1,4},{2,7},{3,6},{4,1},{5,0},{6,3},{7,2},{8,13},{9,12},{10,... | collective-permute-start | bytes 196616 | tf_op jit(solution)/shard_map/ppermute | solution.py:560

commit v2 on v1

--- a/solution.py
+++ b/solution.py
@@ -14,6 +14,7 @@
 SUB = 8
 PITCH_PAD = 8
 PREP_CHUNKS = 4
+SWAP_UNROLL = 16
 
 
 VM = pl.BlockSpec(memory_space=pltpu.VMEM)
@@ -58,26 +59,25 @@
         self.slab_dev = departures.shape[2]
         self.obs = cells.shape[-1]
         self.nx, self.ny = self.n_tx * self.cx, self.n_ty * self.cy
-        self.groups = LANES // self.ny
-        self.xl = self.nx // self.groups
+        self.halves = LANES // self.ny
+        self.hg = self.rg // self.halves
         self.nq = LANES // self.cy
         self.xq = self.cx // self.nq
         self.t_rows = self.xq * self.rg
         self.ct = self.bcells // LANES
         self.ot = self.obs // LANES
         self.blk_x, self.blk_y = self.cx // CB, self.cy // CB
-        assert self.n_tx % 2 == 0 and self.groups * self.ny == LANES and self.ny == CB * CB
-        assert self.xl % CB == 0 and self.nq * self.cy == LANES and self.xq * self.nq == self.cx
-        assert self.xq <= SUB and self.rows % SUB == 0 and self.groups == 2
+        assert self.n_tx % 2 == 0 and self.halves * self.ny == LANES and self.ny == CB * CB
+        assert self.nq * self.cy == LANES and self.xq * self.nq == self.cx and self.xq <= SUB
+        assert self.halves == 2 and self.hg * 2 * SUB == self.rows
+        assert self.nq == self.halves * self.n_ty
         assert self.slab_dev * self.ot <= self.slabs
 
     def block_place(self, bid):
         tile, kb = split2(bid, self.blk_x * self.blk_y)
         a, b = split2(tile, self.n_ty)
         bx, by = split2(kb, self.blk_y)
-        gx, gy = a * self.blk_x + bx, b * self.blk_y + by
-        g, xg = split2(gx, self.xl // CB)
-        return xg * CB + gy, g
+        return (a * self.blk_x + bx) * CB + b * self.blk_y + by
 
     def tile_at(self, step, back, other_core):
         tx, ty = lax.axis_index("tx"), lax.axis_index("ty")
@@ -106,16 +106,6 @@
     def core_perm(self):
         return [(i, (i // self.n_ty ^ 1) * self.n_ty + i % self.n_ty) for i in range(self.tiles)]
 
-    def pieces(self):
-        table = [[] for _ in range(self.xl)]
-        for a in range(self.n_tx):
-            for x in range(self.cx):
-                g, xl = divmod(a * self.cx + x, self.xl)
-                q, xq = divmod(x, self.xq)
-                for b in range(self.n_ty):
-                    table[xl].append((a * self.n_ty + b, xq, q, g * self.ny // self.cy + b))
-        return table
-
 
 def rolled(v, shift):
     shift %= LANES
@@ -131,13 +121,19 @@
         copy.start()
     for copy in copies:
         copy.wait()
-    out_ref[z.t_rows] = jnp.zeros((SUB, LANES), jnp.float32)
-    for x in range(z.cx):
-        q, xq = divmod(x, z.xq)
-        lanes = slice(q * z.cy, (q + 1) * z.cy)
-        v = alpha_ref[:, x, :]
-        out_ref[xq * z.rg : (xq + 1) * z.rg, :, lanes] = v.reshape(z.rg, SUB, z.cy)
-        out_ref[z.t_rows, xq : xq + 1, lanes] = rate_ref[x : x + 1, :]
+    rate_rows, tiles = [], []
+    for xq in range(z.xq):
+        parts = [alpha_ref[:, q * z.xq + xq, :] for q in range(z.nq)]
+        tiles.append(jnp.concatenate(parts, axis=1).reshape(z.rg, SUB, LANES))
+        parts = [rate_ref[q * z.xq + xq : q * z.xq + xq + 1, :] for q in range(z.nq)]
+        rate_rows.append(jnp.concatenate(parts, axis=1))
+    b = lax.axis_index("ty")
+    for xq in range(z.xq):
+        for g in range(z.rg):
+            turn = (g // z.hg * z.n_ty + b) * z.cy
+            out_ref[xq * z.rg + g] = pltpu.roll(tiles[xq][g], turn, 1)
+    rate_rows += [jnp.zeros((SUB - z.xq, LANES), jnp.float32)]
+    out_ref[z.t_rows] = pltpu.roll(jnp.concatenate(rate_rows, axis=0), b * z.cy, 1)
 
 
 def prep_kernel(z, *refs):
@@ -172,38 +168,51 @@
         lax.fori_loop(i * chunk, (i + 1) * chunk, one, 0, unroll=2)
 
 
-def fill_edges(z, ref):
-    lane = lane_ids((z.rg, SUB, LANES))
-    ref[0] = jnp.where(lane >= z.ny, rolled(ref[z.xl], z.ny), 0.0)
-    ref[z.xl + 1] = jnp.where(lane < LANES - z.ny, rolled(ref[1], -z.ny), 0.0)
-
-
-def beside(z, ref, x, lane_y):
-    c = ref[x + 1]
-    west = jnp.where(lane_y > 0, rolled(c, 1), 0.0)
-    east = jnp.where(lane_y < z.ny - 1, rolled(c, -1), 0.0)
-    return c, (ref[x] + ref[x + 2]) + (west + east)
-
-
-def swap_blocks(z, src, src_off, dst, dst_off):
+def clear_edges(z, ref):
+    for x in (0, z.nx + 1):
+        ref[x] = jnp.zeros((z.hg, SUB, LANES), jnp.float32)
+
+
+def sweeps(z, src, dst, rate_ref):
+    lane_y = lane_ids((z.hg, SUB, LANES)) % z.ny
+    for _ in range(SWEEPS):
+
+        def row(x, carry, src=src, dst=dst):
+            c = src[x + 1]
+            west = jnp.where(lane_y > 0, rolled(c, 1), 0.0)
+            east = jnp.where(lane_y < z.ny - 1, rolled(c, -1), 0.0)
+            near = (src[x] + src[x + 2]) + (west + east)
+            dst[x + 1] = c + rate_ref[x] * (near - 4.0 * c)
+            return carry
+
+        lax.fori_loop(0, z.nx, row, 0, unroll=True)
+        src, dst = dst, src
+    return src, dst
+
+
+def swap_blocks(z, src, dst, rate_ref=None):
     lane = lane_ids((SUB, LANES))
-
-    def one(i, carry):
-        xg, r = split2(i, z.rg)
-        v = [src[xg * CB + j + src_off, r] for j in range(CB)]
-        for bit in (1, 2, 4):
-            shift = bit * CB
-            low = (lane & shift) == 0
+    for bit in (1, 2, 4):
+        shift = bit * CB
+        low = (lane & shift) == 0
+
+        def one(i, carry, src=src, dst=dst):
+            bx, r = split2(i, z.hg)
             for j in range(CB):
                 if j & bit == 0:
-                    a, b = v[j], v[j | bit]
-                    v[j] = jnp.where(low, a, rolled(b, shift))
-                    v[j | bit] = jnp.where(low, rolled(a, -shift), b)
-        for j in range(CB):
-            dst[xg * CB + j + dst_off, r] = v[j]
-        return carry
-
-    lax.fori_loop(0, z.xl // CB * z.rg, one, 0, unroll=8)
+                    at, to = bx * CB + j, bx * CB + (j | bit)
+                    a, b = src[at + 1, r], src[to + 1, r]
+                    first = jnp.where(low, a, rolled(b, shift))
+                    second = jnp.where(low, rolled(a, -shift), b)
+                    if rate_ref is not None and bit == 4:
+                        first, second = first * rate_ref[at], second * rate_ref[to]
+                    dst[at + 1, r] = first
+                    dst[to + 1, r] = second
+            return carry
+
+        lax.fori_loop(0, z.nx // CB * z.hg, one, 0, unroll=SWAP_UNROLL)
+        src, dst = dst, src
+    return src, dst
 
 
 def forward_kernel(z, *refs):
@@ -219,45 +228,49 @@
         every[z.tile_at(s, True, False)] = tile_refs[s][...]
         every[z.tile_at(s, True, True)] = tile_refs[z.chips + s][...]
 
-    group = lane_ids((z.rg, SUB, LANES)) // z.cy
-    group_row = lane_ids((SUB, LANES)) // z.cy
-    for xl, pieces in enumerate(z.pieces()):
-        total, rate = None, None
-        for tile, xq, q, to in pieces:
-            shift = (to - q) * z.cy
-            v = rolled(every[tile, xq * z.rg : (xq + 1) * z.rg], shift)
-            w = rolled(jnp.broadcast_to(every[tile, z.t_rows, xq : xq + 1], (SUB, LANES)), shift)
-            total = v if total is None else jnp.where(group == to, v, total)
-            rate = w if rate is None else jnp.where(group_row == to, w, rate)
-        field[xl + 1] = total
-        rate_ref[xl] = rate
-
-    lane_y = lane_ids((z.rg, SUB, LANES)) % z.ny
-    src, dst = field, other
-    for _ in range(SWEEPS):
-        fill_edges(z, src)
-
-        def row(x, carry, src=src, dst=dst):
-            c, near = beside(z, src, x, lane_y)
-            dst[x + 1] = c + rate_ref[x] * (near - 4.0 * c)
-            return carry
-
-        lax.fori_loop(0, z.xl, row, 0, unroll=True)
-        src, dst = dst, src
-    swap_blocks(z, src, 1, dst, 0)
-
-    lane = lane_ids((z.rows, LANES))
-    half = lane // z.block
+    clear_edges(z, field)
+    clear_edges(z, other)
+    group = lane_ids((SUB, LANES)) // z.cy
+    for a in range(z.n_tx):
+        for q in range(z.nq):
+            picks = [divmod((j - q) % z.nq, z.n_ty) for j in range(z.nq)]
+            for xq in range(z.xq):
+                for r in range(z.hg):
+                    total = None
+                    for j, (h, b) in enumerate(picks):
+                        v = every[a * z.n_ty + b, xq * z.rg + h * z.hg + r]
+                        total = v if total is None else jnp.where(group == j, v, total)
+                    field[a * z.cx + q * z.xq + xq + 1, r] = rolled(total, -q * z.cy)
+            total = None
+            for j, (h, b) in enumerate(picks):
+                v = rolled(every[a * z.n_ty + b, z.t_rows], h * z.n_ty * z.cy)
+                total = v if total is None else jnp.where(group == j, v, total)
+            total = rolled(total, -q * z.cy)
+            for xq in range(z.xq):
+                rate_ref[a * z.cx + q * z.xq + xq] = jnp.broadcast_to(
+                    total[xq : xq + 1], (SUB, LANES)
+                )
+
+    src, dst = sweeps(z, field, other, rate_ref)
+    blocks, _ = swap_blocks(z, src, dst)
+
+    first_half = lane_ids((z.rows // 2, LANES)) < z.block
     pitch = z.rows + PITCH_PAD
 
     def fine_block(f, carry):
-        at, g = z.block_place(blocks_ref[f])
-        v = dst[at].reshape(z.rows, LANES)
-        v = jnp.where(half == g, v, rolled(v, z.block))
-        hi = v.astype(jnp.bfloat16)
-        hi32 = hi.astype(jnp.float32)
-        first = jnp.where(half == 0, hi32, v - hi32).astype(jnp.bfloat16)
-        lhs = jnp.concatenate([first, hi[:, : z.block]], axis=1)
+        v = blocks[z.block_place(blocks_ref[f]) + 1].reshape(z.rows // 2, LANES)
+        turned = rolled(v, z.block)
+        hi, turned_hi = v.astype(jnp.bfloat16), turned.astype(jnp.bfloat16)
+        hi32, turned32 = hi.astype(jnp.float32), turned_hi.astype(jnp.float32)
+        upper = jnp.where(first_half, hi32, turned - turned32).astype(jnp.bfloat16)
+        lower = jnp.where(first_half, turned32, v - hi32).astype(jnp.bfloat16)
+        lhs = jnp.concatenate(
+            [
+                jnp.concatenate([upper, lower], axis=0),
+                jnp.concatenate([hi[:, : z.block], turned_hi[:, : z.block]], axis=0),
+            ],
+            axis=1,
+        )
         out = jnp.dot(lhs, w_ref[f], preferred_element_type=jnp.float32)
         start = pl.multiple_of(f * pitch, SUB)
         for t in range(z.ct):
@@ -368,10 +381,10 @@
 
     lax.fori_loop(0, z.levels, level, 0)
     other[...] = jnp.zeros(other.shape, jnp.float32)
-    half = lane_ids((z.rows, LANES)) // z.block
+    first_half = lane_ids((z.rows // 2, LANES)) < z.block
 
     def fine_block(f, carry):
-        at, g = z.block_place(blocks_ref[f])
+        at = z.block_place(blocks_ref[f]) + 1
         grad = jnp.concatenate(
             [fine_ref[t, pl.ds(f, z.rows, stride=pitch), :] for t in range(z.ct)], axis=1
         )
@@ -383,42 +396,34 @@
             preferred_element_type=jnp.float32,
         )
         out = out[: z.rows] + out[z.rows :]
-        out = out + rolled(out, z.block)
-        out = jnp.where(half == g, out, 0.0)
-        other[at] += out.reshape(z.rg, SUB, LANES)
+        upper, lower = out[: z.rows // 2], out[z.rows // 2 :]
+        out = jnp.where(first_half, upper, lower)
+        out = out + rolled(jnp.where(first_half, lower, upper), z.block)
+        other[at] += out.reshape(z.hg, SUB, LANES)
         return carry
 
     lax.fori_loop(0, z.fine, fine_block, 0, unroll=16)
-    swap_blocks(z, other, 0, field, 1)
-
-    lane_y = lane_ids((z.rg, SUB, LANES)) % z.ny
-    for _ in range(SWEEPS):
-
-        def scale(x, carry):
-            other[x + 1] = rate_ref[x] * field[x + 1]
-            return carry
-
-        lax.fori_loop(0, z.xl, scale, 0, unroll=4)
-        fill_edges(z, other)
-
-        def row(x, carry):
-            c, near = beside(z, other, x, lane_y)
-            field[x + 1] = field[x + 1] + near - 4.0 * c
-            return carry
-
-        lax.fori_loop(0, z.xl, row, 0, unroll=True)
-
-    group = lane_ids((z.rg, SUB, LANES)) // z.cy
-    packed = {}
-    for xl, pieces in enumerate(z.pieces()):
-        for tile, xq, q, to in pieces:
-            packed.setdefault((tile, xq), []).append((xl, q, to))
-    for (tile, xq), parts in packed.items():
-        total = None
-        for xl, q, to in parts:
-            v = rolled(field[xl + 1], (q - to) * z.cy)
-            total = v if total is None else jnp.where(group == q, v, total)
-        every[tile, xq * z.rg : (xq + 1) * z.rg] = total
+    swap_blocks(z, other, field, rate_ref)
+    clear_edges(z, field)
+    clear_edges(z, other)
+    grid, _ = sweeps(z, field, other, rate_ref)
+
+    group = lane_ids((SUB, LANES)) // z.cy
+    for a in range(z.n_tx):
+        for xq in range(z.xq):
+            turned = []
+            for q in range(z.nq):
+                x = a * z.cx + q * z.xq + xq
+                inverse = 1.0 / rate_ref[x]
+                turned.append([rolled(grid[x + 1, r] * inverse, q * z.cy) for r in range(z.hg)])
+            for b in range(z.n_ty):
+                for h in range(z.halves):
+                    for r in range(z.hg):
+                        total = turned[-(h * z.n_ty + b) % z.nq][r]
+                        for j in range(1, z.nq):
+                            v = turned[(j - h * z.n_ty - b) % z.nq][r]
+                            total = jnp.where(group == j, v, total)
+                        every[a * z.n_ty + b, xq * z.rg + h * z.hg + r] = total
     for s in range(z.chips):
         keep_ref[s] = every[z.tile_at(s, False, False)]
         send_ref[s] = every[z.tile_at(s, False, True)]
@@ -429,10 +434,16 @@
     total = refs[0][...]
     for ref in refs[1:-1]:
         total = total + ref[...]
-    for x in range(z.cx):
-        q, xq = divmod(x, z.xq)
-        part = total[xq * z.rg : (xq + 1) * z.rg, :, q * z.cy : (q + 1) * z.cy]
-        out_ref[:, x, :] = alpha_ref[:, x, :] + part.reshape(z.rows, z.cy)
+    b = lax.axis_index("ty")
+    for xq in range(z.xq):
+        rows = []
+        for g in range(z.rg):
+            turn = lax.rem(LANES - (g // z.hg * z.n_ty + b) * z.cy, LANES)
+            rows.append(pltpu.roll(total[xq * z.rg + g], turn, 1))
+        part = jnp.concatenate(rows, axis=0)
+        for q in range(z.nq):
+            x = q * z.xq + xq
+            out_ref[:, x, :] = alpha_ref[:, x, :] + part[:, q * z.cy : (q + 1) * z.cy]
 
 
 def on_device(
@@ -458,7 +469,7 @@
     axes = ("tx", "ty")
     tile_shape = (z.t_rows, SUB, LANES)
     full_shape = (z.t_rows + 1, SUB, LANES)
-    grid_shape = (z.xl + 2, z.rg, SUB, LANES)
+    grid_shape = (z.nx + 2, z.hg, SUB, LANES)
 
     own = pl.pallas_call(
         functools.partial(pack_kernel, z),
@@ -504,7 +515,7 @@
         functools.partial(forward_kernel, z),
         out_shape=(
             shape((z.slabs, z.obs + LANES), f32),
-            shape((z.xl, SUB, LANES), f32),
+            shape((z.nx, SUB, LANES), f32),
             *[shape(slab_shape, f32)] * z.n_mem,
         ),
         in_specs=[SM] + [VM] * (z.tiles + 6),

time: 51.8 us -> 49.9 us (0.963)
  Pallas kernels: 16.2 us -> 14.2 us
    pallas_call x1, Pallas kernels: 6.25 us -> 4.68 us  [on_device(): pl.pallas_call(functools.partial(adjoint_kernel, z), out_shape=(shape((z....]
    pallas_call x1, Pallas kernels: 5.18 us -> 4.62 us  [on_device(): pl.pallas_call(functools.partial(forward_kernel, z), out_shape=(shape((z....]
where the time goes in v2:
time: 49.9 us; the launch traced here: 49.7 us
  waiting for transfers between devices  17.7 us (35%)
  starting transfers between devices  15.6 us (31%)
  Pallas kernels  14.2 us (28%)
  between operations  1.46 us (3%)
  other arithmetic  0.72 us (1%)
    ppermute x3, waiting for transfers between devices, on_device(): parts.append(lax.ppermute(incs[s], 'mem', ring(s)))  9.83 us
    ppermute x3, starting transfers between devices, on_device(): seens.append(lax.ppermute(seen, 'mem', ring(s)))  5.57 us
    ppermute x3, waiting for transfers between devices, on_device(): tiles.append(lax.ppermute(own, axes, z.chip_perm(s)))  5.18 us
    pallas_call x1, Pallas kernels, on_device(): pl.pallas_call(functools.partial(adjoint_kernel, z), out_shape=(shape((z....  4.68 us
    pallas_call x1, Pallas kernels, on_device(): pl.pallas_call(functools.partial(forward_kernel, z), out_shape=(shape((z....  4.62 us
    ppermute x3, starting transfers between devices, on_device(): tiles.append(lax.ppermute(own, axes, z.chip_perm(s)))  4.57 us
    ppermute x3, starting transfers between devices, on_device(): parts.append(lax.ppermute(incs[s], 'mem', ring(s)))  3.81 us
    ppermute x3, waiting for transfers between devices, on_device(): seens.append(lax.ppermute(seen, 'mem', ring(s)))  2.68 us
  transfers between devices with their start and end apart: 17, of which 8 were waited for; matrix products, arithmetic and copies ran while one was open for 1% of the time, Pallas kernels for 3%

profile of v2, /device:TPU:0, one launch (start us, length us, event | category | flops | bytes accessed | tf_op | source)
XLA Modules:
  0.0 49.7 jit_solution(12051695006298044172)
XLA Ops:
  0.7 1.4 %pack.1.refs_1_ = f32[17,8,128]{2,1,0:T(8,128)S(1)} custom-call(f32[32,16,32]{2,1,0:T(8,128)} %bitcast.16, f32[16,32]{1,0:T(8,128)} %rate_hbm.1), custom_call_target="tpu_custom_call" | custom-call | tf_op jit(solution)/shard_map/pack/pallas_call | solution.py:474
  2.1 3.0 %collective-permute-start = (f32[17,8,128]{2,1,0:T(8,128)S(1)}, f32[17,8,128]{2,1,0:T(8,128)S(1)}, u32[]{:S(2)}, u32[]{:S(2)}) collective-permute-start(f32[17,8,128]{2,1,0:T(8,128)S(1)} %pack.1.refs_1_), channel_id=1, source_target_pairs={{0,1},{1,0},{2,3},{3,2},{4,5},{5,4},{6,7},{7,6},{8,9},{9,8},{10,11... | collective-permute-start | bytes 208904 | tf_op jit(solution)/shard_map/ppermute | solution.py:489
  5.1 1.5 %collective-permute-start.1 = (f32[17,8,128]{2,1,0:T(8,128)S(1)}, f32[17,8,128]{2,1,0:T(8,128)S(1)}, u32[]{:S(2)}, u32[]{:S(2)}) collective-permute-start(f32[17,8,128]{2,1,0:T(8,128)S(1)} %pack.1.refs_1_), channel_id=1, source_target_pairs={{0,4},{1,5},{2,6},{3,7},{4,0},{5,1},{6,2},{7,3},{8,12},{9,13},{10,... | collective-permute-start | bytes 208904 | tf_op jit(solution)/shard_map/ppermute | solution.py:489
  6.6 0.9 %collective-permute-done.refs_2_ = f32[17,8,128]{2,1,0:T(8,128)S(1)} collective-permute-done((f32[17,8,128]{2,1,0:T(8,128)S(1)}, f32[17,8,128]{2,1,0:T(8,128)S(1)}, u32[]{:S(2)}, u32[]{:S(2)}) %collective-permute-start) | collective-permute-done | bytes 69664 | tf_op jit(solution)/shard_map/ppermute | solution.py:489
  7.5 1.9 %collective-permute-done.1.refs_3_ = f32[17,8,128]{2,1,0:T(8,128)S(1)} collective-permute-done((f32[17,8,128]{2,1,0:T(8,128)S(1)}, f32[17,8,128]{2,1,0:T(8,128)S(1)}, u32[]{:S(2)}, u32[]{:S(2)}) %collective-permute-start.1) | collective-permute-done | bytes 69664 | tf_op jit(solution)/shard_map/ppermute | solution.py:489
  9.4 2.4 %collective-permute-done.2.refs_4_ = f32[17,8,128]{2,1,0:T(8,128)S(1)} collective-permute-done((f32[17,8,128]{2,1,0:T(8,128)S(1)}, f32[17,8,128]{2,1,0:T(8,128)S(1)}, u32[]{:S(2)}, u32[]{:S(2)}) %collective-permute-start.2) | collective-permute-done | bytes 69664 | tf_op jit(solution)/shard_map/ppermute | solution.py:489
  12.5 1.6 %prep.1 = (bf16[32,192,256]{2,1,0:T(8,128)(2,1)S(1)}, bf16[256,512]{1,0:T(8,128)(2,1)S(1)}, f32[1,512]{1,0:T(1,128)S(1)}) custom-call(f32[32,64,256]{2,1,0:T(8,128)} %bitcast.25, s32[1,512]{1,0:T(1,128)} %bitcast.18, s32[1,1]{1,0:T(1,128)S(6)} %copy.12.refs_2_), custom_call_target="tpu_custom_call" | custom-call | flops 4000000 | bytes 5000000 | tf_op jit(solution)/shard_map/prep/pallas_call | solution.py:493
  14.2 4.6 %forward.1 = (f32[16,640]{1,0:T(8,128)S(1)}, f32[64,8,128]{2,1,0:T(8,128)S(1)}, f32[4,32,256]{2,1,0:T(8,128)S(1)}, f32[4,32,256]{2,1,0:T(8,128)S(1)}, f32[4,32,2...) custom-call(s32[32]{0:T(128)S(1)} %bitcast.23, f32[17,8,128]{2,1,0:T(8,128)S(1)} %pack.1.refs_1_, ...), custom_call_target="tpu_custom_call" | custom-call | flops 20000000 | bytes 8000000 | tf_op jit(solution)/shard_map/forward/pallas_call | solution.py:514
  18.8 1.6 %collective-permute-start.10 = (f32[16,640]{1,0:T(8,128)S(1)}, f32[16,640]{1,0:T(8,128)S(1)}, u32[]{:S(2)}, u32[]{:S(2)}) collective-permute-start(f32[16,640]{1,0:T(8,128)S(1)} %get-tuple-element.22.refs_2_), channel_id=1, source_target_pairs={{0,8},{8,16},{16,24},{24,0},{1,9},{9,17},{17,25},{25,1},{2,10},{10... | collective-permute-start | bytes 122888 | tf_op jit(solution)/shard_map/ppermute | solution.py:542
  20.5 2.6 %collective-permute-start.11 = (f32[16,640]{1,0:T(8,128)S(1)}, f32[16,640]{1,0:T(8,128)S(1)}, u32[]{:S(2)}, u32[]{:S(2)}) collective-permute-start(f32[16,640]{1,0:T(8,128)S(1)} %get-tuple-element.22.refs_2_), channel_id=1, source_target_pairs={{0,16},{8,24},{16,0},{24,8},{1,17},{9,25},{17,1},{25,9},{2,18},{10... | collective-permute-start | bytes 122888 | tf_op jit(solution)/shard_map/ppermute | solution.py:542
  23.1 1.4 %collective-permute-start.12 = (f32[16,640]{1,0:T(8,128)S(1)}, f32[16,640]{1,0:T(8,128)S(1)}, u32[]{:S(2)}, u32[]{:S(2)}) collective-permute-start(f32[16,640]{1,0:T(8,128)S(1)} %get-tuple-element.22.refs_2_), channel_id=1, source_target_pairs={{0,24},{8,0},{16,8},{24,16},{1,25},{9,1},{17,9},{25,17},{2,26},{10... | collective-permute-start | bytes 122888 | tf_op jit(solution)/shard_map/ppermute | solution.py:542
  24.4 0.4 collective-permute-done.10.refs_3_
  24.8 1.9 %collective-permute-done.11.refs_4_ = f32[16,640]{1,0:T(8,128)S(1)} collective-permute-done((f32[16,640]{1,0:T(8,128)S(1)}, f32[16,640]{1,0:T(8,128)S(1)}, u32[]{:S(2)}, u32[]{:S(2)}) %collective-permute-start.11) | collective-permute-done | bytes 40992 | tf_op jit(solution)/shard_map/ppermute | solution.py:542
  26.7 0.4 collective-permute-done.12.refs_5_
  27.1 4.7 %adjoint.1 = (f32[4,512]{1,0:T(4,128)}, f32[4,16,8,128]{3,2,1,0:T(8,128)S(1)}, f32[4,16,8,128]{3,2,1,0:T(8,128)S(1)}) custom-call(s32[32]{0:T(128)S(1)} %bitcast.24, f32[1,512]{1,0:T(1,128)S(1)} %get-tuple-element.21.refs_1_, f32[16,640]{1,0:T(8,128)S(1)} %get-tuple-element.22.refs_2_, f32[16,640]{1,0:T(8,128)S(1)} %collective-permute-done.10.refs_3_, ...), custom_call_target="tpu_custom_call" | custom-call | flops 20000000 | bytes 8000000 | tf_op jit(solution)/shard_map/adjoint/pallas_call | solution.py:547
  31.9 3.2 %collective-permute-start.9 = (f32[4,32,256]{2,1,0:T(8,128)S(1)}, f32[4,32,256]{2,1,0:T(8,128)S(1)}, u32[]{:S(2)}, u32[]{:S(2)}) collective-permute-start(f32[4,32,256]{2,1,0:T(8,128)S(1)} %get-tuple-element.20), channel_id=1, source_target_pairs={{0,24},{8,0},{16,8},{24,16},{1,25},{9,1},{17,9},{25,17},{2,26},{10... | collective-permute-start | bytes 393224 | tf_op jit(solution)/shard_map/ppermute | solution.py:544
  35.0 0.6 %collective-permute-start.7 = (f32[4,32,256]{2,1,0:T(8,128)S(1)}, f32[4,32,256]{2,1,0:T(8,128)S(1)}, u32[]{:S(2)}, u32[]{:S(2)}) collective-permute-start(f32[4,32,256]{2,1,0:T(8,128)S(1)} %get-tuple-element.18), channel_id=1, source_target_pairs={{0,8},{8,16},{16,24},{24,0},{1,9},{9,17},{17,25},{25,1},{2,10},{10... | collective-permute-start | bytes 393224 | tf_op jit(solution)/shard_map/ppermute | solution.py:544
  35.7 0.6 %collective-permute-start.14 = (f32[16,8,128]{2,1,0:T(8,128)S(1)}, f32[16,8,128]{2,1,0:T(8,128)S(1)}, u32[]{:S(2)}, u32[]{:S(2)}) collective-permute-start(f32[16,8,128]{2,1,0:T(8,128)S(1)} %get-tuple-element.29), channel_id=1, source_target_pairs={{0,1},{1,0},{2,3},{3,2},{4,5},{5,4},{6,7},{7,6},{8,9},{9,8},{10,11... | collective-permute-start | bytes 196616 | tf_op jit(solution)/shard_map/ppermute | solution.py:571
  36.3 0.5 %collective-permute-start.15 = (f32[16,8,128]{2,1,0:T(8,128)S(1)}, f32[16,8,128]{2,1,0:T(8,128)S(1)}, u32[]{:S(2)}, u32[]{:S(2)}) collective-permute-start(f32[16,8,128]{2,1,0:T(8,128)S(1)} %get-tuple-element.28), channel_id=1, source_target_pairs={{0,4},{1,5},{2,6},{3,7},{4,0},{5,1},{6,2},{7,3},{8,12},{9,13},{10,... | collective-permute-start | bytes 196616 | tf_op jit(solution)/shard_map/ppermute | solution.py:571
  36.8 2.2 %collective-permute-done.9 = f32[4,32,256]{2,1,0:T(8,128)S(1)} collective-permute-done((f32[4,32,256]{2,1,0:T(8,128)S(1)}, f32[4,32,256]{2,1,0:T(8,128)S(1)}, u32[]{:S(2)}, u32[]{:S(2)}) %collective-permute-start.9) | collective-permute-done | bytes 131104 | tf_op jit(solution)/shard_map/ppermute | solution.py:544
  39.0 0.5 collective-permute-start.16
  39.5 7.6 %collective-permute-done.8 = f32[4,32,256]{2,1,0:T(8,128)S(1)} collective-permute-done((f32[4,32,256]{2,1,0:T(8,128)S(1)}, f32[4,32,256]{2,1,0:T(8,128)S(1)}, u32[]{:S(2)}, u32[]{:S(2)}) %collective-permute-start.8) | collective-permute-done | bytes 131104 | tf_op jit(solution)/shard_map/ppermute | solution.py:544
  47.1 0.7 %add_add_fusion = f32[4,32,256]{2,1,0:T(8,128)} fusion(f32[4,32,256]{2,1,0:T(8,128)S(1)} %collective-permute-done.9, f32[4,32,256]{2,1,0:T(8,128)S(1)} %collective-permute-done.8, f32[4,32,256]{2,1,0:T(8,128)S(1)} %get-tuple-element.17, f32[4,32,256]{2,1,0:T(8,128)S(1)} %collective-permute-done.7), kind=kLoop, calls=%fused_computation | loop fusion | flops 98304 | bytes 655360 | tf_op jit(solution)/shard_map/add | solution.py:582
  47.8 1.9 %finish.1 = f32[32,16,32]{2,1,0:T(8,128)} custom-call(f32[32,16,32]{2,1,0:T(8,128)S(1)} %bitcast.17, f32[16,8,128]{2,1,0:T(8,128)S(1)} %get-tuple-element.30.refs_0_, f32[16,8,128]{2,1,0:T(8,128)S(1)} %collective-permute-done.14.refs_1_, f32[16,8,128]{2,1,0:T(8,128)S(1)} %collective-permute-done.15.refs_2_, f32[16,8,128]{2,1,0:T(8,128)S(1)} %collective-permute-done.16.refs_3_), custom_call_target="tpu_custom_call" | custom-call | tf_op jit(solution)/shard_map/finish/pallas_call | solution.py:572
  (29 shorter events, 0.2 us)
Async XLA Ops:
  0.6 13.5 %copy-start.2 = (s32[1,1,512]{2,1,0:T(1,128)S(1)}, s32[1,1,512]{2,1,0:T(1,128)}, u32[]{:S(2)}) copy-start(s32[1,1,512]{2,1,0:T(1,128)} %param.14) | copy-start | bytes 6148
  0.6 13.5 %copy-start.5 = (s32[1,1,32]{2,1,0:T(1,128)S(1)}, s32[1,1,32]{2,1,0:T(1,128)}, u32[]{:S(2)}) copy-start(s32[1,1,32]{2,1,0:T(1,128)} %param.11) | copy-start | bytes 388
  0.7 13.5 %copy-start = (bf16[8,4,4,32,256]{4,3,2,1,0:T(8,128)(2,1)S(1)}, bf16[8,4,4,32,256]{4,3,2,1,0:T(8,128)(2,1)}, u32[]{:S(2)}) copy-start(bf16[8,4,4,32,256]{4,3,2,1,0:T(8,128)(2,1)} %refs_7_.1) | copy-start | bytes 6291460
  0.7 13.5 %copy-start.3 = (f32[1,1,4,512]{3,2,1,0:T(4,128)S(1)}, f32[1,1,4,512]{3,2,1,0:T(4,128)}, u32[]{:S(2)}) copy-start(f32[1,1,4,512]{3,2,1,0:T(4,128)} %param.16) | copy-start | bytes 24580
  0.7 13.5 %copy-start.4 = (f32[1,1,4,512]{3,2,1,0:T(4,128)S(1)}, f32[1,1,4,512]{3,2,1,0:T(4,128)}, u32[]{:S(2)}) copy-start(f32[1,1,4,512]{3,2,1,0:T(4,128)} %param.17) | copy-start | bytes 24580
  2.1 5.5 %collective-permute-start = (f32[17,8,128]{2,1,0:T(8,128)S(1)}, f32[17,8,128]{2,1,0:T(8,128)S(1)}, u32[]{:S(2)}, u32[]{:S(2)}) collective-permute-start(f32[17,8,128]{2,1,0:T(8,128)S(1)} %pack.1.refs_1_), channel_id=1, source_target_pairs={{0,1},{1,0},{2,3},{3,2},{4,5},{5,4},{6,7},{7,6},{8,9},{9,8},{10,11... | collective-permute-start | bytes 208904 | tf_op jit(solution)/shard_map/ppermute | solution.py:489
  5.1 4.3 %collective-permute-start.1 = (f32[17,8,128]{2,1,0:T(8,128)S(1)}, f32[17,8,128]{2,1,0:T(8,128)S(1)}, u32[]{:S(2)}, u32[]{:S(2)}) collective-permute-start(f32[17,8,128]{2,1,0:T(8,128)S(1)} %pack.1.refs_1_), channel_id=1, source_target_pairs={{0,4},{1,5},{2,6},{3,7},{4,0},{5,1},{6,2},{7,3},{8,12},{9,13},{10,... | collective-permute-start | bytes 208904 | tf_op jit(solution)/shard_map/ppermute | solution.py:489
  6.6 5.2 %collective-permute-start.2 = (f32[17,8,128]{2,1,0:T(8,128)S(1)}, f32[17,8,128]{2,1,0:T(8,128)S(1)}, u32[]{:S(2)}, u32[]{:S(2)}) collective-permute-start(f32[17,8,128]{2,1,0:T(8,128)S(1)} %pack.1.refs_1_), channel_id=1, source_target_pairs={{0,5},{1,4},{2,7},{3,6},{4,1},{5,0},{6,3},{7,2},{8,13},{9,12},{10,... | collective-permute-start | bytes 208904 | tf_op jit(solution)/shard_map/ppermute | solution.py:489
  6.6 7.5 %collective-permute-start.3 = (f32[17,8,128]{2,1,0:T(8,128)S(1)}, f32[17,8,128]{2,1,0:T(8,128)S(1)}, u32[]{:S(2)}, u32[]{:S(2)}) collective-permute-start(f32[17,8,128]{2,1,0:T(8,128)S(1)} %pack.1.refs_1_), channel_id=1, source_target_pairs={{0,2},{1,3},{2,0},{3,1},{4,6},{5,7},{6,4},{7,5},{8,10},{9,11},{10,... | collective-permute-start | bytes 208904 | tf_op jit(solution)/shard_map/ppermute | solution.py:491
  7.5 6.6 %collective-permute-start.4 = (f32[17,8,128]{2,1,0:T(8,128)S(1)}, f32[17,8,128]{2,1,0:T(8,128)S(1)}, u32[]{:S(2)}, u32[]{:S(2)}) collective-permute-start(f32[17,8,128]{2,1,0:T(8,128)S(1)} %collective-permute-done.refs_2_), channel_id=1, source_target_pairs={{0,2},{1,3},{2,0},{3,1},{4,6},{5,7},{6,4},{7,5},{8,10},{9,11},{10,... | collective-permute-start | bytes 208904 | tf_op jit(solution)/shard_map/ppermute | solution.py:491
  9.4 4.7 %collective-permute-start.5 = (f32[17,8,128]{2,1,0:T(8,128)S(1)}, f32[17,8,128]{2,1,0:T(8,128)S(1)}, u32[]{:S(2)}, u32[]{:S(2)}) collective-permute-start(f32[17,8,128]{2,1,0:T(8,128)S(1)} %collective-permute-done.1.refs_3_), channel_id=1, source_target_pairs={{0,2},{1,3},{2,0},{3,1},{4,6},{5,7},{6,4},{7,5},{8,10},{9,11},{10,... | collective-permute-start | bytes 208904 | tf_op jit(solution)/shard_map/ppermute | solution.py:491
  11.8 2.3 %collective-permute-start.6 = (f32[17,8,128]{2,1,0:T(8,128)S(1)}, f32[17,8,128]{2,1,0:T(8,128)S(1)}, u32[]{:S(2)}, u32[]{:S(2)}) collective-permute-start(f32[17,8,128]{2,1,0:T(8,128)S(1)} %collective-permute-done.2.refs_4_), channel_id=1, source_target_pairs={{0,2},{1,3},{2,0},{3,1},{4,6},{5,7},{6,4},{7,5},{8,10},{9,11},{10,... | collective-permute-start | bytes 208904 | tf_op jit(solution)/shard_map/ppermute | solution.py:491
  18.8 6.0 %collective-permute-start.10 = (f32[16,640]{1,0:T(8,128)S(1)}, f32[16,640]{1,0:T(8,128)S(1)}, u32[]{:S(2)}, u32[]{:S(2)}) collective-permute-start(f32[16,640]{1,0:T(8,128)S(1)} %get-tuple-element.22.refs_2_), channel_id=1, source_target_pairs={{0,8},{8,16},{16,24},{24,0},{1,9},{9,17},{17,25},{25,1},{2,10},{10... | collective-permute-start | bytes 122888 | tf_op jit(solution)/shard_map/ppermute | solution.py:542
  20.5 6.2 %collective-permute-start.11 = (f32[16,640]{1,0:T(8,128)S(1)}, f32[16,640]{1,0:T(8,128)S(1)}, u32[]{:S(2)}, u32[]{:S(2)}) collective-permute-start(f32[16,640]{1,0:T(8,128)S(1)} %get-tuple-element.22.refs_2_), channel_id=1, source_target_pairs={{0,16},{8,24},{16,0},{24,8},{1,17},{9,25},{17,1},{25,9},{2,18},{10... | collective-permute-start | bytes 122888 | tf_op jit(solution)/shard_map/ppermute | solution.py:542
  23.1 4.0 %collective-permute-start.12 = (f32[16,640]{1,0:T(8,128)S(1)}, f32[16,640]{1,0:T(8,128)S(1)}, u32[]{:S(2)}, u32[]{:S(2)}) collective-permute-start(f32[16,640]{1,0:T(8,128)S(1)} %get-tuple-element.22.refs_2_), channel_id=1, source_target_pairs={{0,24},{8,0},{16,8},{24,16},{1,25},{9,1},{17,9},{25,17},{2,26},{10... | collective-permute-start | bytes 122888 | tf_op jit(solution)/shard_map/ppermute | solution.py:542
  27.1 20.7 %copy-start.1 = (f32[8,4,16,32]{3,2,1,0:T(8,128)S(1)}, f32[8,4,16,32]{3,2,1,0:T(8,128)}, u32[]{:S(2)}) copy-start(f32[8,4,16,32]{3,2,1,0:T(8,128)} %param.9) | copy-start | bytes 196612
  31.8 3.9 %collective-permute-start.13 = (f32[4,16,8,128]{3,2,1,0:T(8,128)S(1)}, f32[4,16,8,128]{3,2,1,0:T(8,128)S(1)}, u32[]{:S(2)}, u32[]{:S(2)}) collective-permute-start(f32[4,16,8,128]{3,2,1,0:T(8,128)S(1)} %get-tuple-element.26), channel_id=1, source_target_pairs={{0,2},{1,3},{2,0},{3,1},{4,6},{5,7},{6,4},{7,5},{8,10},{9,11},{10,... | collective-permute-start | bytes 786440 | tf_op jit(solution)/shard_map/ppermute | solution.py:569
  31.9 7.1 %collective-permute-start.9 = (f32[4,32,256]{2,1,0:T(8,128)S(1)}, f32[4,32,256]{2,1,0:T(8,128)S(1)}, u32[]{:S(2)}, u32[]{:S(2)}) collective-permute-start(f32[4,32,256]{2,1,0:T(8,128)S(1)} %get-tuple-element.20), channel_id=1, source_target_pairs={{0,24},{8,0},{16,8},{24,16},{1,25},{9,1},{17,9},{25,17},{2,26},{10... | collective-permute-start | bytes 393224 | tf_op jit(solution)/shard_map/ppermute | solution.py:544
  35.0 12.1 %collective-permute-start.8 = (f32[4,32,256]{2,1,0:T(8,128)S(1)}, f32[4,32,256]{2,1,0:T(8,128)S(1)}, u32[]{:S(2)}, u32[]{:S(2)}) collective-permute-start(f32[4,32,256]{2,1,0:T(8,128)S(1)} %get-tuple-element.19), channel_id=1, source_target_pairs={{0,16},{8,24},{16,0},{24,8},{1,17},{9,25},{17,1},{25,9},{2,18},{10... | collective-permute-start | bytes 393224 | tf_op jit(solution)/shard_map/ppermute | solution.py:544
  35.0 12.1 %collective-permute-start.7 = (f32[4,32,256]{2,1,0:T(8,128)S(1)}, f32[4,32,256]{2,1,0:T(8,128)S(1)}, u32[]{:S(2)}, u32[]{:S(2)}) collective-permute-start(f32[4,32,256]{2,1,0:T(8,128)S(1)} %get-tuple-element.18), channel_id=1, source_target_pairs={{0,8},{8,16},{16,24},{24,0},{1,9},{9,17},{17,25},{25,1},{2,10},{10... | collective-permute-start | bytes 393224 | tf_op jit(solution)/shard_map/ppermute | solution.py:544
  35.7 12.1 %collective-permute-start.14 = (f32[16,8,128]{2,1,0:T(8,128)S(1)}, f32[16,8,128]{2,1,0:T(8,128)S(1)}, u32[]{:S(2)}, u32[]{:S(2)}) collective-permute-start(f32[16,8,128]{2,1,0:T(8,128)S(1)} %get-tuple-element.29), channel_id=1, source_target_pairs={{0,1},{1,0},{2,3},{3,2},{4,5},{5,4},{6,7},{7,6},{8,9},{9,8},{10,11... | collective-permute-start | bytes 196616 | tf_op jit(solution)/shard_map/ppermute | solution.py:571
  36.3 11.5 %collective-permute-start.15 = (f32[16,8,128]{2,1,0:T(8,128)S(1)}, f32[16,8,128]{2,1,0:T(8,128)S(1)}, u32[]{:S(2)}, u32[]{:S(2)}) collective-permute-start(f32[16,8,128]{2,1,0:T(8,128)S(1)} %get-tuple-element.28), channel_id=1, source_target_pairs={{0,4},{1,5},{2,6},{3,7},{4,0},{5,1},{6,2},{7,3},{8,12},{9,13},{10,... | collective-permute-start | bytes 196616 | tf_op jit(solution)/shard_map/ppermute | solution.py:571
  39.0 8.8 %collective-permute-start.16 = (f32[16,8,128]{2,1,0:T(8,128)S(1)}, f32[16,8,128]{2,1,0:T(8,128)S(1)}, u32[]{:S(2)}, u32[]{:S(2)}) collective-permute-start(f32[16,8,128]{2,1,0:T(8,128)S(1)} %get-tuple-element.27), channel_id=1, source_target_pairs={{0,5},{1,4},{2,7},{3,6},{4,1},{5,0},{6,3},{7,2},{8,13},{9,12},{10,... | collective-permute-start | bytes 196616 | tf_op jit(solution)/shard_map/ppermute | solution.py:571

commit v3 on v2

--- a/solution.py
+++ b/solution.py
@@ -159,8 +159,7 @@
     def one(f, carry):
         hi, lo = hi_lo(weights_ref[f])
         stacked_ref[f, 0:k, :] = hi
-        stacked_ref[f, k : 2 * k, :] = hi
-        stacked_ref[f, 2 * k : 3 * k, :] = lo
+        stacked_ref[f, k : 2 * k, :] = lo
         return carry
 
     for i in range(PREP_CHUNKS):
@@ -255,23 +254,20 @@
     blocks, _ = swap_blocks(z, src, dst)
 
     first_half = lane_ids((z.rows // 2, LANES)) < z.block
+    low_lanes = lane_ids((z.rows, LANES)) < z.block
     pitch = z.rows + PITCH_PAD
 
     def fine_block(f, carry):
         v = blocks[z.block_place(blocks_ref[f]) + 1].reshape(z.rows // 2, LANES)
         turned = rolled(v, z.block)
-        hi, turned_hi = v.astype(jnp.bfloat16), turned.astype(jnp.bfloat16)
-        hi32, turned32 = hi.astype(jnp.float32), turned_hi.astype(jnp.float32)
-        upper = jnp.where(first_half, hi32, turned - turned32).astype(jnp.bfloat16)
-        lower = jnp.where(first_half, turned32, v - hi32).astype(jnp.bfloat16)
-        lhs = jnp.concatenate(
-            [
-                jnp.concatenate([upper, lower], axis=0),
-                jnp.concatenate([hi[:, : z.block], turned_hi[:, : z.block]], axis=0),
-            ],
-            axis=1,
+        v = jnp.concatenate(
+            [jnp.where(first_half, v, turned), jnp.where(first_half, turned, v)], axis=0
         )
+        hi = v.astype(jnp.bfloat16)
+        lo = jnp.where(low_lanes, v - hi.astype(jnp.float32), 0.0).astype(jnp.bfloat16)
+        lhs = jnp.concatenate([hi, lo], axis=0)
         out = jnp.dot(lhs, w_ref[f], preferred_element_type=jnp.float32)
+        out = out[: z.rows] + out[z.rows :]
         start = pl.multiple_of(f * pitch, SUB)
         for t in range(z.ct):
             fine_ref[t, pl.ds(start, z.rows), :] = out[:, t * LANES : (t + 1) * LANES]
@@ -391,7 +387,7 @@
         hi, lo = hi_lo(grad)
         out = lax.dot_general(
             jnp.concatenate([hi, lo], axis=0),
-            w_ref[f, z.block :, :],
+            w_ref[f],
             dims,
             preferred_element_type=jnp.float32,
         )
@@ -436,14 +432,13 @@
         total = total + ref[...]
     b = lax.axis_index("ty")
     for xq in range(z.xq):
-        rows = []
         for g in range(z.rg):
-            turn = lax.rem(LANES - (g // z.hg * z.n_ty + b) * z.cy, LANES)
-            rows.append(pltpu.roll(total[xq * z.rg + g], turn, 1))
-        part = jnp.concatenate(rows, axis=0)
-        for q in range(z.nq):
-            x = q * z.xq + xq
-            out_ref[:, x, :] = alpha_ref[:, x, :] + part[:, q * z.cy : (q + 1) * z.cy]
+            v = total[xq * z.rg + g]
+            for q in range(z.nq):
+                turn = lax.rem(2 * LANES - (q + g // z.hg * z.n_ty + b) * z.cy, LANES)
+                rows = slice(g * SUB, (g + 1) * SUB)
+                x = q * z.xq + xq
+                out_ref[rows, x, :] = alpha_ref[rows, x, :] + pltpu.roll(v, turn, 1)[:, : z.cy]
 
 
 def on_device(
@@ -493,7 +488,7 @@
     stacked, column, used = pl.pallas_call(
         functools.partial(prep_kernel, z),
         out_shape=(
-            shape((z.fine, 3 * z.block, z.bcells), bf16),
+            shape((z.fine, 2 * z.block, z.bcells), bf16),
             shape((z.bcells, z.obs), bf16),
             shape((1, z.obs), f32),
         ),

time: 49.9 us -> 48.8 us (0.978)
  Pallas kernels: 14.2 us -> 13.1 us
    pallas_call x1, Pallas kernels: 1.88 us -> 0.99 us  [on_device(): pl.pallas_call(functools.partial(finish_kernel, z), out_shape=shape((z.ro...]
where the time goes in v3:
time: 48.8 us; the launch traced here: 48.6 us
  waiting for transfers between devices  17.7 us (36%)
  starting transfers between devices  15.6 us (32%)
  Pallas kernels  13.1 us (27%)
  between operations  1.46 us (3%)
  other arithmetic  0.72 us (1%)
    ppermute x3, waiting for transfers between devices, on_device(): parts.append(lax.ppermute(incs[s], 'mem', ring(s)))  9.83 us
    ppermute x3, starting transfers between devices, on_device(): seens.append(lax.ppermute(seen, 'mem', ring(s)))  5.57 us
    ppermute x3, waiting for transfers between devices, on_device(): tiles.append(lax.ppermute(own, axes, z.chip_perm(s)))  5.18 us
    pallas_call x1, Pallas kernels, on_device(): pl.pallas_call(functools.partial(adjoint_kernel, z), out_shape=(shape((z....  4.67 us
    ppermute x3, starting transfers between devices, on_device(): tiles.append(lax.ppermute(own, axes, z.chip_perm(s)))  4.57 us
    pallas_call x1, Pallas kernels, on_device(): pl.pallas_call(functools.partial(forward_kernel, z), out_shape=(shape((z....  4.45 us
    ppermute x3, starting transfers between devices, on_device(): parts.append(lax.ppermute(incs[s], 'mem', ring(s)))  3.81 us
    ppermute x3, waiting for transfers between devices, on_device(): seens.append(lax.ppermute(seen, 'mem', ring(s)))  2.68 us
  transfers between devices with their start and end apart: 17, of which 8 were waited for; matrix products, arithmetic and copies ran while one was open for 1% of the time, Pallas kernels for 3%

profile of v3, /device:TPU:0, one launch (start us, length us, event | category | flops | bytes accessed | tf_op | source)
XLA Modules:
  0.0 48.6 jit_solution(9227727015682001585)
XLA Ops:
  0.7 1.4 %pack.1.refs_1_ = f32[17,8,128]{2,1,0:T(8,128)S(1)} custom-call(f32[32,16,32]{2,1,0:T(8,128)} %bitcast.16, f32[16,32]{1,0:T(8,128)} %rate_hbm.1), custom_call_target="tpu_custom_call" | custom-call | tf_op jit(solution)/shard_map/pack/pallas_call | solution.py:469
  2.1 3.0 %collective-permute-start = (f32[17,8,128]{2,1,0:T(8,128)S(1)}, f32[17,8,128]{2,1,0:T(8,128)S(1)}, u32[]{:S(2)}, u32[]{:S(2)}) collective-permute-start(f32[17,8,128]{2,1,0:T(8,128)S(1)} %pack.1.refs_1_), channel_id=1, source_target_pairs={{0,1},{1,0},{2,3},{3,2},{4,5},{5,4},{6,7},{7,6},{8,9},{9,8},{10,11... | collective-permute-start | bytes 208904 | tf_op jit(solution)/shard_map/ppermute | solution.py:484
  5.1 1.5 %collective-permute-start.1 = (f32[17,8,128]{2,1,0:T(8,128)S(1)}, f32[17,8,128]{2,1,0:T(8,128)S(1)}, u32[]{:S(2)}, u32[]{:S(2)}) collective-permute-start(f32[17,8,128]{2,1,0:T(8,128)S(1)} %pack.1.refs_1_), channel_id=1, source_target_pairs={{0,4},{1,5},{2,6},{3,7},{4,0},{5,1},{6,2},{7,3},{8,12},{9,13},{10,... | collective-permute-start | bytes 208904 | tf_op jit(solution)/shard_map/ppermute | solution.py:484
  6.6 0.9 %collective-permute-done.refs_2_ = f32[17,8,128]{2,1,0:T(8,128)S(1)} collective-permute-done((f32[17,8,128]{2,1,0:T(8,128)S(1)}, f32[17,8,128]{2,1,0:T(8,128)S(1)}, u32[]{:S(2)}, u32[]{:S(2)}) %collective-permute-start) | collective-permute-done | bytes 69664 | tf_op jit(solution)/shard_map/ppermute | solution.py:484
  7.5 1.9 %collective-permute-done.1.refs_3_ = f32[17,8,128]{2,1,0:T(8,128)S(1)} collective-permute-done((f32[17,8,128]{2,1,0:T(8,128)S(1)}, f32[17,8,128]{2,1,0:T(8,128)S(1)}, u32[]{:S(2)}, u32[]{:S(2)}) %collective-permute-start.1) | collective-permute-done | bytes 69664 | tf_op jit(solution)/shard_map/ppermute | solution.py:484
  9.4 2.4 %collective-permute-done.2.refs_4_ = f32[17,8,128]{2,1,0:T(8,128)S(1)} collective-permute-done((f32[17,8,128]{2,1,0:T(8,128)S(1)}, f32[17,8,128]{2,1,0:T(8,128)S(1)}, u32[]{:S(2)}, u32[]{:S(2)}) %collective-permute-start.2) | collective-permute-done | bytes 69664 | tf_op jit(solution)/shard_map/ppermute | solution.py:484
  12.5 1.6 %prep.1 = (bf16[32,128,256]{2,1,0:T(8,128)(2,1)S(1)}, bf16[256,512]{1,0:T(8,128)(2,1)S(1)}, f32[1,512]{1,0:T(1,128)S(1)}) custom-call(f32[32,64,256]{2,1,0:T(8,128)} %bitcast.25, s32[1,512]{1,0:T(1,128)} %bitcast.18, s32[1,1]{1,0:T(1,128)S(6)} %copy.12.refs_2_), custom_call_target="tpu_custom_call" | custom-call | flops 4000000 | bytes 5000000 | tf_op jit(solution)/shard_map/prep/pallas_call | solution.py:488
  14.2 4.4 %forward.1 = (f32[16,640]{1,0:T(8,128)S(1)}, f32[64,8,128]{2,1,0:T(8,128)S(1)}, f32[4,32,256]{2,1,0:T(8,128)S(1)}, f32[4,32,256]{2,1,0:T(8,128)S(1)}, f32[4,32,2...) custom-call(s32[32]{0:T(128)S(1)} %bitcast.23, f32[17,8,128]{2,1,0:T(8,128)S(1)} %pack.1.refs_1_, ...), custom_call_target="tpu_custom_call" | custom-call | flops 20000000 | bytes 8000000 | tf_op jit(solution)/shard_map/forward/pallas_call | solution.py:509
  18.7 1.6 %collective-permute-start.10 = (f32[16,640]{1,0:T(8,128)S(1)}, f32[16,640]{1,0:T(8,128)S(1)}, u32[]{:S(2)}, u32[]{:S(2)}) collective-permute-start(f32[16,640]{1,0:T(8,128)S(1)} %get-tuple-element.22.refs_2_), channel_id=1, source_target_pairs={{0,8},{8,16},{16,24},{24,0},{1,9},{9,17},{17,25},{25,1},{2,10},{10... | collective-permute-start | bytes 122888 | tf_op jit(solution)/shard_map/ppermute | solution.py:537
  20.3 2.6 %collective-permute-start.11 = (f32[16,640]{1,0:T(8,128)S(1)}, f32[16,640]{1,0:T(8,128)S(1)}, u32[]{:S(2)}, u32[]{:S(2)}) collective-permute-start(f32[16,640]{1,0:T(8,128)S(1)} %get-tuple-element.22.refs_2_), channel_id=1, source_target_pairs={{0,16},{8,24},{16,0},{24,8},{1,17},{9,25},{17,1},{25,9},{2,18},{10... | collective-permute-start | bytes 122888 | tf_op jit(solution)/shard_map/ppermute | solution.py:537
  22.9 1.3 %collective-permute-start.12 = (f32[16,640]{1,0:T(8,128)S(1)}, f32[16,640]{1,0:T(8,128)S(1)}, u32[]{:S(2)}, u32[]{:S(2)}) collective-permute-start(f32[16,640]{1,0:T(8,128)S(1)} %get-tuple-element.22.refs_2_), channel_id=1, source_target_pairs={{0,24},{8,0},{16,8},{24,16},{1,25},{9,1},{17,9},{25,17},{2,26},{10... | collective-permute-start | bytes 122888 | tf_op jit(solution)/shard_map/ppermute | solution.py:537
  24.2 0.4 collective-permute-done.10.refs_3_
  24.6 1.9 %collective-permute-done.11.refs_4_ = f32[16,640]{1,0:T(8,128)S(1)} collective-permute-done((f32[16,640]{1,0:T(8,128)S(1)}, f32[16,640]{1,0:T(8,128)S(1)}, u32[]{:S(2)}, u32[]{:S(2)}) %collective-permute-start.11) | collective-permute-done | bytes 40992 | tf_op jit(solution)/shard_map/ppermute | solution.py:537
  26.5 0.4 collective-permute-done.12.refs_5_
  26.9 4.7 %adjoint.1 = (f32[4,512]{1,0:T(4,128)}, f32[4,16,8,128]{3,2,1,0:T(8,128)S(1)}, f32[4,16,8,128]{3,2,1,0:T(8,128)S(1)}) custom-call(s32[32]{0:T(128)S(1)} %bitcast.24, f32[1,512]{1,0:T(1,128)S(1)} %get-tuple-element.21.refs_1_, f32[16,640]{1,0:T(8,128)S(1)} %get-tuple-element.22.refs_2_, f32[16,640]{1,0:T(8,128)S(1)} %collective-permute-done.10.refs_3_, ...), custom_call_target="tpu_custom_call" | custom-call | flops 20000000 | bytes 8000000 | tf_op jit(solution)/shard_map/adjoint/pallas_call | solution.py:542
  31.7 3.2 %collective-permute-start.9 = (f32[4,32,256]{2,1,0:T(8,128)S(1)}, f32[4,32,256]{2,1,0:T(8,128)S(1)}, u32[]{:S(2)}, u32[]{:S(2)}) collective-permute-start(f32[4,32,256]{2,1,0:T(8,128)S(1)} %get-tuple-element.20), channel_id=1, source_target_pairs={{0,24},{8,0},{16,8},{24,16},{1,25},{9,1},{17,9},{25,17},{2,26},{10... | collective-permute-start | bytes 393224 | tf_op jit(solution)/shard_map/ppermute | solution.py:539
  34.8 0.6 %collective-permute-start.7 = (f32[4,32,256]{2,1,0:T(8,128)S(1)}, f32[4,32,256]{2,1,0:T(8,128)S(1)}, u32[]{:S(2)}, u32[]{:S(2)}) collective-permute-start(f32[4,32,256]{2,1,0:T(8,128)S(1)} %get-tuple-element.18), channel_id=1, source_target_pairs={{0,8},{8,16},{16,24},{24,0},{1,9},{9,17},{17,25},{25,1},{2,10},{10... | collective-permute-start | bytes 393224 | tf_op jit(solution)/shard_map/ppermute | solution.py:539
  35.5 0.6 %collective-permute-start.14 = (f32[16,8,128]{2,1,0:T(8,128)S(1)}, f32[16,8,128]{2,1,0:T(8,128)S(1)}, u32[]{:S(2)}, u32[]{:S(2)}) collective-permute-start(f32[16,8,128]{2,1,0:T(8,128)S(1)} %get-tuple-element.29), channel_id=1, source_target_pairs={{0,1},{1,0},{2,3},{3,2},{4,5},{5,4},{6,7},{7,6},{8,9},{9,8},{10,11... | collective-permute-start | bytes 196616 | tf_op jit(solution)/shard_map/ppermute | solution.py:566
  36.1 0.5 %collective-permute-start.15 = (f32[16,8,128]{2,1,0:T(8,128)S(1)}, f32[16,8,128]{2,1,0:T(8,128)S(1)}, u32[]{:S(2)}, u32[]{:S(2)}) collective-permute-start(f32[16,8,128]{2,1,0:T(8,128)S(1)} %get-tuple-element.28), channel_id=1, source_target_pairs={{0,4},{1,5},{2,6},{3,7},{4,0},{5,1},{6,2},{7,3},{8,12},{9,13},{10,... | collective-permute-start | bytes 196616 | tf_op jit(solution)/shard_map/ppermute | solution.py:566
  36.6 2.2 %collective-permute-done.9 = f32[4,32,256]{2,1,0:T(8,128)S(1)} collective-permute-done((f32[4,32,256]{2,1,0:T(8,128)S(1)}, f32[4,32,256]{2,1,0:T(8,128)S(1)}, u32[]{:S(2)}, u32[]{:S(2)}) %collective-permute-start.9) | collective-permute-done | bytes 131104 | tf_op jit(solution)/shard_map/ppermute | solution.py:539
  38.8 0.5 collective-permute-start.16
  39.3 7.6 %collective-permute-done.8 = f32[4,32,256]{2,1,0:T(8,128)S(1)} collective-permute-done((f32[4,32,256]{2,1,0:T(8,128)S(1)}, f32[4,32,256]{2,1,0:T(8,128)S(1)}, u32[]{:S(2)}, u32[]{:S(2)}) %collective-permute-start.8) | collective-permute-done | bytes 131104 | tf_op jit(solution)/shard_map/ppermute | solution.py:539
  46.9 0.7 %add_add_fusion = f32[4,32,256]{2,1,0:T(8,128)} fusion(f32[4,32,256]{2,1,0:T(8,128)S(1)} %collective-permute-done.9, f32[4,32,256]{2,1,0:T(8,128)S(1)} %collective-permute-done.8, f32[4,32,256]{2,1,0:T(8,128)S(1)} %get-tuple-element.17, f32[4,32,256]{2,1,0:T(8,128)S(1)} %collective-permute-done.7), kind=kLoop, calls=%fused_computation | loop fusion | flops 98304 | bytes 655360 | tf_op jit(solution)/shard_map/add | solution.py:577
  47.6 1.0 %finish.1 = f32[32,16,32]{2,1,0:T(8,128)} custom-call(f32[32,16,32]{2,1,0:T(8,128)S(1)} %bitcast.17, f32[16,8,128]{2,1,0:T(8,128)S(1)} %get-tuple-element.30.refs_0_, f32[16,8,128]{2,1,0:T(8,128)S(1)} %collective-permute-done.14.refs_1_, f32[16,8,128]{2,1,0:T(8,128)S(1)} %collective-permute-done.15.refs_2_, f32[16,8,128]{2,1,0:T(8,128)S(1)} %collective-permute-done.16.refs_3_), custom_call_target="tpu_custom_call" | custom-call | tf_op jit(solution)/shard_map/finish/pallas_call | solution.py:567
  (29 shorter events, 0.2 us)
Async XLA Ops:
  0.6 13.5 %copy-start.2 = (s32[1,1,512]{2,1,0:T(1,128)S(1)}, s32[1,1,512]{2,1,0:T(1,128)}, u32[]{:S(2)}) copy-start(s32[1,1,512]{2,1,0:T(1,128)} %param.14) | copy-start | bytes 6148
  0.6 13.5 %copy-start.5 = (s32[1,1,32]{2,1,0:T(1,128)S(1)}, s32[1,1,32]{2,1,0:T(1,128)}, u32[]{:S(2)}) copy-start(s32[1,1,32]{2,1,0:T(1,128)} %param.11) | copy-start | bytes 388
  0.7 13.5 %copy-start = (bf16[8,4,4,32,256]{4,3,2,1,0:T(8,128)(2,1)S(1)}, bf16[8,4,4,32,256]{4,3,2,1,0:T(8,128)(2,1)}, u32[]{:S(2)}) copy-start(bf16[8,4,4,32,256]{4,3,2,1,0:T(8,128)(2,1)} %refs_7_.1) | copy-start | bytes 6291460
  0.7 13.5 %copy-start.3 = (f32[1,1,4,512]{3,2,1,0:T(4,128)S(1)}, f32[1,1,4,512]{3,2,1,0:T(4,128)}, u32[]{:S(2)}) copy-start(f32[1,1,4,512]{3,2,1,0:T(4,128)} %param.16) | copy-start | bytes 24580
  0.7 13.5 %copy-start.4 = (f32[1,1,4,512]{3,2,1,0:T(4,128)S(1)}, f32[1,1,4,512]{3,2,1,0:T(4,128)}, u32[]{:S(2)}) copy-start(f32[1,1,4,512]{3,2,1,0:T(4,128)} %param.17) | copy-start | bytes 24580
  2.1 5.5 %collective-permute-start = (f32[17,8,128]{2,1,0:T(8,128)S(1)}, f32[17,8,128]{2,1,0:T(8,128)S(1)}, u32[]{:S(2)}, u32[]{:S(2)}) collective-permute-start(f32[17,8,128]{2,1,0:T(8,128)S(1)} %pack.1.refs_1_), channel_id=1, source_target_pairs={{0,1},{1,0},{2,3},{3,2},{4,5},{5,4},{6,7},{7,6},{8,9},{9,8},{10,11... | collective-permute-start | bytes 208904 | tf_op jit(solution)/shard_map/ppermute | solution.py:484
  5.1 4.3 %collective-permute-start.1 = (f32[17,8,128]{2,1,0:T(8,128)S(1)}, f32[17,8,128]{2,1,0:T(8,128)S(1)}, u32[]{:S(2)}, u32[]{:S(2)}) collective-permute-start(f32[17,8,128]{2,1,0:T(8,128)S(1)} %pack.1.refs_1_), channel_id=1, source_target_pairs={{0,4},{1,5},{2,6},{3,7},{4,0},{5,1},{6,2},{7,3},{8,12},{9,13},{10,... | collective-permute-start | bytes 208904 | tf_op jit(solution)/shard_map/ppermute | solution.py:484
  6.6 5.2 %collective-permute-start.2 = (f32[17,8,128]{2,1,0:T(8,128)S(1)}, f32[17,8,128]{2,1,0:T(8,128)S(1)}, u32[]{:S(2)}, u32[]{:S(2)}) collective-permute-start(f32[17,8,128]{2,1,0:T(8,128)S(1)} %pack.1.refs_1_), channel_id=1, source_target_pairs={{0,5},{1,4},{2,7},{3,6},{4,1},{5,0},{6,3},{7,2},{8,13},{9,12},{10,... | collective-permute-start | bytes 208904 | tf_op jit(solution)/shard_map/ppermute | solution.py:484
  6.6 7.5 %collective-permute-start.3 = (f32[17,8,128]{2,1,0:T(8,128)S(1)}, f32[17,8,128]{2,1,0:T(8,128)S(1)}, u32[]{:S(2)}, u32[]{:S(2)}) collective-permute-start(f32[17,8,128]{2,1,0:T(8,128)S(1)} %pack.1.refs_1_), channel_id=1, source_target_pairs={{0,2},{1,3},{2,0},{3,1},{4,6},{5,7},{6,4},{7,5},{8,10},{9,11},{10,... | collective-permute-start | bytes 208904 | tf_op jit(solution)/shard_map/ppermute | solution.py:486
  7.5 6.6 %collective-permute-start.4 = (f32[17,8,128]{2,1,0:T(8,128)S(1)}, f32[17,8,128]{2,1,0:T(8,128)S(1)}, u32[]{:S(2)}, u32[]{:S(2)}) collective-permute-start(f32[17,8,128]{2,1,0:T(8,128)S(1)} %collective-permute-done.refs_2_), channel_id=1, source_target_pairs={{0,2},{1,3},{2,0},{3,1},{4,6},{5,7},{6,4},{7,5},{8,10},{9,11},{10,... | collective-permute-start | bytes 208904 | tf_op jit(solution)/shard_map/ppermute | solution.py:486
  9.4 4.7 %collective-permute-start.5 = (f32[17,8,128]{2,1,0:T(8,128)S(1)}, f32[17,8,128]{2,1,0:T(8,128)S(1)}, u32[]{:S(2)}, u32[]{:S(2)}) collective-permute-start(f32[17,8,128]{2,1,0:T(8,128)S(1)} %collective-permute-done.1.refs_3_), channel_id=1, source_target_pairs={{0,2},{1,3},{2,0},{3,1},{4,6},{5,7},{6,4},{7,5},{8,10},{9,11},{10,... | collective-permute-start | bytes 208904 | tf_op jit(solution)/shard_map/ppermute | solution.py:486
  11.8 2.3 %collective-permute-start.6 = (f32[17,8,128]{2,1,0:T(8,128)S(1)}, f32[17,8,128]{2,1,0:T(8,128)S(1)}, u32[]{:S(2)}, u32[]{:S(2)}) collective-permute-start(f32[17,8,128]{2,1,0:T(8,128)S(1)} %collective-permute-done.2.refs_4_), channel_id=1, source_target_pairs={{0,2},{1,3},{2,0},{3,1},{4,6},{5,7},{6,4},{7,5},{8,10},{9,11},{10,... | collective-permute-start | bytes 208904 | tf_op jit(solution)/shard_map/ppermute | solution.py:486
  18.7 5.9 %collective-permute-start.10 = (f32[16,640]{1,0:T(8,128)S(1)}, f32[16,640]{1,0:T(8,128)S(1)}, u32[]{:S(2)}, u32[]{:S(2)}) collective-permute-start(f32[16,640]{1,0:T(8,128)S(1)} %get-tuple-element.22.refs_2_), channel_id=1, source_target_pairs={{0,8},{8,16},{16,24},{24,0},{1,9},{9,17},{17,25},{25,1},{2,10},{10... | collective-permute-start | bytes 122888 | tf_op jit(solution)/shard_map/ppermute | solution.py:537
  20.3 6.2 %collective-permute-start.11 = (f32[16,640]{1,0:T(8,128)S(1)}, f32[16,640]{1,0:T(8,128)S(1)}, u32[]{:S(2)}, u32[]{:S(2)}) collective-permute-start(f32[16,640]{1,0:T(8,128)S(1)} %get-tuple-element.22.refs_2_), channel_id=1, source_target_pairs={{0,16},{8,24},{16,0},{24,8},{1,17},{9,25},{17,1},{25,9},{2,18},{10... | collective-permute-start | bytes 122888 | tf_op jit(solution)/shard_map/ppermute | solution.py:537
  22.9 4.0 %collective-permute-start.12 = (f32[16,640]{1,0:T(8,128)S(1)}, f32[16,640]{1,0:T(8,128)S(1)}, u32[]{:S(2)}, u32[]{:S(2)}) collective-permute-start(f32[16,640]{1,0:T(8,128)S(1)} %get-tuple-element.22.refs_2_), channel_id=1, source_target_pairs={{0,24},{8,0},{16,8},{24,16},{1,25},{9,1},{17,9},{25,17},{2,26},{10... | collective-permute-start | bytes 122888 | tf_op jit(solution)/shard_map/ppermute | solution.py:537
  26.9 20.7 %copy-start.1 = (f32[8,4,16,32]{3,2,1,0:T(8,128)S(1)}, f32[8,4,16,32]{3,2,1,0:T(8,128)}, u32[]{:S(2)}) copy-start(f32[8,4,16,32]{3,2,1,0:T(8,128)} %param.9) | copy-start | bytes 196612
  31.6 3.9 %collective-permute-start.13 = (f32[4,16,8,128]{3,2,1,0:T(8,128)S(1)}, f32[4,16,8,128]{3,2,1,0:T(8,128)S(1)}, u32[]{:S(2)}, u32[]{:S(2)}) collective-permute-start(f32[4,16,8,128]{3,2,1,0:T(8,128)S(1)} %get-tuple-element.26), channel_id=1, source_target_pairs={{0,2},{1,3},{2,0},{3,1},{4,6},{5,7},{6,4},{7,5},{8,10},{9,11},{10,... | collective-permute-start | bytes 786440 | tf_op jit(solution)/shard_map/ppermute | solution.py:564
  31.7 7.1 %collective-permute-start.9 = (f32[4,32,256]{2,1,0:T(8,128)S(1)}, f32[4,32,256]{2,1,0:T(8,128)S(1)}, u32[]{:S(2)}, u32[]{:S(2)}) collective-permute-start(f32[4,32,256]{2,1,0:T(8,128)S(1)} %get-tuple-element.20), channel_id=1, source_target_pairs={{0,24},{8,0},{16,8},{24,16},{1,25},{9,1},{17,9},{25,17},{2,26},{10... | collective-permute-start | bytes 393224 | tf_op jit(solution)/shard_map/ppermute | solution.py:539
  34.8 12.1 %collective-permute-start.8 = (f32[4,32,256]{2,1,0:T(8,128)S(1)}, f32[4,32,256]{2,1,0:T(8,128)S(1)}, u32[]{:S(2)}, u32[]{:S(2)}) collective-permute-start(f32[4,32,256]{2,1,0:T(8,128)S(1)} %get-tuple-element.19), channel_id=1, source_target_pairs={{0,16},{8,24},{16,0},{24,8},{1,17},{9,25},{17,1},{25,9},{2,18},{10... | collective-permute-start | bytes 393224 | tf_op jit(solution)/shard_map/ppermute | solution.py:539
  34.8 12.1 %collective-permute-start.7 = (f32[4,32,256]{2,1,0:T(8,128)S(1)}, f32[4,32,256]{2,1,0:T(8,128)S(1)}, u32[]{:S(2)}, u32[]{:S(2)}) collective-permute-start(f32[4,32,256]{2,1,0:T(8,128)S(1)} %get-tuple-element.18), channel_id=1, source_target_pairs={{0,8},{8,16},{16,24},{24,0},{1,9},{9,17},{17,25},{25,1},{2,10},{10... | collective-permute-start | bytes 393224 | tf_op jit(solution)/shard_map/ppermute | solution.py:539
  35.5 12.1 %collective-permute-start.14 = (f32[16,8,128]{2,1,0:T(8,128)S(1)}, f32[16,8,128]{2,1,0:T(8,128)S(1)}, u32[]{:S(2)}, u32[]{:S(2)}) collective-permute-start(f32[16,8,128]{2,1,0:T(8,128)S(1)} %get-tuple-element.29), channel_id=1, source_target_pairs={{0,1},{1,0},{2,3},{3,2},{4,5},{5,4},{6,7},{7,6},{8,9},{9,8},{10,11... | collective-permute-start | bytes 196616 | tf_op jit(solution)/shard_map/ppermute | solution.py:566
  36.1 11.5 %collective-permute-start.15 = (f32[16,8,128]{2,1,0:T(8,128)S(1)}, f32[16,8,128]{2,1,0:T(8,128)S(1)}, u32[]{:S(2)}, u32[]{:S(2)}) collective-permute-start(f32[16,8,128]{2,1,0:T(8,128)S(1)} %get-tuple-element.28), channel_id=1, source_target_pairs={{0,4},{1,5},{2,6},{3,7},{4,0},{5,1},{6,2},{7,3},{8,12},{9,13},{10,... | collective-permute-start | bytes 196616 | tf_op jit(solution)/shard_map/ppermute | solution.py:566
  38.8 8.8 %collective-permute-start.16 = (f32[16,8,128]{2,1,0:T(8,128)S(1)}, f32[16,8,128]{2,1,0:T(8,128)S(1)}, u32[]{:S(2)}, u32[]{:S(2)}) collective-permute-start(f32[16,8,128]{2,1,0:T(8,128)S(1)} %get-tuple-element.27), channel_id=1, source_target_pairs={{0,5},{1,4},{2,7},{3,6},{4,1},{5,0},{6,3},{7,2},{8,13},{9,12},{10,... | collective-permute-start | bytes 196616 | tf_op jit(solution)/shard_map/ppermute | solution.py:566

commit v4 on v3

--- a/solution.py
+++ b/solution.py
@@ -15,6 +15,7 @@
 PITCH_PAD = 8
 PREP_CHUNKS = 4
 SWAP_UNROLL = 16
+PRODUCTS = 2
 
 
 VM = pl.BlockSpec(memory_space=pltpu.VMEM)
@@ -295,16 +296,17 @@
     where, _ = split2(cells_ref[...], z.bcells)
     ids = lax.broadcasted_iota(jnp.int32, (z.fine, z.obs), 0)
     here = ids == where
-    for l in range(z.levels):
-        part = inc[l * z.vars : (l + 1) * z.vars].reshape(z.vars * z.fine, z.bcells)
-        hi, lo = hi_lo(part)
-        seen = jnp.dot(hi, column_ref[...], preferred_element_type=jnp.float32) + jnp.dot(
-            lo, column_ref[...], preferred_element_type=jnp.float32
+    n = z.slabs // PRODUCTS
+    for i in range(PRODUCTS):
+        hi, lo = hi_lo(inc[i * n : (i + 1) * n].reshape(n * z.fine, z.bcells))
+        seen = jnp.dot(
+            jnp.concatenate([hi, lo], axis=0), column_ref[...], preferred_element_type=jnp.float32
         )
-        for v in range(z.vars):
-            s = l * z.vars + v
-            got = jnp.where(here, seen[v * z.fine : (v + 1) * z.fine], 0.0)
-            seen_ref[s : s + 1, : z.obs] = jnp.sum(got, axis=0, keepdims=True)
+        for k in range(n):
+            part = seen[k * z.fine : (k + 1) * z.fine] + seen[(n + k) * z.fine : (n + k + 1) * z.fine]
+            seen_ref[i * n + k : i * n + k + 1, : z.obs] = jnp.sum(
+                jnp.where(here, part, 0.0), axis=0, keepdims=True
+            )
     seen_ref[:, z.obs :] = jnp.zeros((z.slabs, LANES), jnp.float32)
     for g in range(z.n_mem):
         mine = slice(g * z.slab_dev, (g + 1) * z.slab_dev)
@@ -346,19 +348,21 @@
             mine = jnp.where(g == me, rows[g * z.slab_dev + j], mine)
         out_ref[j : j + 1] = mine
     dims = (((1,), (1,)), ((), ()))
-    for l in range(z.levels):
+    n = z.slabs // PRODUCTS
+    for i in range(PRODUCTS):
         his, los = [], []
-        for v in range(z.vars):
-            row = jnp.where(here, rows[l * z.vars + v], 0.0)
-            hi, lo = hi_lo(row)
-            his.append(hi)
-            los.append(lo)
+        for k in range(n):
+            hi, lo = hi_lo(rows[i * n + k])
+            his.append(jnp.where(here, hi.astype(jnp.float32), 0.0).astype(jnp.bfloat16))
+            los.append(jnp.where(here, lo.astype(jnp.float32), 0.0).astype(jnp.bfloat16))
         part = lax.dot_general(
-            jnp.concatenate(his, axis=0), column_ref[...], dims, preferred_element_type=jnp.float32
-        ) + lax.dot_general(
-            jnp.concatenate(los, axis=0), column_ref[...], dims, preferred_element_type=jnp.float32
+            jnp.concatenate(his + los, axis=0),
+            column_ref[...],
+            dims,
+            preferred_element_type=jnp.float32,
         )
-        force[l * z.vars : (l + 1) * z.vars] = part.reshape(z.vars, z.fine, z.bcells)
+        part = part[: n * z.fine] + part[n * z.fine :]
+        force[i * n : (i + 1) * n] = part.reshape(n, z.fine, z.bcells)
 
     pitch = z.fine + PITCH_PAD
 

time: 48.8 us -> 48.5 us (level)
  no operation moved by 1% of the time
where the time goes in v4:
time: 48.5 us; the launch traced here: 48.3 us
  waiting for transfers between devices  17.7 us (36%)
  starting transfers between devices  15.6 us (32%)
  Pallas kernels  12.8 us (26%)
  between operations  1.46 us (3%)
  other arithmetic  0.72 us (1%)
    ppermute x3, waiting for transfers between devices, on_device(): parts.append(lax.ppermute(incs[s], 'mem', ring(s)))  9.82 us
    ppermute x3, starting transfers between devices, on_device(): seens.append(lax.ppermute(seen, 'mem', ring(s)))  5.57 us
    ppermute x3, waiting for transfers between devices, on_device(): tiles.append(lax.ppermute(own, axes, z.chip_perm(s)))  5.18 us
    ppermute x3, starting transfers between devices, on_device(): tiles.append(lax.ppermute(own, axes, z.chip_perm(s)))  4.57 us
    pallas_call x1, Pallas kernels, on_device(): pl.pallas_call(functools.partial(forward_kernel, z), out_shape=(shape((z....  4.44 us
    pallas_call x1, Pallas kernels, on_device(): pl.pallas_call(functools.partial(adjoint_kernel, z), out_shape=(shape((z....  4.35 us
    ppermute x3, starting transfers between devices, on_device(): parts.append(lax.ppermute(incs[s], 'mem', ring(s)))  3.81 us
    ppermute x3, waiting for transfers between devices, on_device(): seens.append(lax.ppermute(seen, 'mem', ring(s)))  2.69 us
  transfers between devices with their start and end apart: 17, of which 8 were waited for; matrix products, arithmetic and copies ran while one was open for 1% of the time, Pallas kernels for 3%

profile of v4, /device:TPU:0, one launch (start us, length us, event | category | flops | bytes accessed | tf_op | source)
XLA Modules:
  0.0 48.3 jit_solution(2403902535959266374)
XLA Ops:
  0.7 1.4 %pack.1.refs_1_ = f32[17,8,128]{2,1,0:T(8,128)S(1)} custom-call(f32[32,16,32]{2,1,0:T(8,128)} %bitcast.16, f32[16,32]{1,0:T(8,128)} %rate_hbm.1), custom_call_target="tpu_custom_call" | custom-call | tf_op jit(solution)/shard_map/pack/pallas_call | solution.py:473
  2.1 3.0 %collective-permute-start = (f32[17,8,128]{2,1,0:T(8,128)S(1)}, f32[17,8,128]{2,1,0:T(8,128)S(1)}, u32[]{:S(2)}, u32[]{:S(2)}) collective-permute-start(f32[17,8,128]{2,1,0:T(8,128)S(1)} %pack.1.refs_1_), channel_id=1, source_target_pairs={{0,1},{1,0},{2,3},{3,2},{4,5},{5,4},{6,7},{7,6},{8,9},{9,8},{10,11... | collective-permute-start | bytes 208904 | tf_op jit(solution)/shard_map/ppermute | solution.py:488
  5.1 1.5 %collective-permute-start.1 = (f32[17,8,128]{2,1,0:T(8,128)S(1)}, f32[17,8,128]{2,1,0:T(8,128)S(1)}, u32[]{:S(2)}, u32[]{:S(2)}) collective-permute-start(f32[17,8,128]{2,1,0:T(8,128)S(1)} %pack.1.refs_1_), channel_id=1, source_target_pairs={{0,4},{1,5},{2,6},{3,7},{4,0},{5,1},{6,2},{7,3},{8,12},{9,13},{10,... | collective-permute-start | bytes 208904 | tf_op jit(solution)/shard_map/ppermute | solution.py:488
  6.6 0.9 %collective-permute-done.refs_2_ = f32[17,8,128]{2,1,0:T(8,128)S(1)} collective-permute-done((f32[17,8,128]{2,1,0:T(8,128)S(1)}, f32[17,8,128]{2,1,0:T(8,128)S(1)}, u32[]{:S(2)}, u32[]{:S(2)}) %collective-permute-start) | collective-permute-done | bytes 69664 | tf_op jit(solution)/shard_map/ppermute | solution.py:488
  7.5 1.9 %collective-permute-done.1.refs_3_ = f32[17,8,128]{2,1,0:T(8,128)S(1)} collective-permute-done((f32[17,8,128]{2,1,0:T(8,128)S(1)}, f32[17,8,128]{2,1,0:T(8,128)S(1)}, u32[]{:S(2)}, u32[]{:S(2)}) %collective-permute-start.1) | collective-permute-done | bytes 69664 | tf_op jit(solution)/shard_map/ppermute | solution.py:488
  9.4 2.4 %collective-permute-done.2.refs_4_ = f32[17,8,128]{2,1,0:T(8,128)S(1)} collective-permute-done((f32[17,8,128]{2,1,0:T(8,128)S(1)}, f32[17,8,128]{2,1,0:T(8,128)S(1)}, u32[]{:S(2)}, u32[]{:S(2)}) %collective-permute-start.2) | collective-permute-done | bytes 69664 | tf_op jit(solution)/shard_map/ppermute | solution.py:488
  12.5 1.6 %prep.1 = (bf16[32,128,256]{2,1,0:T(8,128)(2,1)S(1)}, bf16[256,512]{1,0:T(8,128)(2,1)S(1)}, f32[1,512]{1,0:T(1,128)S(1)}) custom-call(f32[32,64,256]{2,1,0:T(8,128)} %bitcast.25, s32[1,512]{1,0:T(1,128)} %bitcast.18, s32[1,1]{1,0:T(1,128)S(6)} %copy.12.refs_2_), custom_call_target="tpu_custom_call" | custom-call | flops 4000000 | bytes 5000000 | tf_op jit(solution)/shard_map/prep/pallas_call | solution.py:492
  14.2 4.4 %forward.1 = (f32[16,640]{1,0:T(8,128)S(1)}, f32[64,8,128]{2,1,0:T(8,128)S(1)}, f32[4,32,256]{2,1,0:T(8,128)S(1)}, f32[4,32,256]{2,1,0:T(8,128)S(1)}, f32[4,32,2...) custom-call(s32[32]{0:T(128)S(1)} %bitcast.23, f32[17,8,128]{2,1,0:T(8,128)S(1)} %pack.1.refs_1_, ...), custom_call_target="tpu_custom_call" | custom-call | flops 20000000 | bytes 8000000 | tf_op jit(solution)/shard_map/forward/pallas_call | solution.py:513
  18.7 1.6 %collective-permute-start.10 = (f32[16,640]{1,0:T(8,128)S(1)}, f32[16,640]{1,0:T(8,128)S(1)}, u32[]{:S(2)}, u32[]{:S(2)}) collective-permute-start(f32[16,640]{1,0:T(8,128)S(1)} %get-tuple-element.22.refs_2_), channel_id=1, source_target_pairs={{0,8},{8,16},{16,24},{24,0},{1,9},{9,17},{17,25},{25,1},{2,10},{10... | collective-permute-start | bytes 122888 | tf_op jit(solution)/shard_map/ppermute | solution.py:541
  20.3 2.6 %collective-permute-start.11 = (f32[16,640]{1,0:T(8,128)S(1)}, f32[16,640]{1,0:T(8,128)S(1)}, u32[]{:S(2)}, u32[]{:S(2)}) collective-permute-start(f32[16,640]{1,0:T(8,128)S(1)} %get-tuple-element.22.refs_2_), channel_id=1, source_target_pairs={{0,16},{8,24},{16,0},{24,8},{1,17},{9,25},{17,1},{25,9},{2,18},{10... | collective-permute-start | bytes 122888 | tf_op jit(solution)/shard_map/ppermute | solution.py:541
  22.9 1.3 %collective-permute-start.12 = (f32[16,640]{1,0:T(8,128)S(1)}, f32[16,640]{1,0:T(8,128)S(1)}, u32[]{:S(2)}, u32[]{:S(2)}) collective-permute-start(f32[16,640]{1,0:T(8,128)S(1)} %get-tuple-element.22.refs_2_), channel_id=1, source_target_pairs={{0,24},{8,0},{16,8},{24,16},{1,25},{9,1},{17,9},{25,17},{2,26},{10... | collective-permute-start | bytes 122888 | tf_op jit(solution)/shard_map/ppermute | solution.py:541
  24.2 0.4 collective-permute-done.10.refs_3_
  24.6 1.9 %collective-permute-done.11.refs_4_ = f32[16,640]{1,0:T(8,128)S(1)} collective-permute-done((f32[16,640]{1,0:T(8,128)S(1)}, f32[16,640]{1,0:T(8,128)S(1)}, u32[]{:S(2)}, u32[]{:S(2)}) %collective-permute-start.11) | collective-permute-done | bytes 40992 | tf_op jit(solution)/shard_map/ppermute | solution.py:541
  26.5 0.4 collective-permute-done.12.refs_5_
  26.9 4.3 %adjoint.1 = (f32[4,512]{1,0:T(4,128)}, f32[4,16,8,128]{3,2,1,0:T(8,128)S(1)}, f32[4,16,8,128]{3,2,1,0:T(8,128)S(1)}) custom-call(s32[32]{0:T(128)S(1)} %bitcast.24, f32[1,512]{1,0:T(1,128)S(1)} %get-tuple-element.21.refs_1_, f32[16,640]{1,0:T(8,128)S(1)} %get-tuple-element.22.refs_2_, f32[16,640]{1,0:T(8,128)S(1)} %collective-permute-done.10.refs_3_, ...), custom_call_target="tpu_custom_call" | custom-call | flops 20000000 | bytes 8000000 | tf_op jit(solution)/shard_map/adjoint/pallas_call | solution.py:546
  31.3 3.2 %collective-permute-start.9 = (f32[4,32,256]{2,1,0:T(8,128)S(1)}, f32[4,32,256]{2,1,0:T(8,128)S(1)}, u32[]{:S(2)}, u32[]{:S(2)}) collective-permute-start(f32[4,32,256]{2,1,0:T(8,128)S(1)} %get-tuple-element.20), channel_id=1, source_target_pairs={{0,24},{8,0},{16,8},{24,16},{1,25},{9,1},{17,9},{25,17},{2,26},{10... | collective-permute-start | bytes 393224 | tf_op jit(solution)/shard_map/ppermute | solution.py:543
  34.5 0.6 %collective-permute-start.7 = (f32[4,32,256]{2,1,0:T(8,128)S(1)}, f32[4,32,256]{2,1,0:T(8,128)S(1)}, u32[]{:S(2)}, u32[]{:S(2)}) collective-permute-start(f32[4,32,256]{2,1,0:T(8,128)S(1)} %get-tuple-element.18), channel_id=1, source_target_pairs={{0,8},{8,16},{16,24},{24,0},{1,9},{9,17},{17,25},{25,1},{2,10},{10... | collective-permute-start | bytes 393224 | tf_op jit(solution)/shard_map/ppermute | solution.py:543
  35.2 0.6 %collective-permute-start.14 = (f32[16,8,128]{2,1,0:T(8,128)S(1)}, f32[16,8,128]{2,1,0:T(8,128)S(1)}, u32[]{:S(2)}, u32[]{:S(2)}) collective-permute-start(f32[16,8,128]{2,1,0:T(8,128)S(1)} %get-tuple-element.29), channel_id=1, source_target_pairs={{0,1},{1,0},{2,3},{3,2},{4,5},{5,4},{6,7},{7,6},{8,9},{9,8},{10,11... | collective-permute-start | bytes 196616 | tf_op jit(solution)/shard_map/ppermute | solution.py:570
  35.8 0.5 %collective-permute-start.15 = (f32[16,8,128]{2,1,0:T(8,128)S(1)}, f32[16,8,128]{2,1,0:T(8,128)S(1)}, u32[]{:S(2)}, u32[]{:S(2)}) collective-permute-start(f32[16,8,128]{2,1,0:T(8,128)S(1)} %get-tuple-element.28), channel_id=1, source_target_pairs={{0,4},{1,5},{2,6},{3,7},{4,0},{5,1},{6,2},{7,3},{8,12},{9,13},{10,... | collective-permute-start | bytes 196616 | tf_op jit(solution)/shard_map/ppermute | solution.py:570
  36.3 2.2 %collective-permute-done.9 = f32[4,32,256]{2,1,0:T(8,128)S(1)} collective-permute-done((f32[4,32,256]{2,1,0:T(8,128)S(1)}, f32[4,32,256]{2,1,0:T(8,128)S(1)}, u32[]{:S(2)}, u32[]{:S(2)}) %collective-permute-start.9) | collective-permute-done | bytes 131104 | tf_op jit(solution)/shard_map/ppermute | solution.py:543
  38.5 0.5 collective-permute-start.16
  39.0 7.6 %collective-permute-done.8 = f32[4,32,256]{2,1,0:T(8,128)S(1)} collective-permute-done((f32[4,32,256]{2,1,0:T(8,128)S(1)}, f32[4,32,256]{2,1,0:T(8,128)S(1)}, u32[]{:S(2)}, u32[]{:S(2)}) %collective-permute-start.8) | collective-permute-done | bytes 131104 | tf_op jit(solution)/shard_map/ppermute | solution.py:543
  46.6 0.7 %add_add_fusion = f32[4,32,256]{2,1,0:T(8,128)} fusion(f32[4,32,256]{2,1,0:T(8,128)S(1)} %collective-permute-done.9, f32[4,32,256]{2,1,0:T(8,128)S(1)} %collective-permute-done.8, f32[4,32,256]{2,1,0:T(8,128)S(1)} %get-tuple-element.17, f32[4,32,256]{2,1,0:T(8,128)S(1)} %collective-permute-done.7), kind=kLoop, calls=%fused_computation | loop fusion | flops 98304 | bytes 655360 | tf_op jit(solution)/shard_map/add | solution.py:581
  47.3 1.0 %finish.1 = f32[32,16,32]{2,1,0:T(8,128)} custom-call(f32[32,16,32]{2,1,0:T(8,128)S(1)} %bitcast.17, f32[16,8,128]{2,1,0:T(8,128)S(1)} %get-tuple-element.30.refs_0_, f32[16,8,128]{2,1,0:T(8,128)S(1)} %collective-permute-done.14.refs_1_, f32[16,8,128]{2,1,0:T(8,128)S(1)} %collective-permute-done.15.refs_2_, f32[16,8,128]{2,1,0:T(8,128)S(1)} %collective-permute-done.16.refs_3_), custom_call_target="tpu_custom_call" | custom-call | tf_op jit(solution)/shard_map/finish/pallas_call | solution.py:571
  (29 shorter events, 0.2 us)
Async XLA Ops:
  0.6 13.5 %copy-start.2 = (s32[1,1,512]{2,1,0:T(1,128)S(1)}, s32[1,1,512]{2,1,0:T(1,128)}, u32[]{:S(2)}) copy-start(s32[1,1,512]{2,1,0:T(1,128)} %param.14) | copy-start | bytes 6148
  0.6 13.5 %copy-start.5 = (s32[1,1,32]{2,1,0:T(1,128)S(1)}, s32[1,1,32]{2,1,0:T(1,128)}, u32[]{:S(2)}) copy-start(s32[1,1,32]{2,1,0:T(1,128)} %param.11) | copy-start | bytes 388
  0.7 13.5 %copy-start = (bf16[8,4,4,32,256]{4,3,2,1,0:T(8,128)(2,1)S(1)}, bf16[8,4,4,32,256]{4,3,2,1,0:T(8,128)(2,1)}, u32[]{:S(2)}) copy-start(bf16[8,4,4,32,256]{4,3,2,1,0:T(8,128)(2,1)} %refs_7_.1) | copy-start | bytes 6291460
  0.7 13.5 %copy-start.3 = (f32[1,1,4,512]{3,2,1,0:T(4,128)S(1)}, f32[1,1,4,512]{3,2,1,0:T(4,128)}, u32[]{:S(2)}) copy-start(f32[1,1,4,512]{3,2,1,0:T(4,128)} %param.16) | copy-start | bytes 24580
  0.7 13.5 %copy-start.4 = (f32[1,1,4,512]{3,2,1,0:T(4,128)S(1)}, f32[1,1,4,512]{3,2,1,0:T(4,128)}, u32[]{:S(2)}) copy-start(f32[1,1,4,512]{3,2,1,0:T(4,128)} %param.17) | copy-start | bytes 24580
  2.1 5.5 %collective-permute-start = (f32[17,8,128]{2,1,0:T(8,128)S(1)}, f32[17,8,128]{2,1,0:T(8,128)S(1)}, u32[]{:S(2)}, u32[]{:S(2)}) collective-permute-start(f32[17,8,128]{2,1,0:T(8,128)S(1)} %pack.1.refs_1_), channel_id=1, source_target_pairs={{0,1},{1,0},{2,3},{3,2},{4,5},{5,4},{6,7},{7,6},{8,9},{9,8},{10,11... | collective-permute-start | bytes 208904 | tf_op jit(solution)/shard_map/ppermute | solution.py:488
  5.1 4.3 %collective-permute-start.1 = (f32[17,8,128]{2,1,0:T(8,128)S(1)}, f32[17,8,128]{2,1,0:T(8,128)S(1)}, u32[]{:S(2)}, u32[]{:S(2)}) collective-permute-start(f32[17,8,128]{2,1,0:T(8,128)S(1)} %pack.1.refs_1_), channel_id=1, source_target_pairs={{0,4},{1,5},{2,6},{3,7},{4,0},{5,1},{6,2},{7,3},{8,12},{9,13},{10,... | collective-permute-start | bytes 208904 | tf_op jit(solution)/shard_map/ppermute | solution.py:488
  6.6 5.2 %collective-permute-start.2 = (f32[17,8,128]{2,1,0:T(8,128)S(1)}, f32[17,8,128]{2,1,0:T(8,128)S(1)}, u32[]{:S(2)}, u32[]{:S(2)}) collective-permute-start(f32[17,8,128]{2,1,0:T(8,128)S(1)} %pack.1.refs_1_), channel_id=1, source_target_pairs={{0,5},{1,4},{2,7},{3,6},{4,1},{5,0},{6,3},{7,2},{8,13},{9,12},{10,... | collective-permute-start | bytes 208904 | tf_op jit(solution)/shard_map/ppermute | solution.py:488
  6.6 7.5 %collective-permute-start.3 = (f32[17,8,128]{2,1,0:T(8,128)S(1)}, f32[17,8,128]{2,1,0:T(8,128)S(1)}, u32[]{:S(2)}, u32[]{:S(2)}) collective-permute-start(f32[17,8,128]{2,1,0:T(8,128)S(1)} %pack.1.refs_1_), channel_id=1, source_target_pairs={{0,2},{1,3},{2,0},{3,1},{4,6},{5,7},{6,4},{7,5},{8,10},{9,11},{10,... | collective-permute-start | bytes 208904 | tf_op jit(solution)/shard_map/ppermute | solution.py:490
  7.5 6.6 %collective-permute-start.4 = (f32[17,8,128]{2,1,0:T(8,128)S(1)}, f32[17,8,128]{2,1,0:T(8,128)S(1)}, u32[]{:S(2)}, u32[]{:S(2)}) collective-permute-start(f32[17,8,128]{2,1,0:T(8,128)S(1)} %collective-permute-done.refs_2_), channel_id=1, source_target_pairs={{0,2},{1,3},{2,0},{3,1},{4,6},{5,7},{6,4},{7,5},{8,10},{9,11},{10,... | collective-permute-start | bytes 208904 | tf_op jit(solution)/shard_map/ppermute | solution.py:490
  9.4 4.7 %collective-permute-start.5 = (f32[17,8,128]{2,1,0:T(8,128)S(1)}, f32[17,8,128]{2,1,0:T(8,128)S(1)}, u32[]{:S(2)}, u32[]{:S(2)}) collective-permute-start(f32[17,8,128]{2,1,0:T(8,128)S(1)} %collective-permute-done.1.refs_3_), channel_id=1, source_target_pairs={{0,2},{1,3},{2,0},{3,1},{4,6},{5,7},{6,4},{7,5},{8,10},{9,11},{10,... | collective-permute-start | bytes 208904 | tf_op jit(solution)/shard_map/ppermute | solution.py:490
  11.8 2.3 %collective-permute-start.6 = (f32[17,8,128]{2,1,0:T(8,128)S(1)}, f32[17,8,128]{2,1,0:T(8,128)S(1)}, u32[]{:S(2)}, u32[]{:S(2)}) collective-permute-start(f32[17,8,128]{2,1,0:T(8,128)S(1)} %collective-permute-done.2.refs_4_), channel_id=1, source_target_pairs={{0,2},{1,3},{2,0},{3,1},{4,6},{5,7},{6,4},{7,5},{8,10},{9,11},{10,... | collective-permute-start | bytes 208904 | tf_op jit(solution)/shard_map/ppermute | solution.py:490
  18.7 5.9 %collective-permute-start.10 = (f32[16,640]{1,0:T(8,128)S(1)}, f32[16,640]{1,0:T(8,128)S(1)}, u32[]{:S(2)}, u32[]{:S(2)}) collective-permute-start(f32[16,640]{1,0:T(8,128)S(1)} %get-tuple-element.22.refs_2_), channel_id=1, source_target_pairs={{0,8},{8,16},{16,24},{24,0},{1,9},{9,17},{17,25},{25,1},{2,10},{10... | collective-permute-start | bytes 122888 | tf_op jit(solution)/shard_map/ppermute | solution.py:541
  20.3 6.2 %collective-permute-start.11 = (f32[16,640]{1,0:T(8,128)S(1)}, f32[16,640]{1,0:T(8,128)S(1)}, u32[]{:S(2)}, u32[]{:S(2)}) collective-permute-start(f32[16,640]{1,0:T(8,128)S(1)} %get-tuple-element.22.refs_2_), channel_id=1, source_target_pairs={{0,16},{8,24},{16,0},{24,8},{1,17},{9,25},{17,1},{25,9},{2,18},{10... | collective-permute-start | bytes 122888 | tf_op jit(solution)/shard_map/ppermute | solution.py:541
  22.9 4.0 %collective-permute-start.12 = (f32[16,640]{1,0:T(8,128)S(1)}, f32[16,640]{1,0:T(8,128)S(1)}, u32[]{:S(2)}, u32[]{:S(2)}) collective-permute-start(f32[16,640]{1,0:T(8,128)S(1)} %get-tuple-element.22.refs_2_), channel_id=1, source_target_pairs={{0,24},{8,0},{16,8},{24,16},{1,25},{9,1},{17,9},{25,17},{2,26},{10... | collective-permute-start | bytes 122888 | tf_op jit(solution)/shard_map/ppermute | solution.py:541
  26.9 20.4 %copy-start.1 = (f32[8,4,16,32]{3,2,1,0:T(8,128)S(1)}, f32[8,4,16,32]{3,2,1,0:T(8,128)}, u32[]{:S(2)}) copy-start(f32[8,4,16,32]{3,2,1,0:T(8,128)} %param.9) | copy-start | bytes 196612
  31.3 3.9 %collective-permute-start.13 = (f32[4,16,8,128]{3,2,1,0:T(8,128)S(1)}, f32[4,16,8,128]{3,2,1,0:T(8,128)S(1)}, u32[]{:S(2)}, u32[]{:S(2)}) collective-permute-start(f32[4,16,8,128]{3,2,1,0:T(8,128)S(1)} %get-tuple-element.26), channel_id=1, source_target_pairs={{0,2},{1,3},{2,0},{3,1},{4,6},{5,7},{6,4},{7,5},{8,10},{9,11},{10,... | collective-permute-start | bytes 786440 | tf_op jit(solution)/shard_map/ppermute | solution.py:568
  31.3 7.1 %collective-permute-start.9 = (f32[4,32,256]{2,1,0:T(8,128)S(1)}, f32[4,32,256]{2,1,0:T(8,128)S(1)}, u32[]{:S(2)}, u32[]{:S(2)}) collective-permute-start(f32[4,32,256]{2,1,0:T(8,128)S(1)} %get-tuple-element.20), channel_id=1, source_target_pairs={{0,24},{8,0},{16,8},{24,16},{1,25},{9,1},{17,9},{25,17},{2,26},{10... | collective-permute-start | bytes 393224 | tf_op jit(solution)/shard_map/ppermute | solution.py:543
  34.5 12.1 %collective-permute-start.8 = (f32[4,32,256]{2,1,0:T(8,128)S(1)}, f32[4,32,256]{2,1,0:T(8,128)S(1)}, u32[]{:S(2)}, u32[]{:S(2)}) collective-permute-start(f32[4,32,256]{2,1,0:T(8,128)S(1)} %get-tuple-element.19), channel_id=1, source_target_pairs={{0,16},{8,24},{16,0},{24,8},{1,17},{9,25},{17,1},{25,9},{2,18},{10... | collective-permute-start | bytes 393224 | tf_op jit(solution)/shard_map/ppermute | solution.py:543
  34.5 12.1 %collective-permute-start.7 = (f32[4,32,256]{2,1,0:T(8,128)S(1)}, f32[4,32,256]{2,1,0:T(8,128)S(1)}, u32[]{:S(2)}, u32[]{:S(2)}) collective-permute-start(f32[4,32,256]{2,1,0:T(8,128)S(1)} %get-tuple-element.18), channel_id=1, source_target_pairs={{0,8},{8,16},{16,24},{24,0},{1,9},{9,17},{17,25},{25,1},{2,10},{10... | collective-permute-start | bytes 393224 | tf_op jit(solution)/shard_map/ppermute | solution.py:543
  35.2 12.1 %collective-permute-start.14 = (f32[16,8,128]{2,1,0:T(8,128)S(1)}, f32[16,8,128]{2,1,0:T(8,128)S(1)}, u32[]{:S(2)}, u32[]{:S(2)}) collective-permute-start(f32[16,8,128]{2,1,0:T(8,128)S(1)} %get-tuple-element.29), channel_id=1, source_target_pairs={{0,1},{1,0},{2,3},{3,2},{4,5},{5,4},{6,7},{7,6},{8,9},{9,8},{10,11... | collective-permute-start | bytes 196616 | tf_op jit(solution)/shard_map/ppermute | solution.py:570
  35.8 11.5 %collective-permute-start.15 = (f32[16,8,128]{2,1,0:T(8,128)S(1)}, f32[16,8,128]{2,1,0:T(8,128)S(1)}, u32[]{:S(2)}, u32[]{:S(2)}) collective-permute-start(f32[16,8,128]{2,1,0:T(8,128)S(1)} %get-tuple-element.28), channel_id=1, source_target_pairs={{0,4},{1,5},{2,6},{3,7},{4,0},{5,1},{6,2},{7,3},{8,12},{9,13},{10,... | collective-permute-start | bytes 196616 | tf_op jit(solution)/shard_map/ppermute | solution.py:570
  38.5 8.8 %collective-permute-start.16 = (f32[16,8,128]{2,1,0:T(8,128)S(1)}, f32[16,8,128]{2,1,0:T(8,128)S(1)}, u32[]{:S(2)}, u32[]{:S(2)}) collective-permute-start(f32[16,8,128]{2,1,0:T(8,128)S(1)} %get-tuple-element.27), channel_id=1, source_target_pairs={{0,5},{1,4},{2,7},{3,6},{4,1},{5,0},{6,3},{7,2},{8,13},{9,12},{10,... | collective-permute-start | bytes 196616 | tf_op jit(solution)/shard_map/ppermute | solution.py:570

commit v5 on v4

--- a/solution.py
+++ b/solution.py
@@ -12,7 +12,7 @@
 SWEEPS = 4
 LANES = 128
 SUB = 8
-PITCH_PAD = 8
+PITCH_PAD = 1
 PREP_CHUNKS = 4
 SWAP_UNROLL = 16
 PRODUCTS = 2
@@ -269,7 +269,7 @@
         lhs = jnp.concatenate([hi, lo], axis=0)
         out = jnp.dot(lhs, w_ref[f], preferred_element_type=jnp.float32)
         out = out[: z.rows] + out[z.rows :]
-        start = pl.multiple_of(f * pitch, SUB)
+        start = f * pitch
         for t in range(z.ct):
             fine_ref[t, pl.ds(start, z.rows), :] = out[:, t * LANES : (t + 1) * LANES]
         return carry
@@ -291,7 +291,7 @@
                 inc[l * z.vars + v, :, cols] = total
         return carry
 
-    lax.fori_loop(0, z.levels, level, 0)
+    lax.fori_loop(0, z.levels, level, 0, unroll=True)
 
     where, _ = split2(cells_ref[...], z.bcells)
     ids = lax.broadcasted_iota(jnp.int32, (z.fine, z.obs), 0)
@@ -375,11 +375,11 @@
                 for v in range(z.vars):
                     term = f[v] * pert_ref[m, l, v, :, cols].astype(jnp.float32)
                     grad = term if grad is None else grad + term
-                start = pl.multiple_of((m * z.levels + l) * pitch, SUB)
+                start = (m * z.levels + l) * pitch
                 fine_ref[t, pl.ds(start, z.fine), :] = grad
         return carry
 
-    lax.fori_loop(0, z.levels, level, 0)
+    lax.fori_loop(0, z.levels, level, 0, unroll=True)
     other[...] = jnp.zeros(other.shape, jnp.float32)
     first_half = lane_ids((z.rows // 2, LANES)) < z.block
 

time: 48.5 us -> 48.3 us (level)
  no operation moved by 1% of the time
where the time goes in v5:
time: 48.3 us; the launch traced here: 48.1 us
  waiting for transfers between devices  17.7 us (37%)
  starting transfers between devices  15.6 us (32%)
  Pallas kernels  12.6 us (26%)
  between operations  1.46 us (3%)
  other arithmetic  0.72 us (1%)
    ppermute x3, waiting for transfers between devices, on_device(): parts.append(lax.ppermute(incs[s], 'mem', ring(s)))  9.82 us
    ppermute x3, starting transfers between devices, on_device(): seens.append(lax.ppermute(seen, 'mem', ring(s)))  5.57 us
    ppermute x3, waiting for transfers between devices, on_device(): tiles.append(lax.ppermute(own, axes, z.chip_perm(s)))  5.18 us
    ppermute x3, starting transfers between devices, on_device(): tiles.append(lax.ppermute(own, axes, z.chip_perm(s)))  4.57 us
    pallas_call x1, Pallas kernels, on_device(): pl.pallas_call(functools.partial(adjoint_kernel, z), out_shape=(shape((z....  4.32 us
    pallas_call x1, Pallas kernels, on_device(): pl.pallas_call(functools.partial(forward_kernel, z), out_shape=(shape((z....  4.25 us
    ppermute x3, starting transfers between devices, on_device(): parts.append(lax.ppermute(incs[s], 'mem', ring(s)))  3.81 us
    ppermute x3, waiting for transfers between devices, on_device(): seens.append(lax.ppermute(seen, 'mem', ring(s)))  2.68 us
  transfers between devices with their start and end apart: 17, of which 8 were waited for; matrix products, arithmetic and copies ran while one was open for 1% of the time, Pallas kernels for 3%

profile of v5, /device:TPU:0, one launch (start us, length us, event | category | flops | bytes accessed | tf_op | source)
XLA Modules:
  0.0 48.1 jit_solution(4952684588733191997)
XLA Ops:
  0.7 1.4 %pack.1.refs_1_ = f32[17,8,128]{2,1,0:T(8,128)S(1)} custom-call(f32[32,16,32]{2,1,0:T(8,128)} %bitcast.16, f32[16,32]{1,0:T(8,128)} %rate_hbm.1), custom_call_target="tpu_custom_call" | custom-call | tf_op jit(solution)/shard_map/pack/pallas_call | solution.py:473
  2.1 3.0 %collective-permute-start = (f32[17,8,128]{2,1,0:T(8,128)S(1)}, f32[17,8,128]{2,1,0:T(8,128)S(1)}, u32[]{:S(2)}, u32[]{:S(2)}) collective-permute-start(f32[17,8,128]{2,1,0:T(8,128)S(1)} %pack.1.refs_1_), channel_id=1, source_target_pairs={{0,1},{1,0},{2,3},{3,2},{4,5},{5,4},{6,7},{7,6},{8,9},{9,8},{10,11... | collective-permute-start | bytes 208904 | tf_op jit(solution)/shard_map/ppermute | solution.py:488
  5.1 1.5 %collective-permute-start.1 = (f32[17,8,128]{2,1,0:T(8,128)S(1)}, f32[17,8,128]{2,1,0:T(8,128)S(1)}, u32[]{:S(2)}, u32[]{:S(2)}) collective-permute-start(f32[17,8,128]{2,1,0:T(8,128)S(1)} %pack.1.refs_1_), channel_id=1, source_target_pairs={{0,4},{1,5},{2,6},{3,7},{4,0},{5,1},{6,2},{7,3},{8,12},{9,13},{10,... | collective-permute-start | bytes 208904 | tf_op jit(solution)/shard_map/ppermute | solution.py:488
  6.6 0.9 %collective-permute-done.refs_2_ = f32[17,8,128]{2,1,0:T(8,128)S(1)} collective-permute-done((f32[17,8,128]{2,1,0:T(8,128)S(1)}, f32[17,8,128]{2,1,0:T(8,128)S(1)}, u32[]{:S(2)}, u32[]{:S(2)}) %collective-permute-start) | collective-permute-done | bytes 69664 | tf_op jit(solution)/shard_map/ppermute | solution.py:488
  7.5 1.9 %collective-permute-done.1.refs_3_ = f32[17,8,128]{2,1,0:T(8,128)S(1)} collective-permute-done((f32[17,8,128]{2,1,0:T(8,128)S(1)}, f32[17,8,128]{2,1,0:T(8,128)S(1)}, u32[]{:S(2)}, u32[]{:S(2)}) %collective-permute-start.1) | collective-permute-done | bytes 69664 | tf_op jit(solution)/shard_map/ppermute | solution.py:488
  9.4 2.4 %collective-permute-done.2.refs_4_ = f32[17,8,128]{2,1,0:T(8,128)S(1)} collective-permute-done((f32[17,8,128]{2,1,0:T(8,128)S(1)}, f32[17,8,128]{2,1,0:T(8,128)S(1)}, u32[]{:S(2)}, u32[]{:S(2)}) %collective-permute-start.2) | collective-permute-done | bytes 69664 | tf_op jit(solution)/shard_map/ppermute | solution.py:488
  12.5 1.6 %prep.1 = (bf16[32,128,256]{2,1,0:T(8,128)(2,1)S(1)}, bf16[256,512]{1,0:T(8,128)(2,1)S(1)}, f32[1,512]{1,0:T(1,128)S(1)}) custom-call(f32[32,64,256]{2,1,0:T(8,128)} %bitcast.25, s32[1,512]{1,0:T(1,128)} %bitcast.18, s32[1,1]{1,0:T(1,128)S(6)} %copy.12.refs_2_), custom_call_target="tpu_custom_call" | custom-call | flops 4000000 | bytes 5000000 | tf_op jit(solution)/shard_map/prep/pallas_call | solution.py:492
  14.2 4.2 %forward.1 = (f32[16,640]{1,0:T(8,128)S(1)}, f32[64,8,128]{2,1,0:T(8,128)S(1)}, f32[4,32,256]{2,1,0:T(8,128)S(1)}, f32[4,32,256]{2,1,0:T(8,128)S(1)}, f32[4,32,2...) custom-call(s32[32]{0:T(128)S(1)} %bitcast.23, f32[17,8,128]{2,1,0:T(8,128)S(1)} %pack.1.refs_1_, ...), custom_call_target="tpu_custom_call" | custom-call | flops 20000000 | bytes 8000000 | tf_op jit(solution)/shard_map/forward/pallas_call | solution.py:513
  18.5 1.6 %collective-permute-start.10 = (f32[16,640]{1,0:T(8,128)S(1)}, f32[16,640]{1,0:T(8,128)S(1)}, u32[]{:S(2)}, u32[]{:S(2)}) collective-permute-start(f32[16,640]{1,0:T(8,128)S(1)} %get-tuple-element.22.refs_2_), channel_id=1, source_target_pairs={{0,8},{8,16},{16,24},{24,0},{1,9},{9,17},{17,25},{25,1},{2,10},{10... | collective-permute-start | bytes 122888 | tf_op jit(solution)/shard_map/ppermute | solution.py:541
  20.1 2.6 %collective-permute-start.11 = (f32[16,640]{1,0:T(8,128)S(1)}, f32[16,640]{1,0:T(8,128)S(1)}, u32[]{:S(2)}, u32[]{:S(2)}) collective-permute-start(f32[16,640]{1,0:T(8,128)S(1)} %get-tuple-element.22.refs_2_), channel_id=1, source_target_pairs={{0,16},{8,24},{16,0},{24,8},{1,17},{9,25},{17,1},{25,9},{2,18},{10... | collective-permute-start | bytes 122888 | tf_op jit(solution)/shard_map/ppermute | solution.py:541
  22.7 1.3 %collective-permute-start.12 = (f32[16,640]{1,0:T(8,128)S(1)}, f32[16,640]{1,0:T(8,128)S(1)}, u32[]{:S(2)}, u32[]{:S(2)}) collective-permute-start(f32[16,640]{1,0:T(8,128)S(1)} %get-tuple-element.22.refs_2_), channel_id=1, source_target_pairs={{0,24},{8,0},{16,8},{24,16},{1,25},{9,1},{17,9},{25,17},{2,26},{10... | collective-permute-start | bytes 122888 | tf_op jit(solution)/shard_map/ppermute | solution.py:541
  24.0 0.4 collective-permute-done.10.refs_3_
  24.4 1.9 %collective-permute-done.11.refs_4_ = f32[16,640]{1,0:T(8,128)S(1)} collective-permute-done((f32[16,640]{1,0:T(8,128)S(1)}, f32[16,640]{1,0:T(8,128)S(1)}, u32[]{:S(2)}, u32[]{:S(2)}) %collective-permute-start.11) | collective-permute-done | bytes 40992 | tf_op jit(solution)/shard_map/ppermute | solution.py:541
  26.3 0.4 collective-permute-done.12.refs_5_
  26.7 4.3 %adjoint.1 = (f32[4,512]{1,0:T(4,128)}, f32[4,16,8,128]{3,2,1,0:T(8,128)S(1)}, f32[4,16,8,128]{3,2,1,0:T(8,128)S(1)}) custom-call(s32[32]{0:T(128)S(1)} %bitcast.24, f32[1,512]{1,0:T(1,128)S(1)} %get-tuple-element.21.refs_1_, f32[16,640]{1,0:T(8,128)S(1)} %get-tuple-element.22.refs_2_, f32[16,640]{1,0:T(8,128)S(1)} %collective-permute-done.10.refs_3_, ...), custom_call_target="tpu_custom_call" | custom-call | flops 20000000 | bytes 8000000 | tf_op jit(solution)/shard_map/adjoint/pallas_call | solution.py:546
  31.1 3.2 %collective-permute-start.9 = (f32[4,32,256]{2,1,0:T(8,128)S(1)}, f32[4,32,256]{2,1,0:T(8,128)S(1)}, u32[]{:S(2)}, u32[]{:S(2)}) collective-permute-start(f32[4,32,256]{2,1,0:T(8,128)S(1)} %get-tuple-element.20), channel_id=1, source_target_pairs={{0,24},{8,0},{16,8},{24,16},{1,25},{9,1},{17,9},{25,17},{2,26},{10... | collective-permute-start | bytes 393224 | tf_op jit(solution)/shard_map/ppermute | solution.py:543
  34.3 0.6 %collective-permute-start.7 = (f32[4,32,256]{2,1,0:T(8,128)S(1)}, f32[4,32,256]{2,1,0:T(8,128)S(1)}, u32[]{:S(2)}, u32[]{:S(2)}) collective-permute-start(f32[4,32,256]{2,1,0:T(8,128)S(1)} %get-tuple-element.18), channel_id=1, source_target_pairs={{0,8},{8,16},{16,24},{24,0},{1,9},{9,17},{17,25},{25,1},{2,10},{10... | collective-permute-start | bytes 393224 | tf_op jit(solution)/shard_map/ppermute | solution.py:543
  35.0 0.6 %collective-permute-start.14 = (f32[16,8,128]{2,1,0:T(8,128)S(1)}, f32[16,8,128]{2,1,0:T(8,128)S(1)}, u32[]{:S(2)}, u32[]{:S(2)}) collective-permute-start(f32[16,8,128]{2,1,0:T(8,128)S(1)} %get-tuple-element.29), channel_id=1, source_target_pairs={{0,1},{1,0},{2,3},{3,2},{4,5},{5,4},{6,7},{7,6},{8,9},{9,8},{10,11... | collective-permute-start | bytes 196616 | tf_op jit(solution)/shard_map/ppermute | solution.py:570
  35.6 0.5 %collective-permute-start.15 = (f32[16,8,128]{2,1,0:T(8,128)S(1)}, f32[16,8,128]{2,1,0:T(8,128)S(1)}, u32[]{:S(2)}, u32[]{:S(2)}) collective-permute-start(f32[16,8,128]{2,1,0:T(8,128)S(1)} %get-tuple-element.28), channel_id=1, source_target_pairs={{0,4},{1,5},{2,6},{3,7},{4,0},{5,1},{6,2},{7,3},{8,12},{9,13},{10,... | collective-permute-start | bytes 196616 | tf_op jit(solution)/shard_map/ppermute | solution.py:570
  36.1 2.2 %collective-permute-done.9 = f32[4,32,256]{2,1,0:T(8,128)S(1)} collective-permute-done((f32[4,32,256]{2,1,0:T(8,128)S(1)}, f32[4,32,256]{2,1,0:T(8,128)S(1)}, u32[]{:S(2)}, u32[]{:S(2)}) %collective-permute-start.9) | collective-permute-done | bytes 131104 | tf_op jit(solution)/shard_map/ppermute | solution.py:543
  38.3 0.5 collective-permute-start.16
  38.8 7.6 %collective-permute-done.8 = f32[4,32,256]{2,1,0:T(8,128)S(1)} collective-permute-done((f32[4,32,256]{2,1,0:T(8,128)S(1)}, f32[4,32,256]{2,1,0:T(8,128)S(1)}, u32[]{:S(2)}, u32[]{:S(2)}) %collective-permute-start.8) | collective-permute-done | bytes 131104 | tf_op jit(solution)/shard_map/ppermute | solution.py:543
  46.4 0.7 %add_add_fusion = f32[4,32,256]{2,1,0:T(8,128)} fusion(f32[4,32,256]{2,1,0:T(8,128)S(1)} %collective-permute-done.9, f32[4,32,256]{2,1,0:T(8,128)S(1)} %collective-permute-done.8, f32[4,32,256]{2,1,0:T(8,128)S(1)} %get-tuple-element.17, f32[4,32,256]{2,1,0:T(8,128)S(1)} %collective-permute-done.7), kind=kLoop, calls=%fused_computation | loop fusion | flops 98304 | bytes 655360 | tf_op jit(solution)/shard_map/add | solution.py:581
  47.1 1.0 %finish.1 = f32[32,16,32]{2,1,0:T(8,128)} custom-call(f32[32,16,32]{2,1,0:T(8,128)S(1)} %bitcast.17, f32[16,8,128]{2,1,0:T(8,128)S(1)} %get-tuple-element.30.refs_0_, f32[16,8,128]{2,1,0:T(8,128)S(1)} %collective-permute-done.14.refs_1_, f32[16,8,128]{2,1,0:T(8,128)S(1)} %collective-permute-done.15.refs_2_, f32[16,8,128]{2,1,0:T(8,128)S(1)} %collective-permute-done.16.refs_3_), custom_call_target="tpu_custom_call" | custom-call | tf_op jit(solution)/shard_map/finish/pallas_call | solution.py:571
  (29 shorter events, 0.2 us)
Async XLA Ops:
  0.6 13.5 %copy-start.2 = (s32[1,1,512]{2,1,0:T(1,128)S(1)}, s32[1,1,512]{2,1,0:T(1,128)}, u32[]{:S(2)}) copy-start(s32[1,1,512]{2,1,0:T(1,128)} %param.14) | copy-start | bytes 6148
  0.6 13.5 %copy-start.5 = (s32[1,1,32]{2,1,0:T(1,128)S(1)}, s32[1,1,32]{2,1,0:T(1,128)}, u32[]{:S(2)}) copy-start(s32[1,1,32]{2,1,0:T(1,128)} %param.11) | copy-start | bytes 388
  0.7 13.5 %copy-start = (bf16[8,4,4,32,256]{4,3,2,1,0:T(8,128)(2,1)S(1)}, bf16[8,4,4,32,256]{4,3,2,1,0:T(8,128)(2,1)}, u32[]{:S(2)}) copy-start(bf16[8,4,4,32,256]{4,3,2,1,0:T(8,128)(2,1)} %refs_7_.1) | copy-start | bytes 6291460
  0.7 13.5 %copy-start.3 = (f32[1,1,4,512]{3,2,1,0:T(4,128)S(1)}, f32[1,1,4,512]{3,2,1,0:T(4,128)}, u32[]{:S(2)}) copy-start(f32[1,1,4,512]{3,2,1,0:T(4,128)} %param.16) | copy-start | bytes 24580
  0.7 13.5 %copy-start.4 = (f32[1,1,4,512]{3,2,1,0:T(4,128)S(1)}, f32[1,1,4,512]{3,2,1,0:T(4,128)}, u32[]{:S(2)}) copy-start(f32[1,1,4,512]{3,2,1,0:T(4,128)} %param.17) | copy-start | bytes 24580
  2.1 5.5 %collective-permute-start = (f32[17,8,128]{2,1,0:T(8,128)S(1)}, f32[17,8,128]{2,1,0:T(8,128)S(1)}, u32[]{:S(2)}, u32[]{:S(2)}) collective-permute-start(f32[17,8,128]{2,1,0:T(8,128)S(1)} %pack.1.refs_1_), channel_id=1, source_target_pairs={{0,1},{1,0},{2,3},{3,2},{4,5},{5,4},{6,7},{7,6},{8,9},{9,8},{10,11... | collective-permute-start | bytes 208904 | tf_op jit(solution)/shard_map/ppermute | solution.py:488
  5.1 4.3 %collective-permute-start.1 = (f32[17,8,128]{2,1,0:T(8,128)S(1)}, f32[17,8,128]{2,1,0:T(8,128)S(1)}, u32[]{:S(2)}, u32[]{:S(2)}) collective-permute-start(f32[17,8,128]{2,1,0:T(8,128)S(1)} %pack.1.refs_1_), channel_id=1, source_target_pairs={{0,4},{1,5},{2,6},{3,7},{4,0},{5,1},{6,2},{7,3},{8,12},{9,13},{10,... | collective-permute-start | bytes 208904 | tf_op jit(solution)/shard_map/ppermute | solution.py:488
  6.6 5.2 %collective-permute-start.2 = (f32[17,8,128]{2,1,0:T(8,128)S(1)}, f32[17,8,128]{2,1,0:T(8,128)S(1)}, u32[]{:S(2)}, u32[]{:S(2)}) collective-permute-start(f32[17,8,128]{2,1,0:T(8,128)S(1)} %pack.1.refs_1_), channel_id=1, source_target_pairs={{0,5},{1,4},{2,7},{3,6},{4,1},{5,0},{6,3},{7,2},{8,13},{9,12},{10,... | collective-permute-start | bytes 208904 | tf_op jit(solution)/shard_map/ppermute | solution.py:488
  6.6 7.5 %collective-permute-start.3 = (f32[17,8,128]{2,1,0:T(8,128)S(1)}, f32[17,8,128]{2,1,0:T(8,128)S(1)}, u32[]{:S(2)}, u32[]{:S(2)}) collective-permute-start(f32[17,8,128]{2,1,0:T(8,128)S(1)} %pack.1.refs_1_), channel_id=1, source_target_pairs={{0,2},{1,3},{2,0},{3,1},{4,6},{5,7},{6,4},{7,5},{8,10},{9,11},{10,... | collective-permute-start | bytes 208904 | tf_op jit(solution)/shard_map/ppermute | solution.py:490
  7.5 6.6 %collective-permute-start.4 = (f32[17,8,128]{2,1,0:T(8,128)S(1)}, f32[17,8,128]{2,1,0:T(8,128)S(1)}, u32[]{:S(2)}, u32[]{:S(2)}) collective-permute-start(f32[17,8,128]{2,1,0:T(8,128)S(1)} %collective-permute-done.refs_2_), channel_id=1, source_target_pairs={{0,2},{1,3},{2,0},{3,1},{4,6},{5,7},{6,4},{7,5},{8,10},{9,11},{10,... | collective-permute-start | bytes 208904 | tf_op jit(solution)/shard_map/ppermute | solution.py:490
  9.4 4.7 %collective-permute-start.5 = (f32[17,8,128]{2,1,0:T(8,128)S(1)}, f32[17,8,128]{2,1,0:T(8,128)S(1)}, u32[]{:S(2)}, u32[]{:S(2)}) collective-permute-start(f32[17,8,128]{2,1,0:T(8,128)S(1)} %collective-permute-done.1.refs_3_), channel_id=1, source_target_pairs={{0,2},{1,3},{2,0},{3,1},{4,6},{5,7},{6,4},{7,5},{8,10},{9,11},{10,... | collective-permute-start | bytes 208904 | tf_op jit(solution)/shard_map/ppermute | solution.py:490
  11.8 2.3 %collective-permute-start.6 = (f32[17,8,128]{2,1,0:T(8,128)S(1)}, f32[17,8,128]{2,1,0:T(8,128)S(1)}, u32[]{:S(2)}, u32[]{:S(2)}) collective-permute-start(f32[17,8,128]{2,1,0:T(8,128)S(1)} %collective-permute-done.2.refs_4_), channel_id=1, source_target_pairs={{0,2},{1,3},{2,0},{3,1},{4,6},{5,7},{6,4},{7,5},{8,10},{9,11},{10,... | collective-permute-start | bytes 208904 | tf_op jit(solution)/shard_map/ppermute | solution.py:490
  18.5 6.0 %collective-permute-start.10 = (f32[16,640]{1,0:T(8,128)S(1)}, f32[16,640]{1,0:T(8,128)S(1)}, u32[]{:S(2)}, u32[]{:S(2)}) collective-permute-start(f32[16,640]{1,0:T(8,128)S(1)} %get-tuple-element.22.refs_2_), channel_id=1, source_target_pairs={{0,8},{8,16},{16,24},{24,0},{1,9},{9,17},{17,25},{25,1},{2,10},{10... | collective-permute-start | bytes 122888 | tf_op jit(solution)/shard_map/ppermute | solution.py:541
  20.1 6.2 %collective-permute-start.11 = (f32[16,640]{1,0:T(8,128)S(1)}, f32[16,640]{1,0:T(8,128)S(1)}, u32[]{:S(2)}, u32[]{:S(2)}) collective-permute-start(f32[16,640]{1,0:T(8,128)S(1)} %get-tuple-element.22.refs_2_), channel_id=1, source_target_pairs={{0,16},{8,24},{16,0},{24,8},{1,17},{9,25},{17,1},{25,9},{2,18},{10... | collective-permute-start | bytes 122888 | tf_op jit(solution)/shard_map/ppermute | solution.py:541
  22.7 4.0 %collective-permute-start.12 = (f32[16,640]{1,0:T(8,128)S(1)}, f32[16,640]{1,0:T(8,128)S(1)}, u32[]{:S(2)}, u32[]{:S(2)}) collective-permute-start(f32[16,640]{1,0:T(8,128)S(1)} %get-tuple-element.22.refs_2_), channel_id=1, source_target_pairs={{0,24},{8,0},{16,8},{24,16},{1,25},{9,1},{17,9},{25,17},{2,26},{10... | collective-permute-start | bytes 122888 | tf_op jit(solution)/shard_map/ppermute | solution.py:541
  26.7 20.4 %copy-start.1 = (f32[8,4,16,32]{3,2,1,0:T(8,128)S(1)}, f32[8,4,16,32]{3,2,1,0:T(8,128)}, u32[]{:S(2)}) copy-start(f32[8,4,16,32]{3,2,1,0:T(8,128)} %param.9) | copy-start | bytes 196612
  31.0 3.9 %collective-permute-start.13 = (f32[4,16,8,128]{3,2,1,0:T(8,128)S(1)}, f32[4,16,8,128]{3,2,1,0:T(8,128)S(1)}, u32[]{:S(2)}, u32[]{:S(2)}) collective-permute-start(f32[4,16,8,128]{3,2,1,0:T(8,128)S(1)} %get-tuple-element.26), channel_id=1, source_target_pairs={{0,2},{1,3},{2,0},{3,1},{4,6},{5,7},{6,4},{7,5},{8,10},{9,11},{10,... | collective-permute-start | bytes 786440 | tf_op jit(solution)/shard_map/ppermute | solution.py:568
  31.1 7.1 %collective-permute-start.9 = (f32[4,32,256]{2,1,0:T(8,128)S(1)}, f32[4,32,256]{2,1,0:T(8,128)S(1)}, u32[]{:S(2)}, u32[]{:S(2)}) collective-permute-start(f32[4,32,256]{2,1,0:T(8,128)S(1)} %get-tuple-element.20), channel_id=1, source_target_pairs={{0,24},{8,0},{16,8},{24,16},{1,25},{9,1},{17,9},{25,17},{2,26},{10... | collective-permute-start | bytes 393224 | tf_op jit(solution)/shard_map/ppermute | solution.py:543
  34.3 12.1 %collective-permute-start.8 = (f32[4,32,256]{2,1,0:T(8,128)S(1)}, f32[4,32,256]{2,1,0:T(8,128)S(1)}, u32[]{:S(2)}, u32[]{:S(2)}) collective-permute-start(f32[4,32,256]{2,1,0:T(8,128)S(1)} %get-tuple-element.19), channel_id=1, source_target_pairs={{0,16},{8,24},{16,0},{24,8},{1,17},{9,25},{17,1},{25,9},{2,18},{10... | collective-permute-start | bytes 393224 | tf_op jit(solution)/shard_map/ppermute | solution.py:543
  34.3 12.1 %collective-permute-start.7 = (f32[4,32,256]{2,1,0:T(8,128)S(1)}, f32[4,32,256]{2,1,0:T(8,128)S(1)}, u32[]{:S(2)}, u32[]{:S(2)}) collective-permute-start(f32[4,32,256]{2,1,0:T(8,128)S(1)} %get-tuple-element.18), channel_id=1, source_target_pairs={{0,8},{8,16},{16,24},{24,0},{1,9},{9,17},{17,25},{25,1},{2,10},{10... | collective-permute-start | bytes 393224 | tf_op jit(solution)/shard_map/ppermute | solution.py:543
  35.0 12.1 %collective-permute-start.14 = (f32[16,8,128]{2,1,0:T(8,128)S(1)}, f32[16,8,128]{2,1,0:T(8,128)S(1)}, u32[]{:S(2)}, u32[]{:S(2)}) collective-permute-start(f32[16,8,128]{2,1,0:T(8,128)S(1)} %get-tuple-element.29), channel_id=1, source_target_pairs={{0,1},{1,0},{2,3},{3,2},{4,5},{5,4},{6,7},{7,6},{8,9},{9,8},{10,11... | collective-permute-start | bytes 196616 | tf_op jit(solution)/shard_map/ppermute | solution.py:570
  35.6 11.5 %collective-permute-start.15 = (f32[16,8,128]{2,1,0:T(8,128)S(1)}, f32[16,8,128]{2,1,0:T(8,128)S(1)}, u32[]{:S(2)}, u32[]{:S(2)}) collective-permute-start(f32[16,8,128]{2,1,0:T(8,128)S(1)} %get-tuple-element.28), channel_id=1, source_target_pairs={{0,4},{1,5},{2,6},{3,7},{4,0},{5,1},{6,2},{7,3},{8,12},{9,13},{10,... | collective-permute-start | bytes 196616 | tf_op jit(solution)/shard_map/ppermute | solution.py:570
  38.3 8.8 %collective-permute-start.16 = (f32[16,8,128]{2,1,0:T(8,128)S(1)}, f32[16,8,128]{2,1,0:T(8,128)S(1)}, u32[]{:S(2)}, u32[]{:S(2)}) collective-permute-start(f32[16,8,128]{2,1,0:T(8,128)S(1)} %get-tuple-element.27), channel_id=1, source_target_pairs={{0,5},{1,4},{2,7},{3,6},{4,1},{5,0},{6,3},{7,2},{8,13},{9,12},{10,... | collective-permute-start | bytes 196616 | tf_op jit(solution)/shard_map/ppermute | solution.py:570
